TPU v7x, 256 devices: a whole 4x4x8 slice. The times are simulated.
256 devices in a mesh: mem: 32 (over z, x), tp: 8 (over y, core).
Axes of the slice: x: 4, y: 4, z: 8, core: 2. Of those that a mesh axis runs over, the one named last changes fastest.
Arguments:
- tokens: bfloat16 [16384, 5120], P('mem'), may hold values from -6 to 6
- query_weight: bfloat16 [5120, 5120], P('mem', 'tp'), may hold values from -0.078125 to 0.078125
- output_weight: bfloat16 [5120, 5120], P('tp', 'mem'), may hold values from -0.078125 to 0.078125
- time_modulation: float32 [50, 2, 5120], replicated, may hold values from -3 to 3
- timestep: int32 [1], replicated, may hold values from 0 to 49
- memory_store: bfloat16 [2048, 2, 8, 5120], P('mem', None, None, 'tp'), may hold values from -480 to 480
- retrieved: int32 [16, 8], replicated, may hold values from 0 to 2047, as said below
- fresh_entry: bfloat16 [2, 8, 5120], P(None, None, ('tp', 'mem')), may hold values from -4 to 4
- write_slot: int32 [1], replicated, may hold values from 0 to 2047
Outputs:
- memory_out: bfloat16 [16384, 5120], P('mem', 'tp')
- updated_store: bfloat16 [2048, 2, 8, 5120], P('mem', None, None, 'tp')
Inputs may be any that keep to these rules, and one draw needn't show every extreme that they name: `retrieved`: in each row, no two indices lie in the same aligned block of 64 stored frames.
All inputs are finite; a program needn't handle non-finite values.
Results may differ from a plain program's by a relative error of at most 0.014.
The roundings to bfloat16 on the way count: a program that leaves them out, or rounds other values in their place, can miss the bound.
Values may be sent and summed in bfloat16 or wider, within the bound.
No kernel may reach another device: no remote copies, remote signals or barrier semaphores. Data moves between devices by JAX's collectives and lax.ppermute only.
A program may use at most 128 MiB of HBM per device.

v0:
```python
import functools

import jax
import jax.numpy as jnp
from jax import lax
from jax.experimental import pallas as pl
from jax.experimental.pallas import tpu as pltpu
from jax.sharding import Mesh
from jax.sharding import PartitionSpec as P

HEAD_SIZE = 128
MEM = ("mem_0", "mem_1")
TP = ("tp_0", "tp_1")
TP_MEM = TP + MEM

EPS = 1e-06


def shift(array, axis, by):
    n = lax.axis_size(axis)
    return lax.ppermute(array, axis, [(i, (i + by) % n) for i in range(n)])


def around(block, axis, whole, direction=1):
    n = lax.axis_size(axis)
    got = [(block, 0, None)]
    fore = back = block
    for step in range(1, (n - 1) // 2 + 1):
        fore, back = shift(fore, axis, 1), shift(back, axis, -1)
        got += [(fore, -step, None), (back, step, None)]
    half = n // 2
    if whole:
        last = shift(fore, axis, 1) if direction > 0 else shift(back, axis, -1)
        got.append((last, half, None))
    else:
        cut = block.shape[0] // 2
        got.append((shift(fore[:cut], axis, 1), half, (0, cut)))
        got.append((shift(back[cut:], axis, -1), half, (cut, block.shape[0])))
    return got


def in_order(got, n):
    return jnp.stack([next(a for a, off, _ in got if off % n == i) for i in range(n)])


def attend_kernel(plan, rows, nx, xm_ref, k_ref, v_ref, *rest):
    pieces, (out_ref, w_ref, acc_ref, sems) = rest[: len(plan)], rest[len(plan):]
    x = lax.axis_index("mem_1")
    copies = []
    for piece, entries in zip(pieces, plan):
        for index, at_z, off_x, lane, lanes in entries:
            block = at_z * nx + lax.rem(x + (off_x % nx), nx)
            start = pl.multiple_of(block * rows, 32)
            copy = pltpu.make_async_copy(
                piece.at[index],
                w_ref.at[pl.ds(start, rows), pl.ds(lane, lanes)],
                sems.at[len(copies)],
            )
            copy.start()
            copies.append(copy)
    for copy in copies:
        copy.wait()
    depth = w_ref.shape[0]
    step = depth // 4

    def accumulate(i, carry):
        at = pl.ds(pl.multiple_of(i * step, 128), step)
        acc_ref[...] += jnp.dot(xm_ref[:, at], w_ref[at, :], preferred_element_type=jnp.float32)
        return carry

    acc_ref[...] = jnp.zeros_like(acc_ref)
    lax.fori_loop(0, 4, accumulate, 0)

    def attend(i, carry):
        part = pl.ds(pl.multiple_of(i * 2 * HEAD_SIZE, HEAD_SIZE), 2 * HEAD_SIZE)
        for head in range(w_ref.shape[1] // HEAD_SIZE):
            at = pl.ds(head * HEAD_SIZE, HEAD_SIZE)
            query = acc_ref[part, at].astype(jnp.bfloat16)
            logits = lax.dot_general(
                query, k_ref[:, at], (((1,), (1,)), ((), ())), preferred_element_type=jnp.float32
            ) * HEAD_SIZE ** (-0.5)
            expo = jnp.exp(logits - jnp.max(logits, axis=-1, keepdims=True))
            probs = (expo / jnp.sum(expo, axis=-1, keepdims=True)).astype(jnp.bfloat16)
            out_ref[part, at] = jnp.dot(
                probs, v_ref[:, at], preferred_element_type=jnp.float32
            ).astype(jnp.bfloat16)
        return carry

    lax.fori_loop(0, acc_ref.shape[0] // (2 * HEAD_SIZE), attend, 0)


def place_kernel(offs, nx, *refs):
    pieces, (out_ref, held) = refs[: len(offs)], refs[len(offs):]
    x = lax.axis_index("mem_1")
    for piece, off in zip(pieces, offs):
        rows = piece.shape[0]
        start = lax.rem(x + (off % nx), nx) * rows
        held[pl.ds(pl.multiple_of(start, 32), rows), :] = piece[...].astype(jnp.float32)
    out_ref[...] = held[...].T.astype(jnp.bfloat16)


def shards(
    tokens,
    query_weight,
    output_weight,
    time_modulation,
    timestep,
    memory_store,
    retrieved,
    fresh_entry,
    write_slot,
):
    nz, nx = lax.axis_size("mem_0"), lax.axis_size("mem_1")
    n_mem = nz * nx
    myself = lax.axis_index(MEM)
    frames = retrieved.shape[0]
    per_frame = n_mem // frames
    stored, _, slots_rows, width = memory_store.shape
    count, model = tokens.shape
    rows = query_weight.shape[0]

    cut = 2 * HEAD_SIZE
    late = width - cut
    joint = jnp.concatenate([query_weight[:, cut:], output_weight.T], axis=1)
    joint = lax.all_gather(joint, "mem_0", axis=0, tiled=False)
    q_a = in_order(around(query_weight[:, :cut], "mem_1", True), nx)
    q_a, joint = lax.optimization_barrier((q_a, joint))
    q_a = lax.all_gather(q_a, "mem_0", axis=0, tiled=False)

    owners = retrieved // stored
    offsets = retrieved % stored
    chosen = jnp.sum(jnp.where(owners == myself, offsets, 0), axis=1)
    picks = (chosen[:, None] * 2 + jnp.arange(per_frame, dtype=jnp.int32)[None]).reshape(-1)
    outgoing = jnp.take(memory_store.reshape(stored * 2, slots_rows, width), picks, axis=0)
    own_fresh = jnp.concatenate([fresh_entry[0], fresh_entry[1]], axis=1)
    extra = own_fresh.shape[1]
    own_fresh = jnp.pad(own_fresh, ((0, 0), (0, HEAD_SIZE - extra)))
    outgoing = jnp.concatenate(
        [outgoing, jnp.broadcast_to(own_fresh, (n_mem, *own_fresh.shape))], axis=2
    )
    incoming = lax.all_to_all(outgoing, MEM, split_axis=0, concat_axis=0, tiled=True)
    my_owners = lax.dynamic_index_in_dim(owners, myself // per_frame, 0, keepdims=False)
    fetched = jnp.take(incoming[:, :, :width], my_owners, axis=0).reshape(-1, width)
    other = lax.ppermute(fetched, "mem_1", [(i, i ^ 1) for i in range(nx)])
    even = myself % 2 == 0
    keys = jnp.where(even, fetched, other)
    vals = jnp.where(even, other, fetched)

    modrow = lax.dynamic_index_in_dim(time_modulation, timestep[0], 0, keepdims=False)
    values = tokens.astype(jnp.float32)
    factor = lax.rsqrt(jnp.mean(values * values, axis=1, keepdims=True) + EPS)
    modulated = (values * factor * (1.0 + modrow[0]) + modrow[1]).astype(jnp.bfloat16)

    joint, modulated, keys, vals = lax.optimization_barrier((joint, modulated, keys, vals))
    qb_all = around(joint[:, :, :late], "mem_1", False)

    fresh = incoming[:, :, width: width + extra].reshape(n_mem, slots_rows, 2, extra // 2)
    fresh = fresh.transpose(2, 1, 0, 3).reshape(2, slots_rows, width)
    slots = myself * stored + jnp.arange(stored, dtype=jnp.int32)
    updated_store = jnp.where(
        (slots == write_slot[0])[:, None, None, None], fresh[None], memory_store
    )

    ny, nc = lax.axis_size("tp_0"), lax.axis_size("tp_1")
    core = lax.axis_index("tp_1")
    weight = joint[:, :, late:].reshape(ny, nc, rows, width)
    weight = lax.dynamic_slice_in_dim(
        jnp.concatenate([weight, weight], axis=0), lax.axis_index("tp_0"), ny, 0
    )
    mine = lax.dynamic_index_in_dim(weight, core, 1, keepdims=False)
    other = lax.dynamic_index_in_dim(weight, 1 - core, 1, keepdims=False)
    modulated, mine, other, updated_store = lax.optimization_barrier(
        (modulated, mine, other, updated_store)
    )

    pieces = [q_a]
    plan = [[((i, j), i, j, 0, cut) for i in range(nz) for j in range(nx)]]
    for array, off, part in qb_all:
        low = 0 if part is None else part[0]
        pieces.append(array)
        plan.append([(i, low + i, off, cut, late) for i in range(array.shape[0])])
    copies = sum(len(entries) for entries in plan)
    vmem = pl.BlockSpec(memory_space=pltpu.VMEM)
    attended = pl.pallas_call(
        functools.partial(attend_kernel, plan, rows, nx),
        out_shape=jax.ShapeDtypeStruct((count, width), jnp.bfloat16),
        in_specs=[vmem] * 3 + [pl.BlockSpec(memory_space=pl.ANY)] * len(pieces),
        out_specs=vmem,
        scratch_shapes=[
            pltpu.VMEM((model, width), jnp.bfloat16),
            pltpu.VMEM((count, width), jnp.float32),
            pltpu.SemaphoreType.DMA((copies,)),
        ],
        compiler_params=pltpu.CompilerParams(vmem_limit_bytes=40 * 1024 * 1024),
        cost_estimate=pl.CostEstimate(
            flops=2 * count * model * width, bytes_accessed=2 * model * width, transcendentals=0
        ),
        name="query_attend",
    )(modulated, keys, vals, *pieces)

    def term(weight, group):
        return lax.dot_general(
            weight, group, (((2,), (1,)), ((), ())), preferred_element_type=jnp.float32
        ).astype(jnp.bfloat16)

    def paired(group):
        away = lax.ppermute(term(other, group), "tp_1", [(0, 1), (1, 0)])
        here = term(mine, group)
        pair = (here.astype(jnp.float32) + away.astype(jnp.float32)).astype(jnp.bfloat16)
        return [pair[d] for d in range(ny)]

    def sent(parts):
        return [parts[0]] + [shift(parts[d], "tp_0", d) for d in range(1, ny)]

    def summed(parts):
        return sum(part.astype(jnp.float32) for part in parts).astype(jnp.bfloat16)

    left, right = shift(attended, "mem_1", 1), shift(attended, "mem_1", -1)
    own_parts = sent(paired(attended))
    far = [shift(left[: count // 2], "mem_1", 1), shift(right[count // 2:], "mem_1", -1)]
    left, right, own_parts = lax.optimization_barrier((left, right, own_parts))
    near_parts = paired(jnp.concatenate([left, right], axis=0))
    far, _ = lax.optimization_barrier((far, near_parts))
    near_parts = sent(near_parts)
    far_parts = sent(paired(jnp.concatenate(far, axis=0)))
    out_own, near, out_far = summed(own_parts), summed(near_parts), summed(far_parts)
    blocks = [
        out_own,
        shift(near[:, :count], "mem_1", -1),
        shift(near[:, count:], "mem_1", 1),
        shift(out_far, "mem_1", 2),
    ]
    places = (0, 1, -1, 2)
    memory_out = pl.pallas_call(
        functools.partial(place_kernel, places, nx),
        out_shape=jax.ShapeDtypeStruct((count, width), jnp.bfloat16),
        in_specs=[vmem] * 4,
        out_specs=vmem,
        scratch_shapes=[pltpu.VMEM((width, count), jnp.float32)],
        name="place",
    )(*blocks)

    return (memory_out, updated_store)


def solution(mesh):
    split = Mesh(mesh.devices.reshape(8, 4, 4, 2), MEM + TP)
    in_specs = (
        P(MEM, None),
        P(MEM, TP),
        P(TP, MEM),
        P(),
        P(),
        P(MEM, None, None, TP),
        P(),
        P(None, None, TP_MEM),
        P(),
    )
    out_specs = (P(MEM, TP), P(MEM, None, None, TP))
    return jax.shard_map(
        shards, mesh=split, in_specs=in_specs, out_specs=out_specs, check_vma=False
    )
```

profile of v0, /device:TPU:2, one launch (start us, length us, event | category | flops | bytes accessed | tf_op | source)
XLA Modules:
  0.0 212.7 jit_solution(1315757113668725538)
XLA Ops:
  7.2 0.9 slice.87
  8.2 1.7 pad_maximum_fusion.2
  9.9 0.9 slice_bitcast_fusion.14
  10.8 2.3 %collective-permute-start = (bf16[160,256]{1,0:T(8,128)(2,1)S(1)}, bf16[160,256]{1,0:T(8,128)(2,1)S(1)}, u32[]{:S(2)}, u32[]{:S(2)}) collective-permute-start(bf16[160,256]{1,0:T(8,128)(2,1)S(1)} %get-tuple-element.55), channel_id=1, source_target_pairs={{0,24},{8,0},{16,8},{24,16},{1,25},{9,1},{17,9},{25,17},{2,26},{10... | collective-permute-start | bytes 245768 | tf_op jit(solution)/shard_map/ppermute | solution.py:21
  13.4 1.9 gather_fusion
  16.4 12.3 %all-to-all-start = ((bf16[32,8,768]{2,1,0:T(8,128)(2,1)}), bf16[32,8,768]{2,1,0:T(8,128)(2,1)S(1)}, u32[]{:S(2)}, u32[]{:S(2)}) async-start(bf16[32,8,768]{2,1,0:T(8,128)(2,1)} %pad_maximum_fusion), calls=%async_computation | async-start | bytes 786432 | tf_op jit(solution)/shard_map/all_to_all | solution.py:141
  29.8 1.5 collective-permute-start.2
  31.4 3.5 %collective-permute-done.2 = bf16[160,256]{1,0:T(8,128)(2,1)S(1)} collective-permute-done((bf16[160,256]{1,0:T(8,128)(2,1)S(1)}, bf16[160,256]{1,0:T(8,128)(2,1)S(1)}, u32[]{:S(2)}, u32[]{:S(2)}) %collective-permute-start.2) | collective-permute-done | bytes 81952 | tf_op jit(solution)/shard_map/ppermute | solution.py:21
  35.6 27.6 %all-gather.5.cloned.1.call-done = bf16[1280,1024]{1,0:T(8,128)(2,1)} async-done(((bf16[160,1024]{1,0:T(8,128)(2,1)}), bf16[1280,1024]{1,0:T(8,128)(2,1)}) %all-gather.5.cloned.1.call-update) | async-done | bytes 2621456 | tf_op jit(solution)/shard_map/all_gather | solution.py:125
  63.3 3.6 %fusion = f32[512]{0:T(512)S(1)} fusion(bf16[512,5120]{1,0:T(8,128)(2,1)} %param.9), kind=kLoop, calls=%fused_computation.4 | loop fusion | flops 7863808 | bytes 5244928 | tf_op jit(solution)/shard_map/reduce_sum | solution.py:151
  66.9 0.9 dynamic-slice_add_fusion
  69.1 6.8 %fusion.3.xm_ref = bf16[512,5120]{1,0:T(8,128)(2,1)} fusion(bf16[512,5120]{1,0:T(8,128)(2,1)} %param.9, f32[5120]{0:T(1024)S(1)} %bitcast.99, f32[5120]{0:T(1024)S(1)} %bitcast.98, f32[512]{0:T(512)S(1)} %add_rsqrt_fusion), kind=kLoop, calls=%fused_computation.7 | loop fusion | flops 13107200 | bytes 10528768 | tf_op jit(solution)/shard_map/convert_element_type | solution.py:152
  76.7 1.3 slice.95.rest_1_
  78.0 1.6 collective-permute-start.5
  80.9 18.5 %collective-permute-done.5.rest_3_ = bf16[8,160,384]{2,1,0:T(8,128)(2,1)S(1)} collective-permute-done((bf16[8,160,384]{2,1,0:T(8,128)(2,1)S(1)}, bf16[8,160,384]{2,1,0:T(8,128)(2,1)S(1)}, u32[]{:S(2)}, u32[]{:S(2)}) %collective-permute-start.5) | collective-permute-done | bytes 983072 | tf_op jit(solution)/shard_map/ppermute | solution.py:21
  100.2 1.1 collective-permute-start.7
  102.1 1.0 collective-permute-start.6
  103.1 1.5 slice.119
  104.6 1.6 copy.17
  106.2 1.7 copy.18
  107.9 1.1 broadcast_in_dim.60
  109.0 2.7 %broadcast_select_fusion = bf16[64,2,8,640]{3,2,1,0:T(8,128)(2,1)} fusion(bf16[64,2,8,640]{3,2,1,0:T(8,128)(2,1)} %param.14, pred[64]{0:T(512)(128)(4,1)S(1)} %add_compare_fusion, bf16[2,8,640]{2,1,0:T(8,128)(2,1)S(1)} %broadcast_in_dim.60), kind=kLoop, calls=%fused_computation.25 | loop fusion | flops 655360 | bytes 2641984 | tf_op jit(solution)/shard_map/jit(_where)/select_n | solution.py:160
  111.9 1.9 fusion.9
  113.9 2.5 %copy-done = bf16[512,5120]{1,0:T(8,128)(2,1)S(1)} copy-done((bf16[512,5120]{1,0:T(8,128)(2,1)S(1)}, bf16[512,5120]{1,0:T(8,128)(2,1)}, u32[]{:S(2)}) %copy-start) | copy-done | bytes 5242904
  116.4 1.7 copy-done.1
  119.0 9.1 %query_attend.1 = bf16[512,640]{1,0:T(8,128)(2,1)S(1)} custom-call(bf16[512,5120]{1,0:T(8,128)(2,1)S(1)} %copy-done, bf16[64,640]{1,0:T(8,128)(2,1)S(1)} %copy-done.2, bf16[64,640]{1,0:T(8,128)(2,1)S(1)} %get-tuple-element.25.v_ref, bf16[8,4,160,256]{3,2,1,0:T(8,128)(2,1)S(1)} %bitcast.91, bf16[8,160,384]{2,1,0:T(8,128)(2,1)S(1)} %slice.95.rest_1_, ...), custom_call_target="tpu_custom_call" | custom-call | flops 3355443200 | bytes 6553600 | tf_op jit(solution)/shard_map/query_attend/pallas_call | solution.py:184
  128.9 2.6 %collective-permute-start.9 = (bf16[512,640]{1,0:T(8,128)(2,1)S(1)}, bf16[512,640]{1,0:T(8,128)(2,1)S(1)}, u32[]{:S(2)}, u32[]{:S(2)}) collective-permute-start(bf16[512,640]{1,0:T(8,128)(2,1)S(1)} %query_attend.1), channel_id=1, source_target_pairs={{0,24},{8,0},{16,8},{24,16},{1,25},{9,1},{17,9},{25,17},{2,26},{10... | collective-permute-start | bytes 1966088 | tf_op jit(solution)/shard_map/ppermute | solution.py:21
  132.4 2.8 %collective-permute-start.13 = (bf16[160,512]{1,0:T(8,128)(2,1)S(1)}, bf16[160,512]{1,0:T(8,128)(2,1)S(1)}, u32[]{:S(2)}, u32[]{:S(2)}) collective-permute-start(bf16[160,512]{1,0:T(8,128)(2,1)S(1)} %get-tuple-element.48), channel_id=1, source_target_pairs={{0,6},{2,0},{4,2},{6,4},{1,7},{3,1},{5,3},{7,5},{8,14},{10,8},{12,... | collective-permute-start | bytes 491528 | tf_op jit(solution)/shard_map/ppermute | solution.py:21
  136.0 1.1 collective-permute-start.11
  137.1 9.0 %collective-permute-done.9 = bf16[512,640]{1,0:T(8,128)(2,1)S(1)} collective-permute-done((bf16[512,640]{1,0:T(8,128)(2,1)S(1)}, bf16[512,640]{1,0:T(8,128)(2,1)S(1)}, u32[]{:S(2)}, u32[]{:S(2)}) %collective-permute-start.9) | collective-permute-done | bytes 655392 | tf_op jit(solution)/shard_map/ppermute | solution.py:21
  146.2 3.5 %collective-permute-done.8 = bf16[512,640]{1,0:T(8,128)(2,1)S(1)} collective-permute-done((bf16[512,640]{1,0:T(8,128)(2,1)S(1)}, bf16[512,640]{1,0:T(8,128)(2,1)S(1)}, u32[]{:S(2)}, u32[]{:S(2)}) %collective-permute-start.8) | collective-permute-done | bytes 655392 | tf_op jit(solution)/shard_map/ppermute | solution.py:21
  149.7 1.2 convolution_convert_fusion
  151.1 3.0 %collective-permute-start.21 = (bf16[256,640]{1,0:T(8,128)(2,1)S(1)}, bf16[256,640]{1,0:T(8,128)(2,1)S(1)}, u32[]{:S(2)}, u32[]{:S(2)}) collective-permute-start(bf16[256,640]{1,0:T(8,128)(2,1)S(1)} %slice.133), channel_id=1, source_target_pairs={{0,24},{8,0},{16,8},{24,16},{1,25},{9,1},{17,9},{25,17},{2,26},{10... | collective-permute-start | bytes 983048 | tf_op jit(solution)/shard_map/ppermute | solution.py:21
  154.4 1.2 add_convert_fusion
  155.8 6.0 %collective-permute-done.21 = bf16[256,640]{1,0:T(8,128)(2,1)S(1)} collective-permute-done((bf16[256,640]{1,0:T(8,128)(2,1)S(1)}, bf16[256,640]{1,0:T(8,128)(2,1)S(1)}, u32[]{:S(2)}, u32[]{:S(2)}) %collective-permute-start.21) | collective-permute-done | bytes 327712 | tf_op jit(solution)/shard_map/ppermute | solution.py:21
  161.7 2.5 %collective-permute-done.20 = bf16[256,640]{1,0:T(8,128)(2,1)S(1)} collective-permute-done((bf16[256,640]{1,0:T(8,128)(2,1)S(1)}, bf16[256,640]{1,0:T(8,128)(2,1)S(1)}, u32[]{:S(2)}, u32[]{:S(2)}) %collective-permute-start.20) | collective-permute-done | bytes 327712 | tf_op jit(solution)/shard_map/ppermute | solution.py:21
  165.1 1.6 collective-permute-start.15
  166.6 1.8 collective-permute-start.17
  168.4 1.9 collective-permute-start.16
  170.3 6.1 %collective-permute-done.15 = bf16[160,1024]{1,0:T(8,128)(2,1)S(1)} collective-permute-done((bf16[160,1024]{1,0:T(8,128)(2,1)S(1)}, bf16[160,1024]{1,0:T(8,128)(2,1)S(1)}, u32[]{:S(2)}, u32[]{:S(2)}) %collective-permute-start.15) | collective-permute-done | bytes 327712 | tf_op jit(solution)/shard_map/ppermute | solution.py:21
  176.4 6.3 %collective-permute-done.17 = bf16[160,1024]{1,0:T(8,128)(2,1)S(1)} collective-permute-done((bf16[160,1024]{1,0:T(8,128)(2,1)S(1)}, bf16[160,1024]{1,0:T(8,128)(2,1)S(1)}, u32[]{:S(2)}, u32[]{:S(2)}) %collective-permute-start.17) | collective-permute-done | bytes 327712 | tf_op jit(solution)/shard_map/ppermute | solution.py:21
  182.7 1.7 collective-permute-done.16
  185.4 1.2 collective-permute-start.23
  186.6 2.1 collective-permute-start.25
  189.3 1.7 collective-permute-start.18
  191.0 4.8 %collective-permute-done.23 = bf16[160,512]{1,0:T(8,128)(2,1)S(1)} collective-permute-done((bf16[160,512]{1,0:T(8,128)(2,1)S(1)}, bf16[160,512]{1,0:T(8,128)(2,1)S(1)}, u32[]{:S(2)}, u32[]{:S(2)}) %collective-permute-start.23) | collective-permute-done | bytes 163872 | tf_op jit(solution)/shard_map/ppermute | solution.py:21
  197.1 5.8 %collective-permute-done.26.refs_3_ = bf16[160,512]{1,0:T(8,128)(2,1)S(1)} collective-permute-done((bf16[160,512]{1,0:T(8,128)(2,1)S(1)}, bf16[160,512]{1,0:T(8,128)(2,1)S(1)}, u32[]{:S(2)}, u32[]{:S(2)}) %collective-permute-start.26) | collective-permute-done | bytes 163872 | tf_op jit(solution)/shard_map/ppermute | solution.py:21
  203.5 2.3 %place.1 = bf16[512,640]{1,0:T(8,128)(2,1)} custom-call(bf16[160,512]{1,0:T(8,128)(2,1)} %add_convert_fusion.3.refs_0_, bf16[160,512]{1,0:T(8,128)(2,1)} %copy-done.8, bf16[160,512]{1,0:T(8,128)(2,1)} %copy-done.7, bf16[160,512]{1,0:T(8,128)(2,1)} %copy-done.9), custom_call_target="tpu_custom_call" | custom-call | tf_op jit(solution)/shard_map/place/pallas_call | solution.py:234
  (98 shorter events, 15.3 us)
Async XLA Ops:
  7.2 5.9 %copy-start.10 = (s32[16,8]{0,1:T(8,128)S(1)}, s32[16,8]{0,1:T(8,128)}, u32[]{:S(2)}) copy-start(s32[16,8]{0,1:T(8,128)} %param.15) | copy-start | bytes 1540
  7.2 8.2 %copy-start.11 = (bf16[2,8,20]{2,1,0:T(8,128)(2,1)S(1)}, bf16[2,8,20]{2,1,0:T(8,128)(2,1)}, u32[]{:S(2)}) copy-start(bf16[2,8,20]{2,1,0:T(8,128)(2,1)} %param.16) | copy-start | bytes 1924
  7.2 56.1 %all-gather.5.cloned.1.call-start = ((), (), s32[]{:S(2)}) async-start(), calls=%async_computation.1 | async-start | bytes 2949120 | tf_op jit(solution)/shard_map/all_gather | solution.py:125
  10.8 20.6 %collective-permute-start = (bf16[160,256]{1,0:T(8,128)(2,1)S(1)}, bf16[160,256]{1,0:T(8,128)(2,1)S(1)}, u32[]{:S(2)}, u32[]{:S(2)}) collective-permute-start(bf16[160,256]{1,0:T(8,128)(2,1)S(1)} %get-tuple-element.55), channel_id=1, source_target_pairs={{0,24},{8,0},{16,8},{24,16},{1,25},{9,1},{17,9},{25,17},{2,26},{10... | collective-permute-start | bytes 245768 | tf_op jit(solution)/shard_map/ppermute | solution.py:21
  13.1 16.7 %collective-permute-start.1 = (bf16[160,256]{1,0:T(8,128)(2,1)S(1)}, bf16[160,256]{1,0:T(8,128)(2,1)S(1)}, u32[]{:S(2)}, u32[]{:S(2)}) collective-permute-start(bf16[160,256]{1,0:T(8,128)(2,1)S(1)} %get-tuple-element.55), channel_id=1, source_target_pairs={{0,8},{8,16},{16,24},{24,0},{1,9},{9,17},{17,25},{25,1},{2,10},{10... | collective-permute-start | bytes 245768 | tf_op jit(solution)/shard_map/ppermute | solution.py:21
  16.4 51.4 %all-to-all-start = ((bf16[32,8,768]{2,1,0:T(8,128)(2,1)}), bf16[32,8,768]{2,1,0:T(8,128)(2,1)S(1)}, u32[]{:S(2)}, u32[]{:S(2)}) async-start(bf16[32,8,768]{2,1,0:T(8,128)(2,1)} %pad_maximum_fusion), calls=%async_computation | async-start | bytes 786432 | tf_op jit(solution)/shard_map/all_to_all | solution.py:141
  28.7 85.2 %all-gather.7.cloned.1.call-start = ((), (), s32[]{:S(2)}) async-start(), calls=%async_computation.2 | async-start | bytes 2949120 | tf_op jit(solution)/shard_map/all_gather | solution.py:128
  29.8 5.0 %collective-permute-start.2 = (bf16[160,256]{1,0:T(8,128)(2,1)S(1)}, bf16[160,256]{1,0:T(8,128)(2,1)S(1)}, u32[]{:S(2)}, u32[]{:S(2)}) collective-permute-start(bf16[160,256]{1,0:T(8,128)(2,1)S(1)} %collective-permute-done.1), channel_id=1, source_target_pairs={{0,8},{8,16},{16,24},{24,0},{1,9},{9,17},{17,25},{25,1},{2,10},{10... | collective-permute-start | bytes 245768 | tf_op jit(solution)/shard_map/ppermute | solution.py:21
  67.8 8.1 %copy-start.4 = (bf16[32,8,768]{2,1,0:T(8,128)(2,1)}, bf16[32,8,768]{2,1,0:T(8,128)(2,1)S(1)}, u32[]{:S(2)}) copy-start(bf16[32,8,768]{2,1,0:T(8,128)(2,1)S(1)} %all-to-all-done) | copy-start | bytes 1179652
  68.5 7.4 %collective-permute-start.3 = (bf16[64,640]{1,0:T(8,128)(2,1)S(1)}, bf16[64,640]{1,0:T(8,128)(2,1)S(1)}, u32[]{:S(2)}, u32[]{:S(2)}) collective-permute-start(bf16[64,640]{1,0:T(8,128)(2,1)S(1)} %bitcast_select_fusion), channel_id=1, source_target_pairs={{0,8},{8,0},{16,24},{24,16},{1,9},{9,1},{17,25},{25,17},{2,10},{10... | collective-permute-start | bytes 245768 | tf_op jit(solution)/shard_map/ppermute | solution.py:144
  78.0 21.4 %collective-permute-start.5 = (bf16[8,160,384]{2,1,0:T(8,128)(2,1)S(1)}, bf16[8,160,384]{2,1,0:T(8,128)(2,1)S(1)}, u32[]{:S(2)}, u32[]{:S(2)}) collective-permute-start(bf16[8,160,384]{2,1,0:T(8,128)(2,1)S(1)} %slice.95.rest_1_), channel_id=1, source_target_pairs={{0,24},{8,0},{16,8},{24,16},{1,25},{9,1},{17,9},{25,17},{2,26},{10... | collective-permute-start | bytes 2949128 | tf_op jit(solution)/shard_map/ppermute | solution.py:21
  79.6 21.7 %collective-permute-start.4 = (bf16[8,160,384]{2,1,0:T(8,128)(2,1)S(1)}, bf16[8,160,384]{2,1,0:T(8,128)(2,1)S(1)}, u32[]{:S(2)}, u32[]{:S(2)}) collective-permute-start(bf16[8,160,384]{2,1,0:T(8,128)(2,1)S(1)} %slice.95.rest_1_), channel_id=1, source_target_pairs={{0,8},{8,16},{16,24},{24,0},{1,9},{9,17},{17,25},{25,1},{2,10},{10... | collective-permute-start | bytes 2949128 | tf_op jit(solution)/shard_map/ppermute | solution.py:21
  100.2 13.6 %collective-permute-start.7 = (bf16[4,160,384]{2,1,0:T(8,128)(2,1)}, bf16[4,160,384]{2,1,0:T(8,128)(2,1)S(1)}, u32[]{:S(2)}, u32[]{:S(2)}) collective-permute-start(bf16[4,160,384]{2,1,0:T(8,128)(2,1)} %slice.121), channel_id=1, source_target_pairs={{0,24},{8,0},{16,8},{24,16},{1,25},{9,1},{17,9},{25,17},{2,26},{10... | collective-permute-start | bytes 1474568 | tf_op jit(solution)/shard_map/ppermute | solution.py:21
  102.1 11.7 %collective-permute-start.6 = (bf16[4,160,384]{2,1,0:T(8,128)(2,1)}, bf16[4,160,384]{2,1,0:T(8,128)(2,1)}, u32[]{:S(2)}, u32[]{:S(2)}) collective-permute-start(bf16[4,160,384]{2,1,0:T(8,128)(2,1)} %slice.120), channel_id=1, source_target_pairs={{0,8},{8,16},{16,24},{24,0},{1,9},{9,17},{17,25},{25,1},{2,10},{10... | collective-permute-start | bytes 1474568 | tf_op jit(solution)/shard_map/ppermute | solution.py:21
  109.0 2.7 %copy-start.3 = (bf16[1280,1024]{1,0:T(8,128)(2,1)S(1)}, bf16[1280,1024]{1,0:T(8,128)(2,1)}, u32[]{:S(2)}) copy-start(bf16[1280,1024]{1,0:T(8,128)(2,1)} %all-gather.5.cloned.1.call-done) | copy-start | bytes 7864324
  113.9 2.5 %copy-start = (bf16[512,5120]{1,0:T(8,128)(2,1)S(1)}, bf16[512,5120]{1,0:T(8,128)(2,1)}, u32[]{:S(2)}) copy-start(bf16[512,5120]{1,0:T(8,128)(2,1)} %fusion.3.xm_ref) | copy-start | bytes 15728644
  116.4 1.7 copy-start.1
  118.1 0.9 copy-start.2
  119.0 9.1 %copy-start.6 = (bf16[4,160,640]{2,1,0:T(8,128)(2,1)S(1)}, bf16[4,160,640]{2,1,0:T(8,128)(2,1)}, u32[]{:S(2)}) copy-start(bf16[4,160,640]{2,1,0:T(8,128)(2,1)} %get-tuple-element.28) | copy-start | bytes 2457604
  128.1 3.5 %copy-start.5 = (bf16[4,160,640]{2,1,0:T(8,128)(2,1)S(1)}, bf16[4,160,640]{2,1,0:T(8,128)(2,1)}, u32[]{:S(2)}) copy-start(bf16[4,160,640]{2,1,0:T(8,128)(2,1)} %get-tuple-element.27) | copy-start | bytes 2457604
  128.8 2.7 %collective-permute-start.10 = (bf16[4,160,512]{2,1,0:T(8,128)(2,1)S(1)}, bf16[4,160,512]{2,1,0:T(8,128)(2,1)S(1)}, u32[]{:S(2)}, u32[]{:S(2)}) collective-permute-start(bf16[4,160,512]{2,1,0:T(8,128)(2,1)S(1)} %convolution_convert_fusion.4), channel_id=1, source_target_pairs={{0,1},{1,0},{2,3},{3,2},{4,5},{5,4},{6,7},{7,6},{8,9},{9,8},{10,11... | collective-permute-start | bytes 1966088 | tf_op jit(solution)/shard_map/ppermute | solution.py:207
  128.9 17.2 %collective-permute-start.9 = (bf16[512,640]{1,0:T(8,128)(2,1)S(1)}, bf16[512,640]{1,0:T(8,128)(2,1)S(1)}, u32[]{:S(2)}, u32[]{:S(2)}) collective-permute-start(bf16[512,640]{1,0:T(8,128)(2,1)S(1)} %query_attend.1), channel_id=1, source_target_pairs={{0,24},{8,0},{16,8},{24,16},{1,25},{9,1},{17,9},{25,17},{2,26},{10... | collective-permute-start | bytes 1966088 | tf_op jit(solution)/shard_map/ppermute | solution.py:21
  131.6 18.1 %collective-permute-start.8 = (bf16[512,640]{1,0:T(8,128)(2,1)S(1)}, bf16[512,640]{1,0:T(8,128)(2,1)S(1)}, u32[]{:S(2)}, u32[]{:S(2)}) collective-permute-start(bf16[512,640]{1,0:T(8,128)(2,1)S(1)} %query_attend.1), channel_id=1, source_target_pairs={{0,8},{8,16},{16,24},{24,0},{1,9},{9,17},{17,25},{25,1},{2,10},{10... | collective-permute-start | bytes 1966088 | tf_op jit(solution)/shard_map/ppermute | solution.py:21
  132.4 17.3 %collective-permute-start.13 = (bf16[160,512]{1,0:T(8,128)(2,1)S(1)}, bf16[160,512]{1,0:T(8,128)(2,1)S(1)}, u32[]{:S(2)}, u32[]{:S(2)}) collective-permute-start(bf16[160,512]{1,0:T(8,128)(2,1)S(1)} %get-tuple-element.48), channel_id=1, source_target_pairs={{0,6},{2,0},{4,2},{6,4},{1,7},{3,1},{5,3},{7,5},{8,14},{10,8},{12,... | collective-permute-start | bytes 491528 | tf_op jit(solution)/shard_map/ppermute | solution.py:21
  135.2 14.5 %collective-permute-start.12 = (bf16[160,512]{1,0:T(8,128)(2,1)S(1)}, bf16[160,512]{1,0:T(8,128)(2,1)S(1)}, u32[]{:S(2)}, u32[]{:S(2)}) collective-permute-start(bf16[160,512]{1,0:T(8,128)(2,1)S(1)} %get-tuple-element.49), channel_id=1, source_target_pairs={{0,4},{2,6},{4,0},{6,2},{1,5},{3,7},{5,1},{7,3},{8,12},{10,14},{12... | collective-permute-start | bytes 491528 | tf_op jit(solution)/shard_map/ppermute | solution.py:21
  136.0 13.7 %collective-permute-start.11 = (bf16[160,512]{1,0:T(8,128)(2,1)S(1)}, bf16[160,512]{1,0:T(8,128)(2,1)S(1)}, u32[]{:S(2)}, u32[]{:S(2)}) collective-permute-start(bf16[160,512]{1,0:T(8,128)(2,1)S(1)} %get-tuple-element.50), channel_id=1, source_target_pairs={{0,2},{2,4},{4,6},{6,0},{1,3},{3,5},{5,7},{7,1},{8,10},{10,12},{12... | collective-permute-start | bytes 491528 | tf_op jit(solution)/shard_map/ppermute | solution.py:21
  150.9 3.5 %collective-permute-start.14 = (bf16[4,160,1024]{2,1,0:T(8,128)(2,1)S(1)}, bf16[4,160,1024]{2,1,0:T(8,128)(2,1)S(1)}, u32[]{:S(2)}, u32[]{:S(2)}) collective-permute-start(bf16[4,160,1024]{2,1,0:T(8,128)(2,1)S(1)} %convolution_convert_fusion), channel_id=1, source_target_pairs={{0,1},{1,0},{2,3},{3,2},{4,5},{5,4},{6,7},{7,6},{8,9},{9,8},{10,11... | collective-permute-start | bytes 3932168 | tf_op jit(solution)/shard_map/ppermute | solution.py:207
  151.1 10.7 %collective-permute-start.21 = (bf16[256,640]{1,0:T(8,128)(2,1)S(1)}, bf16[256,640]{1,0:T(8,128)(2,1)S(1)}, u32[]{:S(2)}, u32[]{:S(2)}) collective-permute-start(bf16[256,640]{1,0:T(8,128)(2,1)S(1)} %slice.133), channel_id=1, source_target_pairs={{0,24},{8,0},{16,8},{24,16},{1,25},{9,1},{17,9},{25,17},{2,26},{10... | collective-permute-start | bytes 983048 | tf_op jit(solution)/shard_map/ppermute | solution.py:21
  154.1 10.1 %collective-permute-start.20 = (bf16[256,640]{1,0:T(8,128)(2,1)S(1)}, bf16[256,640]{1,0:T(8,128)(2,1)S(1)}, u32[]{:S(2)}, u32[]{:S(2)}) collective-permute-start(bf16[256,640]{1,0:T(8,128)(2,1)S(1)} %slice.132), channel_id=1, source_target_pairs={{0,8},{8,16},{16,24},{24,0},{1,9},{9,17},{17,25},{25,1},{2,10},{10... | collective-permute-start | bytes 983048 | tf_op jit(solution)/shard_map/ppermute | solution.py:21
  165.0 19.6 %collective-permute-start.22 = (bf16[4,160,512]{2,1,0:T(8,128)(2,1)S(1)}, bf16[4,160,512]{2,1,0:T(8,128)(2,1)S(1)}, u32[]{:S(2)}, u32[]{:S(2)}) collective-permute-start(bf16[4,160,512]{2,1,0:T(8,128)(2,1)S(1)} %convolution_convert_fusion.2), channel_id=1, source_target_pairs={{0,1},{1,0},{2,3},{3,2},{4,5},{5,4},{6,7},{7,6},{8,9},{9,8},{10,11... | collective-permute-start | bytes 1966088 | tf_op jit(solution)/shard_map/ppermute | solution.py:207
  165.1 11.3 %collective-permute-start.15 = (bf16[160,1024]{1,0:T(8,128)(2,1)S(1)}, bf16[160,1024]{1,0:T(8,128)(2,1)S(1)}, u32[]{:S(2)}, u32[]{:S(2)}) collective-permute-start(bf16[160,1024]{1,0:T(8,128)(2,1)S(1)} %get-tuple-element.42), channel_id=1, source_target_pairs={{0,2},{2,4},{4,6},{6,0},{1,3},{3,5},{5,7},{7,1},{8,10},{10,12},{12... | collective-permute-start | bytes 983048 | tf_op jit(solution)/shard_map/ppermute | solution.py:21
  166.6 16.1 %collective-permute-start.17 = (bf16[160,1024]{1,0:T(8,128)(2,1)S(1)}, bf16[160,1024]{1,0:T(8,128)(2,1)S(1)}, u32[]{:S(2)}, u32[]{:S(2)}) collective-permute-start(bf16[160,1024]{1,0:T(8,128)(2,1)S(1)} %get-tuple-element.43), channel_id=1, source_target_pairs={{0,6},{2,0},{4,2},{6,4},{1,7},{3,1},{5,3},{7,5},{8,14},{10,8},{12,... | collective-permute-start | bytes 983048 | tf_op jit(solution)/shard_map/ppermute | solution.py:21
  168.4 16.0 %collective-permute-start.16 = (bf16[160,1024]{1,0:T(8,128)(2,1)S(1)}, bf16[160,1024]{1,0:T(8,128)(2,1)S(1)}, u32[]{:S(2)}, u32[]{:S(2)}) collective-permute-start(bf16[160,1024]{1,0:T(8,128)(2,1)S(1)} %get-tuple-element.44), channel_id=1, source_target_pairs={{0,4},{2,6},{4,0},{6,2},{1,5},{3,7},{5,1},{7,3},{8,12},{10,14},{12... | collective-permute-start | bytes 983048 | tf_op jit(solution)/shard_map/ppermute | solution.py:21
  185.4 10.5 %collective-permute-start.23 = (bf16[160,512]{1,0:T(8,128)(2,1)S(1)}, bf16[160,512]{1,0:T(8,128)(2,1)S(1)}, u32[]{:S(2)}, u32[]{:S(2)}) collective-permute-start(bf16[160,512]{1,0:T(8,128)(2,1)S(1)} %get-tuple-element.45), channel_id=1, source_target_pairs={{0,2},{2,4},{4,6},{6,0},{1,3},{3,5},{5,7},{7,1},{8,10},{10,12},{12... | collective-permute-start | bytes 491528 | tf_op jit(solution)/shard_map/ppermute | solution.py:21
  186.6 9.2 %collective-permute-start.25 = (bf16[160,512]{1,0:T(8,128)(2,1)S(1)}, bf16[160,512]{1,0:T(8,128)(2,1)S(1)}, u32[]{:S(2)}, u32[]{:S(2)}) collective-permute-start(bf16[160,512]{1,0:T(8,128)(2,1)S(1)} %get-tuple-element.46), channel_id=1, source_target_pairs={{0,6},{2,0},{4,2},{6,4},{1,7},{3,1},{5,3},{7,5},{8,14},{10,8},{12,... | collective-permute-start | bytes 491528 | tf_op jit(solution)/shard_map/ppermute | solution.py:21
  188.7 7.2 %collective-permute-start.24 = (bf16[160,512]{1,0:T(8,128)(2,1)S(1)}, bf16[160,512]{1,0:T(8,128)(2,1)S(1)}, u32[]{:S(2)}, u32[]{:S(2)}) collective-permute-start(bf16[160,512]{1,0:T(8,128)(2,1)S(1)} %get-tuple-element.47), channel_id=1, source_target_pairs={{0,4},{2,6},{4,0},{6,2},{1,5},{3,7},{5,1},{7,3},{8,12},{10,14},{12... | collective-permute-start | bytes 491528 | tf_op jit(solution)/shard_map/ppermute | solution.py:21
  188.9 8.1 %collective-permute-start.19 = (bf16[160,512]{1,0:T(8,128)(2,1)S(1)}, bf16[160,512]{1,0:T(8,128)(2,1)S(1)}, u32[]{:S(2)}, u32[]{:S(2)}) collective-permute-start(bf16[160,512]{1,0:T(8,128)(2,1)S(1)} %get-tuple-element.52), channel_id=1, source_target_pairs={{0,8},{8,16},{16,24},{24,0},{1,9},{9,17},{17,25},{25,1},{2,10},{10... | collective-permute-start | bytes 491528 | tf_op jit(solution)/shard_map/ppermute | solution.py:21
  189.3 7.8 %collective-permute-start.18 = (bf16[160,512]{1,0:T(8,128)(2,1)S(1)}, bf16[160,512]{1,0:T(8,128)(2,1)S(1)}, u32[]{:S(2)}, u32[]{:S(2)}) collective-permute-start(bf16[160,512]{1,0:T(8,128)(2,1)S(1)} %get-tuple-element.53), channel_id=1, source_target_pairs={{0,24},{8,0},{16,8},{24,16},{1,25},{9,1},{17,9},{25,17},{2,26},{10... | collective-permute-start | bytes 491528 | tf_op jit(solution)/shard_map/ppermute | solution.py:21
  195.9 6.9 %collective-permute-start.26 = (bf16[160,512]{1,0:T(8,128)(2,1)S(1)}, bf16[160,512]{1,0:T(8,128)(2,1)S(1)}, u32[]{:S(2)}, u32[]{:S(2)}) collective-permute-start(bf16[160,512]{1,0:T(8,128)(2,1)S(1)} %fusion.16), channel_id=1, source_target_pairs={{0,16},{8,24},{16,0},{24,8},{1,17},{9,25},{17,1},{25,9},{2,18},{10... | collective-permute-start | bytes 491528 | tf_op jit(solution)/shard_map/ppermute | solution.py:21
  197.1 5.8 %copy-start.7 = (bf16[160,512]{1,0:T(8,128)(2,1)}, bf16[160,512]{1,0:T(8,128)(2,1)S(1)}, u32[]{:S(2)}) copy-start(bf16[160,512]{1,0:T(8,128)(2,1)S(1)} %collective-permute-done.19.refs_2_) | copy-start | bytes 491524
  197.1 5.8 %copy-start.8 = (bf16[160,512]{1,0:T(8,128)(2,1)}, bf16[160,512]{1,0:T(8,128)(2,1)S(1)}, u32[]{:S(2)}) copy-start(bf16[160,512]{1,0:T(8,128)(2,1)S(1)} %collective-permute-done.18.refs_1_) | copy-start | bytes 491524
  202.8 0.7 copy-start.9
Sparse Core Ops, SparseCore 0:
  10.4 52.8 all-gather.4
  65.0 40.6 all-gather.6
where the time goes:
time: 214 us; the launch traced here: 213 us
  waiting for transfers between devices  95.3 us (45%)
  starting transfers between devices  43.5 us (20%)
  other arithmetic  21.4 us (10%)
  local copies, waits for them, and re-layouts  20 us (9%)
  between operations  15.8 us (7%)
  Pallas kernels  11.4 us (5%)
  matrix products  5.25 us (2%)
    ppermute x23, waiting for transfers between devices, shift(): return lax.ppermute(array, axis, [(i, (i + by) % n) for i in range(n)])  67.7 us
    ppermute x23, starting transfers between devices, shift(): return lax.ppermute(array, axis, [(i, (i + by) % n) for i in range(n)])  30.2 us
    all_gather x1, waiting for transfers between devices, shards(): joint = lax.all_gather(joint, 'mem_0', axis=0, tiled=False)  27.6 us
    all_to_all x1, starting transfers between devices, shards(): lax.all_to_all(outgoing, MEM, split_axis=0, concat_axis=0, tiled=True)  12.3 us
    pallas_call x1, Pallas kernels, shards(): pl.pallas_call(functools.partial(attend_kernel, plan, rows, nx), out_shap...  9.1 us
    convert_element_type x1, other arithmetic, shards(): (values * factor * (1.0 + modrow[0]) + modrow[1]).astype(jnp.bfloat16)  6.82 us
    unnamed x24, local copies, waits for them, and re-layouts  5.81 us
    dot_general x6, matrix products, term(): lax.dot_general(weight, group, (((2,), (1,)), ((), ())), preferred_elemen...  5.25 us
  transfers between devices with their start and end apart: 30, of which 12 were waited for; matrix products, arithmetic and copies ran while one was open for 16% of the time, Pallas kernels for 0%

commit v1 on v0

--- a/solution.py
+++ b/solution.py
@@ -43,36 +43,46 @@
     return jnp.stack([next(a for a, off, _ in got if off % n == i) for i in range(n)])
 
 
-def attend_kernel(plan, rows, nx, xm_ref, k_ref, v_ref, *rest):
-    pieces, (out_ref, w_ref, acc_ref, sems) = rest[: len(plan)], rest[len(plan):]
-    x = lax.axis_index("mem_1")
-    copies = []
-    for piece, entries in zip(pieces, plan):
-        for index, at_z, off_x, lane, lanes in entries:
+def attend_kernel(plan, rows, nx, chunks, xm_ref, k_ref, v_ref, *rest):
+    pieces, rest = rest[: len(plan)], rest[len(plan):]
+    keep_ref, give_ref, x_ref, w_ref, acc_ref, held_ref, x_sems, w_sems = rest
+    x, core = lax.axis_index("mem_1"), lax.axis_index("tp_1")
+    depth = w_ref.shape[0]
+    step = depth // chunks
+    entries = [
+        (piece, *entry) for piece, part in zip(pieces, plan) for entry in part
+    ]
+    per_chunk = step // (rows * nx)
+    for chunk in range(chunks):
+        pltpu.make_async_copy(
+            xm_ref.at[:, pl.ds(chunk * step, step)],
+            x_ref.at[:, pl.ds(chunk * step, step)],
+            x_sems.at[chunk],
+        ).start()
+        for piece, index, at_z, off_x, lane, lanes in entries:
+            if at_z // per_chunk != chunk:
+                continue
             block = at_z * nx + lax.rem(x + (off_x % nx), nx)
             start = pl.multiple_of(block * rows, 32)
-            copy = pltpu.make_async_copy(
+            pltpu.make_async_copy(
                 piece.at[index],
                 w_ref.at[pl.ds(start, rows), pl.ds(lane, lanes)],
-                sems.at[len(copies)],
-            )
-            copy.start()
-            copies.append(copy)
-    for copy in copies:
-        copy.wait()
-    depth = w_ref.shape[0]
-    step = depth // 4
+                w_sems.at[chunk],
+            ).start()
 
     def accumulate(i, carry):
         at = pl.ds(pl.multiple_of(i * step, 128), step)
-        acc_ref[...] += jnp.dot(xm_ref[:, at], w_ref[at, :], preferred_element_type=jnp.float32)
+        pltpu.make_async_copy(x_ref.at[:, at], x_ref.at[:, at], x_sems.at[i]).wait()
+        pltpu.make_async_copy(w_ref.at[at, :], w_ref.at[at, :], w_sems.at[i]).wait()
+        acc_ref[...] += jnp.dot(x_ref[:, at], w_ref[at, :], preferred_element_type=jnp.float32)
         return carry
 
     acc_ref[...] = jnp.zeros_like(acc_ref)
-    lax.fori_loop(0, 4, accumulate, 0)
+    lax.fori_loop(0, chunks, accumulate, 0)
+    half = acc_ref.shape[0] // 2
 
     def attend(i, carry):
-        part = pl.ds(pl.multiple_of(i * 2 * HEAD_SIZE, HEAD_SIZE), 2 * HEAD_SIZE)
+        part = pl.ds(pl.multiple_of(i * half, half), half)
         for head in range(w_ref.shape[1] // HEAD_SIZE):
             at = pl.ds(head * HEAD_SIZE, HEAD_SIZE)
             query = acc_ref[part, at].astype(jnp.bfloat16)
@@ -81,22 +91,28 @@
             ) * HEAD_SIZE ** (-0.5)
             expo = jnp.exp(logits - jnp.max(logits, axis=-1, keepdims=True))
             probs = (expo / jnp.sum(expo, axis=-1, keepdims=True)).astype(jnp.bfloat16)
-            out_ref[part, at] = jnp.dot(
+            held_ref[part, at] = jnp.dot(
                 probs, v_ref[:, at], preferred_element_type=jnp.float32
             ).astype(jnp.bfloat16)
         return carry
 
-    lax.fori_loop(0, acc_ref.shape[0] // (2 * HEAD_SIZE), attend, 0)
+    lax.fori_loop(0, 2, attend, 0)
+    keep_ref[...] = held_ref[pl.ds(pl.multiple_of(core * half, half), half), :]
+    give_ref[...] = held_ref[pl.ds(pl.multiple_of((1 - core) * half, half), half), :]
 
 
 def place_kernel(offs, nx, *refs):
     pieces, (out_ref, held) = refs[: len(offs)], refs[len(offs):]
-    x = lax.axis_index("mem_1")
-    for piece, off in zip(pieces, offs):
-        rows = piece.shape[0]
-        start = lax.rem(x + (off % nx), nx) * rows
-        held[pl.ds(pl.multiple_of(start, 32), rows), :] = piece[...].astype(jnp.float32)
-    out_ref[...] = held[...].T.astype(jnp.bfloat16)
+    x, core = lax.axis_index("mem_1"), lax.axis_index("tp_1")
+    half = out_ref.shape[0] // 2
+    for same in range(2):
+        for piece, (off, mine) in zip(pieces, offs):
+            if mine == same:
+                rows = piece.shape[0]
+                start = lax.rem(x + (off % nx), nx) * rows
+                held[pl.ds(pl.multiple_of(start, 32), rows), :] = piece[...].astype(jnp.float32)
+        to = core if same else 1 - core
+        out_ref[pl.ds(pl.multiple_of(to * half, half), half), :] = held[...].T.astype(jnp.bfloat16)
 
 
 def shards(
@@ -152,7 +168,10 @@
     modulated = (values * factor * (1.0 + modrow[0]) + modrow[1]).astype(jnp.bfloat16)
 
     joint, modulated, keys, vals = lax.optimization_barrier((joint, modulated, keys, vals))
-    qb_all = around(joint[:, :, :late], "mem_1", False)
+    own = joint[:, :, :late]
+    fore, back = shift(own, "mem_1", 1), shift(own, "mem_1", -1)
+    low, high = shift(fore[: nz // 2], "mem_1", 1), shift(back[nz // 2:], "mem_1", -1)
+    qb_all = ((own, 0, 0), (fore, -1, 0), (back, 1, 0), (low, 2, 0), (high, 2, nz // 2))
 
     fresh = incoming[:, :, width: width + extra].reshape(n_mem, slots_rows, 2, extra // 2)
     fresh = fresh.transpose(2, 1, 0, 3).reshape(2, slots_rows, width)
@@ -163,33 +182,46 @@
 
     ny, nc = lax.axis_size("tp_0"), lax.axis_size("tp_1")
     core = lax.axis_index("tp_1")
-    weight = joint[:, :, late:].reshape(ny, nc, rows, width)
+    swap = [(0, 1), (1, 0)]
+    weight = joint[:, :, late:]
+    away = lax.ppermute(weight, "tp_1", swap)
+    weight = jnp.concatenate([weight, away], axis=2)
+    weight = weight.reshape(ny, nc, rows, 2 * width)
     weight = lax.dynamic_slice_in_dim(
         jnp.concatenate([weight, weight], axis=0), lax.axis_index("tp_0"), ny, 0
     )
-    mine = lax.dynamic_index_in_dim(weight, core, 1, keepdims=False)
-    other = lax.dynamic_index_in_dim(weight, 1 - core, 1, keepdims=False)
-    modulated, mine, other, updated_store = lax.optimization_barrier(
-        (modulated, mine, other, updated_store)
+    weight = jnp.concatenate(
+        [
+            lax.dynamic_index_in_dim(weight, core, 1, keepdims=False),
+            lax.dynamic_index_in_dim(weight, 1 - core, 1, keepdims=False),
+        ],
+        axis=1,
+    )
+    modulated, weight, updated_store = lax.optimization_barrier(
+        (modulated, weight, updated_store)
     )
 
     pieces = [q_a]
     plan = [[((i, j), i, j, 0, cut) for i in range(nz) for j in range(nx)]]
-    for array, off, part in qb_all:
-        low = 0 if part is None else part[0]
+    for array, off, low in qb_all:
         pieces.append(array)
         plan.append([(i, low + i, off, cut, late) for i in range(array.shape[0])])
-    copies = sum(len(entries) for entries in plan)
+    chunks = 4
     vmem = pl.BlockSpec(memory_space=pltpu.VMEM)
-    attended = pl.pallas_call(
-        functools.partial(attend_kernel, plan, rows, nx),
-        out_shape=jax.ShapeDtypeStruct((count, width), jnp.bfloat16),
-        in_specs=[vmem] * 3 + [pl.BlockSpec(memory_space=pl.ANY)] * len(pieces),
-        out_specs=vmem,
+    hbm = pl.BlockSpec(memory_space=pltpu.HBM)
+    half = jax.ShapeDtypeStruct((count // 2, width), jnp.bfloat16)
+    keep, give = pl.pallas_call(
+        functools.partial(attend_kernel, plan, rows, nx, chunks),
+        out_shape=(half, half),
+        in_specs=[hbm, vmem, vmem] + [hbm] * len(pieces),
+        out_specs=(vmem, vmem),
         scratch_shapes=[
+            pltpu.VMEM((count, model), jnp.bfloat16),
             pltpu.VMEM((model, width), jnp.bfloat16),
             pltpu.VMEM((count, width), jnp.float32),
-            pltpu.SemaphoreType.DMA((copies,)),
+            pltpu.VMEM((count, width), jnp.bfloat16),
+            pltpu.SemaphoreType.DMA((chunks,)),
+            pltpu.SemaphoreType.DMA((chunks,)),
         ],
         compiler_params=pltpu.CompilerParams(vmem_limit_bytes=40 * 1024 * 1024),
         cost_estimate=pl.CostEstimate(
@@ -198,45 +230,51 @@
         name="query_attend",
     )(modulated, keys, vals, *pieces)
 
-    def term(weight, group):
-        return lax.dot_general(
-            weight, group, (((2,), (1,)), ((), ())), preferred_element_type=jnp.float32
-        ).astype(jnp.bfloat16)
-
-    def paired(group):
-        away = lax.ppermute(term(other, group), "tp_1", [(0, 1), (1, 0)])
-        here = term(mine, group)
-        pair = (here.astype(jnp.float32) + away.astype(jnp.float32)).astype(jnp.bfloat16)
-        return [pair[d] for d in range(ny)]
+    attended = jnp.concatenate([keep, lax.ppermute(give, "tp_1", swap)], axis=1)
+
+    def terms(group):
+        return [
+            lax.dot_general(
+                weight[d], group, (((1,), (1,)), ((), ())), preferred_element_type=jnp.float32
+            ).astype(jnp.bfloat16)
+            for d in range(ny)
+        ]
 
     def sent(parts):
         return [parts[0]] + [shift(parts[d], "tp_0", d) for d in range(1, ny)]
 
     def summed(parts):
-        return sum(part.astype(jnp.float32) for part in parts).astype(jnp.bfloat16)
+        total = sum(part.astype(jnp.float32) for part in parts).astype(jnp.bfloat16)
+        return total[:rows], total[rows:]
+
+    def returned(block, by, mine):
+        pairs = [
+            (i * nc + c, (i + by) % nx * nc + (c if mine else 1 - c))
+            for i in range(nx)
+            for c in range(nc)
+        ]
+        return lax.ppermute(block, ("mem_1", "tp_1"), pairs)
 
     left, right = shift(attended, "mem_1", 1), shift(attended, "mem_1", -1)
-    own_parts = sent(paired(attended))
-    far = [shift(left[: count // 2], "mem_1", 1), shift(right[count // 2:], "mem_1", -1)]
-    left, right, own_parts = lax.optimization_barrier((left, right, own_parts))
-    near_parts = paired(jnp.concatenate([left, right], axis=0))
-    far, _ = lax.optimization_barrier((far, near_parts))
-    near_parts = sent(near_parts)
-    far_parts = sent(paired(jnp.concatenate(far, axis=0)))
-    out_own, near, out_far = summed(own_parts), summed(near_parts), summed(far_parts)
-    blocks = [
-        out_own,
-        shift(near[:, :count], "mem_1", -1),
-        shift(near[:, count:], "mem_1", 1),
-        shift(out_far, "mem_1", 2),
-    ]
-    places = (0, 1, -1, 2)
+    own_parts = sent(terms(attended))
+    quarter = count // 4
+    far = [shift(left[:quarter], "mem_1", 1), shift(right[quarter:], "mem_1", -1)]
+    near_parts = sent(terms(jnp.concatenate([left, right], axis=0)))
+    far_parts = sent(terms(jnp.concatenate(far, axis=0)))
+    blocks, places = [], []
+    for parts, bys in ((own_parts, (0,)), (near_parts, (-1, 1)), (far_parts, (2,))):
+        both = summed(parts)
+        for i, by in enumerate(bys):
+            for mine in (1, 0):
+                block = both[1 - mine][:, i * 2 * quarter: (i + 1) * 2 * quarter]
+                blocks.append(block if mine and not by else returned(block, by, mine))
+                places.append((-by, mine))
     memory_out = pl.pallas_call(
         functools.partial(place_kernel, places, nx),
         out_shape=jax.ShapeDtypeStruct((count, width), jnp.bfloat16),
-        in_specs=[vmem] * 4,
+        in_specs=[vmem] * len(blocks),
         out_specs=vmem,
-        scratch_shapes=[pltpu.VMEM((width, count), jnp.float32)],
+        scratch_shapes=[pltpu.VMEM((width, count // 2), jnp.float32)],
         name="place",
     )(*blocks)
 

time: 214 us -> 212 us (level)
  waiting for transfers between devices: 95.3 us -> 88.1 us
  other arithmetic: 21.4 us -> 23.8 us
    ppermute x23 -> x20, waiting for transfers between devices: 67.7 us -> 57.1 us  [shift(): return lax.ppermute(array, axis, [(i, (i + by) % n) for i in range(n)])]
    ppermute x3 -> x9, starting transfers between devices: 0.28 us -> 8.51 us  [the longest x7 8.42 us: returned(): return lax.ppermute(block, ('mem_1', 'tp_1'), pairs)]
    ppermute x3 -> x9, waiting for transfers between devices: 0.01 us -> 7.76 us  [the longest x7 6.18 us: returned(): return lax.ppermute(block, ('mem_1', 'tp_1'), pairs)]
    ppermute x23 -> x20, starting transfers between devices: 30.2 us -> 23.9 us  [shift(): return lax.ppermute(array, axis, [(i, (i + by) % n) for i in range(n)])]
    all_gather x1, waiting for transfers between devices: 27.6 us -> 23.2 us  [shards(): joint = lax.all_gather(joint, 'mem_0', axis=0, tiled=False)]
    concatenate x0 -> x2, other arithmetic: none -> 4.08 us  [the longest x1 2.21 us: shards(): weight = jnp.concatenate([weight, away], axis=2)]
    unnamed x24 -> x33, local copies, waits for them, and re-layouts: 5.81 us -> 8.57 us
    dot_general x6 -> x12, matrix products: 5.25 us -> 5.89 us  [terms(): lax.dot_general(weight[d], group, (((1,), (1,)), ((), ())), preferred_ele...]
  transfers between devices with their start and end apart: 30 -> 33, of which waited for: 12 -> 16; matrix products, arithmetic and copies ran while one was open for 16% -> 18% of each run, Pallas kernels for 0% -> 0%
where the time goes in v1:
time: 212 us; the launch traced here: 209 us
  waiting for transfers between devices  88.1 us (42%)
  starting transfers between devices  44.4 us (21%)
  other arithmetic  23.8 us (11%)
  local copies, waits for them, and re-layouts  19.9 us (9%)
  between operations  15.8 us (7%)
  Pallas kernels  10.7 us (5%)
  matrix products  5.89 us (3%)
    ppermute x20, waiting for transfers between devices, shift(): return lax.ppermute(array, axis, [(i, (i + by) % n) for i in range(n)])  57.1 us
    ppermute x20, starting transfers between devices, shift(): return lax.ppermute(array, axis, [(i, (i + by) % n) for i in range(n)])  23.9 us
    all_gather x1, waiting for transfers between devices, shards(): joint = lax.all_gather(joint, 'mem_0', axis=0, tiled=False)  23.2 us
    all_to_all x1, starting transfers between devices, shards(): lax.all_to_all(outgoing, MEM, split_axis=0, concat_axis=0, tiled=True)  11.3 us
    unnamed x33, local copies, waits for them, and re-layouts  8.57 us
    ppermute x7, starting transfers between devices, returned(): return lax.ppermute(block, ('mem_1', 'tp_1'), pairs)  8.42 us
    pallas_call x1, Pallas kernels, shards(): pl.pallas_call(functools.partial(attend_kernel, plan, rows, nx, chunks),...  8.35 us
    convert_element_type x1, other arithmetic, shards(): (values * factor * (1.0 + modrow[0]) + modrow[1]).astype(jnp.bfloat16)  6.99 us
  transfers between devices with their start and end apart: 33, of which 16 were waited for; matrix products, arithmetic and copies ran while one was open for 18% of the time, Pallas kernels for 0%

profile of v1, /device:TPU:2, one launch (start us, length us, event | category | flops | bytes accessed | tf_op | source)
XLA Modules:
  0.0 208.7 jit_solution(12092030386142700746)
XLA Ops:
  7.2 0.9 slice.95
  8.1 1.7 pad_maximum_fusion.4
  9.8 0.9 slice_bitcast_fusion.2
  10.7 1.6 collective-permute-start.1
  14.2 1.9 gather_fusion
  17.8 11.3 %all-to-all-start = ((bf16[32,8,768]{2,1,0:T(8,128)(2,1)}), bf16[32,8,768]{2,1,0:T(8,128)(2,1)S(1)}, u32[]{:S(2)}, u32[]{:S(2)}) async-start(bf16[32,8,768]{2,1,0:T(8,128)(2,1)} %pad_maximum_fusion.2), calls=%async_computation | async-start | bytes 786432 | tf_op jit(solution)/shard_map/all_to_all | solution.py:157
  29.8 3.6 %fusion = f32[512]{0:T(512)S(1)} fusion(bf16[512,5120]{1,0:T(8,128)(2,1)} %param.9), kind=kLoop, calls=%fused_computation.4 | loop fusion | flops 7863808 | bytes 5244928 | tf_op jit(solution)/shard_map/reduce_sum | solution.py:167
  33.5 0.9 dynamic-slice_add_fusion
  34.6 1.5 collective-permute-start.2
  36.1 3.3 %collective-permute-done.2 = bf16[160,256]{1,0:T(8,128)(2,1)S(1)} collective-permute-done((bf16[160,256]{1,0:T(8,128)(2,1)S(1)}, bf16[160,256]{1,0:T(8,128)(2,1)S(1)}, u32[]{:S(2)}, u32[]{:S(2)}) %collective-permute-start.2) | collective-permute-done | bytes 81952 | tf_op jit(solution)/shard_map/ppermute | solution.py:21
  40.3 23.2 %all-gather.5.cloned.1.call-done = bf16[1280,1024]{1,0:T(8,128)(2,1)} async-done(((bf16[160,1024]{1,0:T(8,128)(2,1)}), bf16[1280,1024]{1,0:T(8,128)(2,1)}) %all-gather.5.cloned.1.call-update) | async-done | bytes 2621456 | tf_op jit(solution)/shard_map/all_gather | solution.py:141
  65.0 7.0 %fusion.3.xm_ref = bf16[512,5120]{1,0:T(8,128)(2,1)} fusion(bf16[512,5120]{1,0:T(8,128)(2,1)} %param.9, f32[5120]{0:T(1024)S(1)} %bitcast.89, f32[5120]{0:T(1024)S(1)} %bitcast.88, f32[512]{0:T(512)S(1)} %add_rsqrt_fusion), kind=kLoop, calls=%fused_computation.7 | loop fusion | flops 13107200 | bytes 10528768 | tf_op jit(solution)/shard_map/convert_element_type | solution.py:168
  72.1 1.5 slice.101
  73.6 1.3 slice.104.rest_1_
  74.9 2.3 %collective-permute-start.5 = (bf16[8,160,384]{2,1,0:T(8,128)(2,1)S(1)}, bf16[8,160,384]{2,1,0:T(8,128)(2,1)S(1)}, u32[]{:S(2)}, u32[]{:S(2)}) collective-permute-start(bf16[8,160,384]{2,1,0:T(8,128)(2,1)S(1)} %slice.104.rest_1_), channel_id=1, source_target_pairs={{0,8},{8,16},{16,24},{24,0},{1,9},{9,17},{17,25},{25,1},{2,10},{10... | collective-permute-start | bytes 2949128 | tf_op jit(solution)/shard_map/ppermute | solution.py:21
  78.4 1.0 copy.17
  79.8 2.6 %broadcast_select_fusion = bf16[64,2,8,640]{3,2,1,0:T(8,128)(2,1)} fusion(bf16[64,2,8,640]{3,2,1,0:T(8,128)(2,1)} %param.14, pred[64]{0:T(512)(128)(4,1)S(1)} %add_compare_fusion, bf16[2,8,640]{2,1,0:T(8,128)(2,1)S(1)} %broadcast_in_dim.60), kind=kLoop, calls=%fused_computation.18 | loop fusion | flops 655360 | bytes 2641984 | tf_op jit(solution)/shard_map/jit(_where)/select_n | solution.py:179
  82.4 16.7 %collective-permute-done.5.rest_2_ = bf16[8,160,384]{2,1,0:T(8,128)(2,1)S(1)} collective-permute-done((bf16[8,160,384]{2,1,0:T(8,128)(2,1)S(1)}, bf16[8,160,384]{2,1,0:T(8,128)(2,1)S(1)}, u32[]{:S(2)}, u32[]{:S(2)}) %collective-permute-start.5) | collective-permute-done | bytes 983072 | tf_op jit(solution)/shard_map/ppermute | solution.py:21
  99.2 2.2 %collective-permute-start.7 = (bf16[4,160,384]{2,1,0:T(8,128)(2,1)S(1)}, bf16[4,160,384]{2,1,0:T(8,128)(2,1)S(1)}, u32[]{:S(2)}, u32[]{:S(2)}) collective-permute-start(bf16[4,160,384]{2,1,0:T(8,128)(2,1)S(1)} %slice.126), channel_id=1, source_target_pairs={{0,8},{8,16},{16,24},{24,0},{1,9},{9,17},{17,25},{25,1},{2,10},{10... | collective-permute-start | bytes 1474568 | tf_op jit(solution)/shard_map/ppermute | solution.py:21
  102.3 2.2 %pad_maximum_fusion = bf16[8,160,1280]{2,1,0:T(8,128)(2,1)S(1)} fusion(bf16[8,160,640]{2,1,0:T(8,128)(2,1)} %collective-permute-done.4, bf16[8,160,640]{2,1,0:T(8,128)(2,1)} %slice.101), kind=kLoop, calls=%fused_computation.12 | loop fusion | flops 6553600 | bytes 6553600 | tf_op jit(solution)/shard_map/concatenate | solution.py:188
  104.5 1.2 fusion.7
  105.7 1.9 pad_maximum_fusion.1
  107.5 5.4 %collective-permute-done.7.rest_4_ = bf16[4,160,384]{2,1,0:T(8,128)(2,1)S(1)} collective-permute-done((bf16[4,160,384]{2,1,0:T(8,128)(2,1)S(1)}, bf16[4,160,384]{2,1,0:T(8,128)(2,1)S(1)}, u32[]{:S(2)}, u32[]{:S(2)}) %collective-permute-start.7) | collective-permute-done | bytes 491552 | tf_op jit(solution)/shard_map/ppermute | solution.py:21
  114.9 2.5 %copy-done = bf16[512,5120]{1,0:T(8,128)(2,1)S(1)} copy-done((bf16[512,5120]{1,0:T(8,128)(2,1)S(1)}, bf16[512,5120]{1,0:T(8,128)(2,1)}, u32[]{:S(2)}) %copy-start) | copy-done | bytes 5242904
  117.3 1.7 copy-done.1
  119.1 1.0 copy-done.3
  120.1 1.0 copy-done.5
  121.1 8.3 %query_attend.1 = (bf16[256,640]{1,0:T(8,128)(2,1)S(1)}, bf16[256,640]{1,0:T(8,128)(2,1)S(1)}) custom-call(bf16[512,5120]{1,0:T(8,128)(2,1)S(1)} %copy-done, bf16[64,640]{1,0:T(8,128)(2,1)S(1)} %get-tuple-element.18.k_ref, bf16[64,640]{1,0:T(8,128)(2,1)S(1)} %get-tuple-element.19.v_ref, bf16[8,4,160,256]{3,2,1,0:T(8,128)(2,1)S(1)} %bitcast.81, ...), custom_call_target="tpu_custom_call" | custom-call | flops 3355443200 | bytes 6553600 | tf_op jit(solution)/shard_map/query_attend/pallas_call | solution.py:213
  129.6 1.6 collective-permute-done.9
  132.5 1.6 collective-permute-start.10
  134.1 3.0 %collective-permute-start.11 = (bf16[320,256]{1,0:T(8,128)(2,1)S(1)}, bf16[320,256]{1,0:T(8,128)(2,1)S(1)}, u32[]{:S(2)}, u32[]{:S(2)}) collective-permute-start(bf16[320,256]{1,0:T(8,128)(2,1)S(1)} %convolution_convert_fusion.9), channel_id=1, source_target_pairs={{0,4},{2,6},{4,0},{6,2},{1,5},{3,7},{5,1},{7,3},{8,12},{10,14},{12... | collective-permute-start | bytes 491528 | tf_op jit(solution)/shard_map/ppermute | solution.py:21
  137.1 1.3 collective-permute-start.12
  138.4 1.6 collective-permute-start.14
  139.9 1.0 collective-permute-start.15
  141.0 3.8 %collective-permute-done.11 = bf16[320,256]{1,0:T(8,128)(2,1)S(1)} collective-permute-done((bf16[320,256]{1,0:T(8,128)(2,1)S(1)}, bf16[320,256]{1,0:T(8,128)(2,1)S(1)}, u32[]{:S(2)}, u32[]{:S(2)}) %collective-permute-start.11) | collective-permute-done | bytes 163872 | tf_op jit(solution)/shard_map/ppermute | solution.py:21
  145.9 9.3 %collective-permute-done.14 = bf16[256,1280]{1,0:T(8,128)(2,1)S(1)} collective-permute-done((bf16[256,1280]{1,0:T(8,128)(2,1)S(1)}, bf16[256,1280]{1,0:T(8,128)(2,1)S(1)}, u32[]{:S(2)}, u32[]{:S(2)}) %collective-permute-start.14) | collective-permute-done | bytes 655392 | tf_op jit(solution)/shard_map/ppermute | solution.py:21
  155.2 1.2 collective-permute-start.23
  158.1 1.8 collective-permute-start.24
  161.3 1.0 collective-permute-start.17
  162.4 2.2 %collective-permute-done.23 = bf16[128,1280]{1,0:T(8,128)(2,1)S(1)} collective-permute-done((bf16[128,1280]{1,0:T(8,128)(2,1)S(1)}, bf16[128,1280]{1,0:T(8,128)(2,1)S(1)}, u32[]{:S(2)}, u32[]{:S(2)}) %collective-permute-start.23) | collective-permute-done | bytes 327712 | tf_op jit(solution)/shard_map/ppermute | solution.py:21
  165.1 1.5 collective-permute-done.24
  168.7 11.5 %collective-permute-done.16 = bf16[320,512]{1,0:T(8,128)(2,1)S(1)} collective-permute-done((bf16[320,512]{1,0:T(8,128)(2,1)S(1)}, bf16[320,512]{1,0:T(8,128)(2,1)S(1)}, u32[]{:S(2)}, u32[]{:S(2)}) %collective-permute-start.16) | collective-permute-done | bytes 327712 | tf_op jit(solution)/shard_map/ppermute | solution.py:21
  181.0 3.3 %collective-permute-start.19 = (bf16[160,256]{1,0:T(8,128)(2,1)S(1)}, bf16[160,256]{1,0:T(8,128)(2,1)S(1)}, u32[]{:S(2)}, u32[]{:S(2)}) collective-permute-start(bf16[160,256]{1,0:T(8,128)(2,1)S(1)} %get-tuple-element.31), channel_id=1, source_target_pairs={{0,24},{1,25},{8,0},{9,1},{16,8},{17,9},{24,16},{25,17},{2,26},{3,... | collective-permute-start | bytes 245768 | tf_op jit(solution)/shard_map/ppermute | solution.py:256
  184.4 2.6 %collective-permute-done.26 = bf16[320,256]{1,0:T(8,128)(2,1)S(1)} collective-permute-done((bf16[320,256]{1,0:T(8,128)(2,1)S(1)}, bf16[320,256]{1,0:T(8,128)(2,1)S(1)}, u32[]{:S(2)}, u32[]{:S(2)}) %collective-permute-start.26) | collective-permute-done | bytes 163872 | tf_op jit(solution)/shard_map/ppermute | solution.py:21
  188.0 4.6 %collective-permute-start.28 = (bf16[160,256]{1,0:T(8,128)(2,1)S(1)}, bf16[160,256]{1,0:T(8,128)(2,1)S(1)}, u32[]{:S(2)}, u32[]{:S(2)}) collective-permute-start(bf16[160,256]{1,0:T(8,128)(2,1)S(1)} %get-tuple-element.35), channel_id=1, source_target_pairs={{0,16},{1,17},{8,24},{9,25},{16,0},{17,1},{24,8},{25,9},{2,18},{3,... | collective-permute-start | bytes 245768 | tf_op jit(solution)/shard_map/ppermute | solution.py:256
  192.7 2.8 %collective-permute-done.28.refs_6_ = bf16[160,256]{1,0:T(8,128)(2,1)S(1)} collective-permute-done((bf16[160,256]{1,0:T(8,128)(2,1)S(1)}, bf16[160,256]{1,0:T(8,128)(2,1)S(1)}, u32[]{:S(2)}, u32[]{:S(2)}) %collective-permute-start.28) | collective-permute-done | bytes 81952 | tf_op jit(solution)/shard_map/ppermute | solution.py:256
  195.4 3.4 %collective-permute-done.29.refs_7_ = bf16[160,256]{1,0:T(8,128)(2,1)S(1)} collective-permute-done((bf16[160,256]{1,0:T(8,128)(2,1)S(1)}, bf16[160,256]{1,0:T(8,128)(2,1)S(1)}, u32[]{:S(2)}, u32[]{:S(2)}) %collective-permute-start.29) | collective-permute-done | bytes 81952 | tf_op jit(solution)/shard_map/ppermute | solution.py:256
  199.5 2.4 %place.1 = bf16[512,640]{1,0:T(8,128)(2,1)} custom-call(bf16[160,256]{1,0:T(8,128)(2,1)} %get-tuple-element.37.refs_0_, bf16[160,256]{1,0:T(8,128)(2,1)} %copy-done.8, bf16[160,256]{1,0:T(8,128)(2,1)} %copy-done.9, bf16[160,256]{1,0:T(8,128)(2,1)} %copy-done.10, bf16[160,256]{1,0:T(8,128)(2,1)} %copy-done.11, bf16[160,256]{1,0:T(8,128)(2,1)} %copy-done.12, ...), custom_call_target="tpu_custom_call" | custom-call | tf_op jit(solution)/shard_map/place/pallas_call | solution.py:272
  (120 shorter events, 20.8 us)
Async XLA Ops:
  7.2 56.3 %all-gather.5.cloned.1.call-start = ((), (), s32[]{:S(2)}) async-start(), calls=%async_computation.1 | async-start | bytes 2949120 | tf_op jit(solution)/shard_map/all_gather | solution.py:141
  10.7 23.8 %collective-permute-start.1 = (bf16[160,256]{1,0:T(8,128)(2,1)S(1)}, bf16[160,256]{1,0:T(8,128)(2,1)S(1)}, u32[]{:S(2)}, u32[]{:S(2)}) collective-permute-start(bf16[160,256]{1,0:T(8,128)(2,1)S(1)} %get-tuple-element.33), channel_id=1, source_target_pairs={{0,8},{8,16},{16,24},{24,0},{1,9},{9,17},{17,25},{25,1},{2,10},{10... | collective-permute-start | bytes 245768 | tf_op jit(solution)/shard_map/ppermute | solution.py:21
  12.3 23.8 %collective-permute-start = (bf16[160,256]{1,0:T(8,128)(2,1)S(1)}, bf16[160,256]{1,0:T(8,128)(2,1)S(1)}, u32[]{:S(2)}, u32[]{:S(2)}) collective-permute-start(bf16[160,256]{1,0:T(8,128)(2,1)S(1)} %get-tuple-element.33), channel_id=1, source_target_pairs={{0,24},{8,0},{16,8},{24,16},{1,25},{9,1},{17,9},{25,17},{2,26},{10... | collective-permute-start | bytes 245768 | tf_op jit(solution)/shard_map/ppermute | solution.py:21
  17.8 45.8 %all-to-all-start = ((bf16[32,8,768]{2,1,0:T(8,128)(2,1)}), bf16[32,8,768]{2,1,0:T(8,128)(2,1)S(1)}, u32[]{:S(2)}, u32[]{:S(2)}) async-start(bf16[32,8,768]{2,1,0:T(8,128)(2,1)} %pad_maximum_fusion.2), calls=%async_computation | async-start | bytes 786432 | tf_op jit(solution)/shard_map/all_to_all | solution.py:157
  29.1 85.7 %all-gather.7.cloned.1.call-start = ((), (), s32[]{:S(2)}) async-start(), calls=%async_computation.2 | async-start | bytes 2949120 | tf_op jit(solution)/shard_map/all_gather | solution.py:144
  34.6 4.9 %collective-permute-start.2 = (bf16[160,256]{1,0:T(8,128)(2,1)S(1)}, bf16[160,256]{1,0:T(8,128)(2,1)S(1)}, u32[]{:S(2)}, u32[]{:S(2)}) collective-permute-start(bf16[160,256]{1,0:T(8,128)(2,1)S(1)} %collective-permute-done.1), channel_id=1, source_target_pairs={{0,8},{8,16},{16,24},{24,0},{1,9},{9,17},{17,25},{25,1},{2,10},{10... | collective-permute-start | bytes 245768 | tf_op jit(solution)/shard_map/ppermute | solution.py:21
  64.3 7.6 %collective-permute-start.3 = (bf16[64,640]{1,0:T(8,128)(2,1)S(1)}, bf16[64,640]{1,0:T(8,128)(2,1)S(1)}, u32[]{:S(2)}, u32[]{:S(2)}) collective-permute-start(bf16[64,640]{1,0:T(8,128)(2,1)S(1)} %bitcast_select_fusion), channel_id=1, source_target_pairs={{0,8},{8,0},{16,24},{24,16},{1,9},{9,1},{17,25},{25,17},{2,10},{10... | collective-permute-start | bytes 245768 | tf_op jit(solution)/shard_map/ppermute | solution.py:160
  65.0 7.1 %copy-start.7 = (bf16[1280,1024]{1,0:T(8,128)(2,1)S(1)}, bf16[1280,1024]{1,0:T(8,128)(2,1)}, u32[]{:S(2)}) copy-start(bf16[1280,1024]{1,0:T(8,128)(2,1)} %all-gather.5.cloned.1.call-done) | copy-start | bytes 7864324
  73.6 28.7 %collective-permute-start.4 = (bf16[8,160,640]{2,1,0:T(8,128)(2,1)}, bf16[8,160,640]{2,1,0:T(8,128)(2,1)}, u32[]{:S(2)}, u32[]{:S(2)}) collective-permute-start(bf16[8,160,640]{2,1,0:T(8,128)(2,1)} %slice.101), channel_id=1, source_target_pairs={{0,1},{1,0},{2,3},{3,2},{4,5},{5,4},{6,7},{7,6},{8,9},{9,8},{10,11... | collective-permute-start | bytes 4915208 | tf_op jit(solution)/shard_map/ppermute | solution.py:187
  74.9 24.3 %collective-permute-start.5 = (bf16[8,160,384]{2,1,0:T(8,128)(2,1)S(1)}, bf16[8,160,384]{2,1,0:T(8,128)(2,1)S(1)}, u32[]{:S(2)}, u32[]{:S(2)}) collective-permute-start(bf16[8,160,384]{2,1,0:T(8,128)(2,1)S(1)} %slice.104.rest_1_), channel_id=1, source_target_pairs={{0,8},{8,16},{16,24},{24,0},{1,9},{9,17},{17,25},{25,1},{2,10},{10... | collective-permute-start | bytes 2949128 | tf_op jit(solution)/shard_map/ppermute | solution.py:21
  77.1 24.2 %collective-permute-start.6 = (bf16[8,160,384]{2,1,0:T(8,128)(2,1)S(1)}, bf16[8,160,384]{2,1,0:T(8,128)(2,1)S(1)}, u32[]{:S(2)}, u32[]{:S(2)}) collective-permute-start(bf16[8,160,384]{2,1,0:T(8,128)(2,1)S(1)} %slice.104.rest_1_), channel_id=1, source_target_pairs={{0,24},{8,0},{16,8},{24,16},{1,25},{9,1},{17,9},{25,17},{2,26},{10... | collective-permute-start | bytes 2949128 | tf_op jit(solution)/shard_map/ppermute | solution.py:21
  99.2 13.8 %collective-permute-start.7 = (bf16[4,160,384]{2,1,0:T(8,128)(2,1)S(1)}, bf16[4,160,384]{2,1,0:T(8,128)(2,1)S(1)}, u32[]{:S(2)}, u32[]{:S(2)}) collective-permute-start(bf16[4,160,384]{2,1,0:T(8,128)(2,1)S(1)} %slice.126), channel_id=1, source_target_pairs={{0,8},{8,16},{16,24},{24,0},{1,9},{9,17},{17,25},{25,1},{2,10},{10... | collective-permute-start | bytes 1474568 | tf_op jit(solution)/shard_map/ppermute | solution.py:21
  101.4 12.7 %collective-permute-start.8 = (bf16[4,160,384]{2,1,0:T(8,128)(2,1)S(1)}, bf16[4,160,384]{2,1,0:T(8,128)(2,1)S(1)}, u32[]{:S(2)}, u32[]{:S(2)}) collective-permute-start(bf16[4,160,384]{2,1,0:T(8,128)(2,1)S(1)} %slice.127), channel_id=1, source_target_pairs={{0,24},{8,0},{16,8},{24,16},{1,25},{9,1},{17,9},{25,17},{2,26},{10... | collective-permute-start | bytes 1474568 | tf_op jit(solution)/shard_map/ppermute | solution.py:21
  113.0 0.8 copy-start.2
  114.1 0.8 copy-start.4
  114.9 2.5 %copy-start = (bf16[512,5120]{1,0:T(8,128)(2,1)S(1)}, bf16[512,5120]{1,0:T(8,128)(2,1)}, u32[]{:S(2)}) copy-start(bf16[512,5120]{1,0:T(8,128)(2,1)} %fusion.3.xm_ref) | copy-start | bytes 15728644
  117.3 1.7 copy-start.1
  119.1 1.0 copy-start.3
  120.1 1.0 copy-start.5
  121.1 10.1 %copy-start.6 = (bf16[4,320,1280]{2,1,0:T(8,128)(2,1)S(1)}, bf16[4,320,1280]{2,1,0:T(8,128)(2,1)}, u32[]{:S(2)}) copy-start(bf16[4,320,1280]{2,1,0:T(8,128)(2,1)} %pad_maximum_fusion.1) | copy-start | bytes 9830404
  129.5 1.7 collective-permute-start.9
  132.5 8.5 %collective-permute-start.10 = (bf16[320,256]{1,0:T(8,128)(2,1)S(1)}, bf16[320,256]{1,0:T(8,128)(2,1)S(1)}, u32[]{:S(2)}, u32[]{:S(2)}) collective-permute-start(bf16[320,256]{1,0:T(8,128)(2,1)S(1)} %convolution_convert_fusion.10), channel_id=1, source_target_pairs={{0,2},{2,4},{4,6},{6,0},{1,3},{3,5},{5,7},{7,1},{8,10},{10,12},{12... | collective-permute-start | bytes 491528 | tf_op jit(solution)/shard_map/ppermute | solution.py:21
  134.1 10.7 %collective-permute-start.11 = (bf16[320,256]{1,0:T(8,128)(2,1)S(1)}, bf16[320,256]{1,0:T(8,128)(2,1)S(1)}, u32[]{:S(2)}, u32[]{:S(2)}) collective-permute-start(bf16[320,256]{1,0:T(8,128)(2,1)S(1)} %convolution_convert_fusion.9), channel_id=1, source_target_pairs={{0,4},{2,6},{4,0},{6,2},{1,5},{3,7},{5,1},{7,3},{8,12},{10,14},{12... | collective-permute-start | bytes 491528 | tf_op jit(solution)/shard_map/ppermute | solution.py:21
  137.1 7.7 %collective-permute-start.12 = (bf16[320,256]{1,0:T(8,128)(2,1)S(1)}, bf16[320,256]{1,0:T(8,128)(2,1)S(1)}, u32[]{:S(2)}, u32[]{:S(2)}) collective-permute-start(bf16[320,256]{1,0:T(8,128)(2,1)S(1)} %convolution_convert_fusion.8), channel_id=1, source_target_pairs={{0,6},{2,0},{4,2},{6,4},{1,7},{3,1},{5,3},{7,5},{8,14},{10,8},{12,... | collective-permute-start | bytes 491528 | tf_op jit(solution)/shard_map/ppermute | solution.py:21
  138.4 16.8 %collective-permute-start.14 = (bf16[256,1280]{1,0:T(8,128)(2,1)S(1)}, bf16[256,1280]{1,0:T(8,128)(2,1)S(1)}, u32[]{:S(2)}, u32[]{:S(2)}) collective-permute-start(bf16[256,1280]{1,0:T(8,128)(2,1)S(1)} %constant_dynamic-update-slice_fusion), channel_id=1, source_target_pairs={{0,8},{8,16},{16,24},{24,0},{1,9},{9,17},{17,25},{25,1},{2,10},{10... | collective-permute-start | bytes 1966088 | tf_op jit(solution)/shard_map/ppermute | solution.py:21
  139.9 16.8 %collective-permute-start.15 = (bf16[256,1280]{1,0:T(8,128)(2,1)S(1)}, bf16[256,1280]{1,0:T(8,128)(2,1)S(1)}, u32[]{:S(2)}, u32[]{:S(2)}) collective-permute-start(bf16[256,1280]{1,0:T(8,128)(2,1)S(1)} %constant_dynamic-update-slice_fusion), channel_id=1, source_target_pairs={{0,24},{8,0},{16,8},{24,16},{1,25},{9,1},{17,9},{25,17},{2,26},{10... | collective-permute-start | bytes 1966088 | tf_op jit(solution)/shard_map/ppermute | solution.py:21
  145.9 42.1 %collective-permute-start.13 = (bf16[160,256]{1,0:T(8,128)(2,1)S(1)}, bf16[160,256]{1,0:T(8,128)(2,1)S(1)}, u32[]{:S(2)}, u32[]{:S(2)}) collective-permute-start(bf16[160,256]{1,0:T(8,128)(2,1)S(1)} %get-tuple-element.36), channel_id=1, source_target_pairs={{0,1},{1,0},{8,9},{9,8},{16,17},{17,16},{24,25},{25,24},{2,3},{3,2... | collective-permute-start | bytes 245768 | tf_op jit(solution)/shard_map/ppermute | solution.py:256
  155.2 9.4 %collective-permute-start.23 = (bf16[128,1280]{1,0:T(8,128)(2,1)S(1)}, bf16[128,1280]{1,0:T(8,128)(2,1)S(1)}, u32[]{:S(2)}, u32[]{:S(2)}) collective-permute-start(bf16[128,1280]{1,0:T(8,128)(2,1)S(1)} %slice.134), channel_id=1, source_target_pairs={{0,8},{8,16},{16,24},{24,0},{1,9},{9,17},{17,25},{25,1},{2,10},{10... | collective-permute-start | bytes 983048 | tf_op jit(solution)/shard_map/ppermute | solution.py:21
  158.1 8.5 %collective-permute-start.24 = (bf16[128,1280]{1,0:T(8,128)(2,1)S(1)}, bf16[128,1280]{1,0:T(8,128)(2,1)S(1)}, u32[]{:S(2)}, u32[]{:S(2)}) collective-permute-start(bf16[128,1280]{1,0:T(8,128)(2,1)S(1)} %slice.135), channel_id=1, source_target_pairs={{0,24},{8,0},{16,8},{24,16},{1,25},{9,1},{17,9},{25,17},{2,26},{10... | collective-permute-start | bytes 983048 | tf_op jit(solution)/shard_map/ppermute | solution.py:21
  160.6 19.6 %collective-permute-start.16 = (bf16[320,512]{1,0:T(8,128)(2,1)S(1)}, bf16[320,512]{1,0:T(8,128)(2,1)S(1)}, u32[]{:S(2)}, u32[]{:S(2)}) collective-permute-start(bf16[320,512]{1,0:T(8,128)(2,1)S(1)} %convolution_convert_fusion.2), channel_id=1, source_target_pairs={{0,2},{2,4},{4,6},{6,0},{1,3},{3,5},{5,7},{7,1},{8,10},{10,12},{12... | collective-permute-start | bytes 983048 | tf_op jit(solution)/shard_map/ppermute | solution.py:21
  161.3 18.8 %collective-permute-start.17 = (bf16[320,512]{1,0:T(8,128)(2,1)S(1)}, bf16[320,512]{1,0:T(8,128)(2,1)S(1)}, u32[]{:S(2)}, u32[]{:S(2)}) collective-permute-start(bf16[320,512]{1,0:T(8,128)(2,1)S(1)} %convolution_convert_fusion.1), channel_id=1, source_target_pairs={{0,4},{2,6},{4,0},{6,2},{1,5},{3,7},{5,1},{7,3},{8,12},{10,14},{12... | collective-permute-start | bytes 983048 | tf_op jit(solution)/shard_map/ppermute | solution.py:21
  164.6 15.8 %collective-permute-start.18 = (bf16[320,512]{1,0:T(8,128)(2,1)S(1)}, bf16[320,512]{1,0:T(8,128)(2,1)S(1)}, u32[]{:S(2)}, u32[]{:S(2)}) collective-permute-start(bf16[320,512]{1,0:T(8,128)(2,1)S(1)} %convolution_convert_fusion), channel_id=1, source_target_pairs={{0,6},{2,0},{4,2},{6,4},{1,7},{3,1},{5,3},{7,5},{8,14},{10,8},{12,... | collective-permute-start | bytes 983048 | tf_op jit(solution)/shard_map/ppermute | solution.py:21
  167.5 16.9 %collective-permute-start.25 = (bf16[320,256]{1,0:T(8,128)(2,1)S(1)}, bf16[320,256]{1,0:T(8,128)(2,1)S(1)}, u32[]{:S(2)}, u32[]{:S(2)}) collective-permute-start(bf16[320,256]{1,0:T(8,128)(2,1)S(1)} %convolution_convert_fusion.6), channel_id=1, source_target_pairs={{0,2},{2,4},{4,6},{6,0},{1,3},{3,5},{5,7},{7,1},{8,10},{10,12},{12... | collective-permute-start | bytes 491528 | tf_op jit(solution)/shard_map/ppermute | solution.py:21
  180.2 6.8 %collective-permute-start.26 = (bf16[320,256]{1,0:T(8,128)(2,1)S(1)}, bf16[320,256]{1,0:T(8,128)(2,1)S(1)}, u32[]{:S(2)}, u32[]{:S(2)}) collective-permute-start(bf16[320,256]{1,0:T(8,128)(2,1)S(1)} %convolution_convert_fusion.5), channel_id=1, source_target_pairs={{0,4},{2,6},{4,0},{6,2},{1,5},{3,7},{5,1},{7,3},{8,12},{10,14},{12... | collective-permute-start | bytes 491528 | tf_op jit(solution)/shard_map/ppermute | solution.py:21
  180.2 7.3 %collective-permute-start.27 = (bf16[320,256]{1,0:T(8,128)(2,1)S(1)}, bf16[320,256]{1,0:T(8,128)(2,1)S(1)}, u32[]{:S(2)}, u32[]{:S(2)}) collective-permute-start(bf16[320,256]{1,0:T(8,128)(2,1)S(1)} %convolution_convert_fusion.4), channel_id=1, source_target_pairs={{0,6},{2,0},{4,2},{6,4},{1,7},{3,1},{5,3},{7,5},{8,14},{10,8},{12,... | collective-permute-start | bytes 491528 | tf_op jit(solution)/shard_map/ppermute | solution.py:21
  181.0 11.6 %collective-permute-start.19 = (bf16[160,256]{1,0:T(8,128)(2,1)S(1)}, bf16[160,256]{1,0:T(8,128)(2,1)S(1)}, u32[]{:S(2)}, u32[]{:S(2)}) collective-permute-start(bf16[160,256]{1,0:T(8,128)(2,1)S(1)} %get-tuple-element.31), channel_id=1, source_target_pairs={{0,24},{1,25},{8,0},{9,1},{16,8},{17,9},{24,16},{25,17},{2,26},{3,... | collective-permute-start | bytes 245768 | tf_op jit(solution)/shard_map/ppermute | solution.py:256
  184.4 8.3 %collective-permute-start.20 = (bf16[160,256]{1,0:T(8,128)(2,1)S(1)}, bf16[160,256]{1,0:T(8,128)(2,1)S(1)}, u32[]{:S(2)}, u32[]{:S(2)}) collective-permute-start(bf16[160,256]{1,0:T(8,128)(2,1)S(1)} %get-tuple-element.30), channel_id=1, source_target_pairs={{0,25},{1,24},{8,1},{9,0},{16,9},{17,8},{24,17},{25,16},{2,27},{3,... | collective-permute-start | bytes 245768 | tf_op jit(solution)/shard_map/ppermute | solution.py:256
  187.0 5.6 %collective-permute-start.21 = (bf16[160,256]{1,0:T(8,128)(2,1)S(1)}, bf16[160,256]{1,0:T(8,128)(2,1)S(1)}, u32[]{:S(2)}, u32[]{:S(2)}) collective-permute-start(bf16[160,256]{1,0:T(8,128)(2,1)S(1)} %get-tuple-element.29), channel_id=1, source_target_pairs={{0,8},{1,9},{8,16},{9,17},{16,24},{17,25},{24,0},{25,1},{2,10},{3,... | collective-permute-start | bytes 245768 | tf_op jit(solution)/shard_map/ppermute | solution.py:256
  187.5 5.2 %collective-permute-start.22 = (bf16[160,256]{1,0:T(8,128)(2,1)S(1)}, bf16[160,256]{1,0:T(8,128)(2,1)S(1)}, u32[]{:S(2)}, u32[]{:S(2)}) collective-permute-start(bf16[160,256]{1,0:T(8,128)(2,1)S(1)} %get-tuple-element.28), channel_id=1, source_target_pairs={{0,9},{1,8},{8,17},{9,16},{16,25},{17,24},{24,1},{25,0},{2,11},{3,... | collective-permute-start | bytes 245768 | tf_op jit(solution)/shard_map/ppermute | solution.py:256
  188.0 10.8 %copy-start.8 = (bf16[160,256]{1,0:T(8,128)(2,1)}, bf16[160,256]{1,0:T(8,128)(2,1)S(1)}, u32[]{:S(2)}) copy-start(bf16[160,256]{1,0:T(8,128)(2,1)S(1)} %collective-permute-done.13.refs_1_) | copy-start | bytes 245764
  188.0 7.4 %collective-permute-start.28 = (bf16[160,256]{1,0:T(8,128)(2,1)S(1)}, bf16[160,256]{1,0:T(8,128)(2,1)S(1)}, u32[]{:S(2)}, u32[]{:S(2)}) collective-permute-start(bf16[160,256]{1,0:T(8,128)(2,1)S(1)} %get-tuple-element.35), channel_id=1, source_target_pairs={{0,16},{1,17},{8,24},{9,25},{16,0},{17,1},{24,8},{25,9},{2,18},{3,... | collective-permute-start | bytes 245768 | tf_op jit(solution)/shard_map/ppermute | solution.py:256
  192.6 6.2 %copy-start.9 = (bf16[160,256]{1,0:T(8,128)(2,1)}, bf16[160,256]{1,0:T(8,128)(2,1)S(1)}, u32[]{:S(2)}) copy-start(bf16[160,256]{1,0:T(8,128)(2,1)S(1)} %collective-permute-done.19.refs_2_) | copy-start | bytes 245764
  192.6 6.2 %collective-permute-start.29 = (bf16[160,256]{1,0:T(8,128)(2,1)S(1)}, bf16[160,256]{1,0:T(8,128)(2,1)S(1)}, u32[]{:S(2)}, u32[]{:S(2)}) collective-permute-start(bf16[160,256]{1,0:T(8,128)(2,1)S(1)} %get-tuple-element.34), channel_id=1, source_target_pairs={{0,17},{1,16},{8,25},{9,24},{16,1},{17,0},{24,9},{25,8},{2,19},{3,... | collective-permute-start | bytes 245768 | tf_op jit(solution)/shard_map/ppermute | solution.py:256
  192.6 6.2 %copy-start.10 = (bf16[160,256]{1,0:T(8,128)(2,1)}, bf16[160,256]{1,0:T(8,128)(2,1)S(1)}, u32[]{:S(2)}) copy-start(bf16[160,256]{1,0:T(8,128)(2,1)S(1)} %collective-permute-done.20.refs_3_) | copy-start | bytes 245764
  192.6 6.2 %copy-start.11 = (bf16[160,256]{1,0:T(8,128)(2,1)}, bf16[160,256]{1,0:T(8,128)(2,1)S(1)}, u32[]{:S(2)}) copy-start(bf16[160,256]{1,0:T(8,128)(2,1)S(1)} %collective-permute-done.21.refs_4_) | copy-start | bytes 245764
  192.7 6.2 %copy-start.12 = (bf16[160,256]{1,0:T(8,128)(2,1)}, bf16[160,256]{1,0:T(8,128)(2,1)S(1)}, u32[]{:S(2)}) copy-start(bf16[160,256]{1,0:T(8,128)(2,1)S(1)} %collective-permute-done.22.refs_5_) | copy-start | bytes 245764
  195.4 3.4 %copy-start.13 = (bf16[160,256]{1,0:T(8,128)(2,1)}, bf16[160,256]{1,0:T(8,128)(2,1)S(1)}, u32[]{:S(2)}) copy-start(bf16[160,256]{1,0:T(8,128)(2,1)S(1)} %collective-permute-done.28.refs_6_) | copy-start | bytes 245764
  198.8 0.6 copy-start.14
Sparse Core Ops, SparseCore 0:
  10.3 53.0 all-gather.4
  65.2 40.4 all-gather.6

commit v2 on v1

--- a/solution.py
+++ b/solution.py
@@ -223,7 +223,7 @@
             pltpu.SemaphoreType.DMA((chunks,)),
             pltpu.SemaphoreType.DMA((chunks,)),
         ],
-        compiler_params=pltpu.CompilerParams(vmem_limit_bytes=40 * 1024 * 1024),
+        compiler_params=pltpu.CompilerParams(vmem_limit_bytes=62 * 1024 * 1024),
         cost_estimate=pl.CostEstimate(
             flops=2 * count * model * width, bytes_accessed=2 * model * width, transcendentals=0
         ),
@@ -232,13 +232,14 @@
 
     attended = jnp.concatenate([keep, lax.ppermute(give, "tp_1", swap)], axis=1)
 
+    def term(d, group):
+        return lax.dot_general(
+            weight[d], group, (((1,), (1,)), ((), ())), preferred_element_type=jnp.float32
+        ).astype(jnp.bfloat16)
+
     def terms(group):
-        return [
-            lax.dot_general(
-                weight[d], group, (((1,), (1,)), ((), ())), preferred_element_type=jnp.float32
-            ).astype(jnp.bfloat16)
-            for d in range(ny)
-        ]
+        home = term(0, group)
+        return [home] + [term(d, group) for d in range(1, ny)]
 
     def sent(parts):
         return [parts[0]] + [shift(parts[d], "tp_0", d) for d in range(1, ny)]
@@ -262,7 +263,8 @@
     near_parts = sent(terms(jnp.concatenate([left, right], axis=0)))
     far_parts = sent(terms(jnp.concatenate(far, axis=0)))
     blocks, places = [], []
-    for parts, bys in ((own_parts, (0,)), (near_parts, (-1, 1)), (far_parts, (2,))):
+    groups = ((own_parts, (0,)), (near_parts, (-1, 1)), (far_parts, (2,)))
+    for parts, bys in groups:
         both = summed(parts)
         for i, by in enumerate(bys):
             for mine in (1, 0):

time: 212 us -> 214 us (level)
  local copies, waits for them, and re-layouts: 19.9 us -> 15.6 us
  Pallas kernels: 10.7 us -> 14.3 us
  waiting for transfers between devices: 88.1 us -> 91.4 us
    unnamed x33 -> x25, local copies, waits for them, and re-layouts: 8.57 us -> 2.62 us
    ppermute x20, waiting for transfers between devices: 57.1 us -> 61.5 us  [shift(): return lax.ppermute(array, axis, [(i, (i + by) % n) for i in range(n)])]
    pallas_call x1, Pallas kernels: 8.35 us -> 11.9 us  [shards(): pl.pallas_call(functools.partial(attend_kernel, plan, rows, nx, chunks),...]
  transfers between devices with their start and end apart: 33 -> 33, of which waited for: 16 -> 15; matrix products, arithmetic and copies ran while one was open for 18% -> 18% of each run, Pallas kernels for 0% -> 0%
where the time goes in v2:
time: 214 us; the launch traced here: 211 us
  waiting for transfers between devices  91.4 us (43%)
  starting transfers between devices  44.2 us (21%)
  other arithmetic  22.6 us (11%)
  between operations  15.8 us (7%)
  local copies, waits for them, and re-layouts  15.6 us (7%)
  Pallas kernels  14.3 us (7%)
  matrix products  7.04 us (3%)
    ppermute x20, waiting for transfers between devices, shift(): return lax.ppermute(array, axis, [(i, (i + by) % n) for i in range(n)])  61.5 us
    ppermute x20, starting transfers between devices, shift(): return lax.ppermute(array, axis, [(i, (i + by) % n) for i in range(n)])  23.4 us
    all_gather x1, waiting for transfers between devices, shards(): joint = lax.all_gather(joint, 'mem_0', axis=0, tiled=False)  23.2 us
    pallas_call x1, Pallas kernels, shards(): pl.pallas_call(functools.partial(attend_kernel, plan, rows, nx, chunks),...  11.9 us
    all_to_all x1, starting transfers between devices, shards(): lax.all_to_all(outgoing, MEM, split_axis=0, concat_axis=0, tiled=True)  11.3 us
    ppermute x7, starting transfers between devices, returned(): return lax.ppermute(block, ('mem_1', 'tp_1'), pairs)  8.58 us
    dot_general x12, matrix products, term(): lax.dot_general(weight[d], group, (((1,), (1,)), ((), ())), preferred_ele...  7.04 us
    convert_element_type x1, other arithmetic, shards(): (values * factor * (1.0 + modrow[0]) + modrow[1]).astype(jnp.bfloat16)  6.83 us
  transfers between devices with their start and end apart: 33, of which 15 were waited for; matrix products, arithmetic and copies ran while one was open for 18% of the time, Pallas kernels for 0%

profile of v2, /device:TPU:2, one launch (start us, length us, event | category | flops | bytes accessed | tf_op | source)
XLA Modules:
  0.0 210.9 jit_solution(9309001830658881021)
XLA Ops:
  7.2 0.9 slice.95
  8.1 1.7 pad_maximum_fusion.4
  9.8 0.9 slice_bitcast_fusion.2
  10.7 1.6 collective-permute-start.1
  14.2 1.9 gather_fusion
  17.8 11.3 %all-to-all-start = ((bf16[32,8,768]{2,1,0:T(8,128)(2,1)}), bf16[32,8,768]{2,1,0:T(8,128)(2,1)S(1)}, u32[]{:S(2)}, u32[]{:S(2)}) async-start(bf16[32,8,768]{2,1,0:T(8,128)(2,1)} %pad_maximum_fusion.2), calls=%async_computation | async-start | bytes 786432 | tf_op jit(solution)/shard_map/all_to_all | solution.py:157
  29.8 3.6 %fusion = f32[512]{0:T(512)S(1)} fusion(bf16[512,5120]{1,0:T(8,128)(2,1)} %param.9), kind=kLoop, calls=%fused_computation.4 | loop fusion | flops 7863808 | bytes 5244928 | tf_op jit(solution)/shard_map/reduce_sum | solution.py:167
  33.5 0.9 dynamic-slice_add_fusion
  34.6 1.5 collective-permute-start.2
  36.1 3.3 %collective-permute-done.2 = bf16[160,256]{1,0:T(8,128)(2,1)S(1)} collective-permute-done((bf16[160,256]{1,0:T(8,128)(2,1)S(1)}, bf16[160,256]{1,0:T(8,128)(2,1)S(1)}, u32[]{:S(2)}, u32[]{:S(2)}) %collective-permute-start.2) | collective-permute-done | bytes 81952 | tf_op jit(solution)/shard_map/ppermute | solution.py:21
  40.3 23.2 %all-gather.5.cloned.1.call-done = bf16[1280,1024]{1,0:T(8,128)(2,1)} async-done(((bf16[160,1024]{1,0:T(8,128)(2,1)}), bf16[1280,1024]{1,0:T(8,128)(2,1)}) %all-gather.5.cloned.1.call-update) | async-done | bytes 2621456 | tf_op jit(solution)/shard_map/all_gather | solution.py:141
  65.0 6.8 %fusion.3.xm_ref = bf16[512,5120]{1,0:T(8,128)(2,1)} fusion(bf16[512,5120]{1,0:T(8,128)(2,1)} %param.9, f32[5120]{0:T(1024)S(1)} %bitcast.88, f32[5120]{0:T(1024)S(1)} %bitcast.87, f32[512]{0:T(512)S(1)} %add_rsqrt_fusion), kind=kLoop, calls=%fused_computation.7 | loop fusion | flops 13107200 | bytes 10528768 | tf_op jit(solution)/shard_map/convert_element_type | solution.py:168
  72.6 1.6 slice.101
  74.3 2.3 %slice.104.rest_1_ = bf16[8,160,384]{2,1,0:T(8,128)(2,1)} slice(bf16[8,160,1024]{2,1,0:T(8,128)(2,1)} %bitcast.83), slice={[0:8], [0:160], [0:384]} | slice | bytes 1966080 | tf_op jit(solution)/shard_map/slice | solution.py:171
  76.6 2.0 collective-permute-start.5
  79.9 1.3 broadcast_select_fusion
  81.1 19.9 %collective-permute-done.5.rest_2_ = bf16[8,160,384]{2,1,0:T(8,128)(2,1)} collective-permute-done((bf16[8,160,384]{2,1,0:T(8,128)(2,1)}, bf16[8,160,384]{2,1,0:T(8,128)(2,1)}, u32[]{:S(2)}, u32[]{:S(2)}) %collective-permute-start.5) | collective-permute-done | bytes 983072 | tf_op jit(solution)/shard_map/ppermute | solution.py:21
  101.0 1.1 slice.126
  102.1 2.2 %collective-permute-start.7 = (bf16[4,160,384]{2,1,0:T(8,128)(2,1)S(1)}, bf16[4,160,384]{2,1,0:T(8,128)(2,1)S(1)}, u32[]{:S(2)}, u32[]{:S(2)}) collective-permute-start(bf16[4,160,384]{2,1,0:T(8,128)(2,1)S(1)} %slice.126), channel_id=1, source_target_pairs={{0,8},{8,16},{16,24},{24,0},{1,9},{9,17},{17,25},{25,1},{2,10},{10... | collective-permute-start | bytes 1474568 | tf_op jit(solution)/shard_map/ppermute | solution.py:21
  104.3 1.1 slice.127
  106.2 1.7 pad_maximum_fusion
  107.9 1.2 fusion.7
  109.1 1.9 pad_maximum_fusion.1
  111.0 4.8 %collective-permute-done.7.rest_4_ = bf16[4,160,384]{2,1,0:T(8,128)(2,1)S(1)} collective-permute-done((bf16[4,160,384]{2,1,0:T(8,128)(2,1)S(1)}, bf16[4,160,384]{2,1,0:T(8,128)(2,1)S(1)}, u32[]{:S(2)}, u32[]{:S(2)}) %collective-permute-start.7) | collective-permute-done | bytes 491552 | tf_op jit(solution)/shard_map/ppermute | solution.py:21
  115.9 2.2 %collective-permute-done.8.rest_5_ = bf16[4,160,384]{2,1,0:T(8,128)(2,1)S(1)} collective-permute-done((bf16[4,160,384]{2,1,0:T(8,128)(2,1)S(1)}, bf16[4,160,384]{2,1,0:T(8,128)(2,1)S(1)}, u32[]{:S(2)}, u32[]{:S(2)}) %collective-permute-start.8) | collective-permute-done | bytes 491552 | tf_op jit(solution)/shard_map/ppermute | solution.py:21
  118.8 11.9 %query_attend.1 = (bf16[256,640]{1,0:T(8,128)(2,1)}, bf16[256,640]{1,0:T(8,128)(2,1)}) custom-call(bf16[512,5120]{1,0:T(8,128)(2,1)} %fusion.3.xm_ref, bf16[64,640]{1,0:T(8,128)(2,1)} %get-tuple-element.18.k_ref, bf16[64,640]{1,0:T(8,128)(2,1)} %get-tuple-element.19.v_ref, bf16[8,4,160,256]{3,2,1,0:T(8,128)(2,1)} %bitcast.92, ...), custom_call_target="tpu_custom_call" | custom-call | flops 3355443200 | bytes 6553600 | tf_op jit(solution)/shard_map/query_attend/pallas_call | solution.py:213
  130.9 1.2 constant_dynamic-update-slice_fusion.1
  132.7 1.6 convolution_convert_fusion.10
  135.1 1.6 collective-permute-start.10
  136.7 2.9 %collective-permute-start.11 = (bf16[320,256]{1,0:T(8,128)(2,1)S(1)}, bf16[320,256]{1,0:T(8,128)(2,1)S(1)}, u32[]{:S(2)}, u32[]{:S(2)}) collective-permute-start(bf16[320,256]{1,0:T(8,128)(2,1)S(1)} %convolution_convert_fusion.9), channel_id=1, source_target_pairs={{0,4},{2,6},{4,0},{6,2},{1,5},{3,7},{5,1},{7,3},{8,12},{10,14},{12... | collective-permute-start | bytes 491528 | tf_op jit(solution)/shard_map/ppermute | solution.py:21
  139.6 1.3 collective-permute-start.12
  140.9 1.5 collective-permute-start.14
  142.9 4.4 %collective-permute-done.11 = bf16[320,256]{1,0:T(8,128)(2,1)S(1)} collective-permute-done((bf16[320,256]{1,0:T(8,128)(2,1)S(1)}, bf16[320,256]{1,0:T(8,128)(2,1)S(1)}, u32[]{:S(2)}, u32[]{:S(2)}) %collective-permute-start.11) | collective-permute-done | bytes 163872 | tf_op jit(solution)/shard_map/ppermute | solution.py:21
  148.4 8.4 %collective-permute-done.14 = bf16[256,1280]{1,0:T(8,128)(2,1)S(1)} collective-permute-done((bf16[256,1280]{1,0:T(8,128)(2,1)S(1)}, bf16[256,1280]{1,0:T(8,128)(2,1)S(1)}, u32[]{:S(2)}, u32[]{:S(2)}) %collective-permute-start.14) | collective-permute-done | bytes 655392 | tf_op jit(solution)/shard_map/ppermute | solution.py:21
  156.9 2.0 collective-permute-start.23
  160.6 1.1 collective-permute-start.24
  162.4 1.0 collective-permute-start.16
  163.4 1.0 collective-permute-start.17
  164.4 2.4 %collective-permute-done.23 = bf16[128,1280]{1,0:T(8,128)(2,1)S(1)} collective-permute-done((bf16[128,1280]{1,0:T(8,128)(2,1)S(1)}, bf16[128,1280]{1,0:T(8,128)(2,1)S(1)}, u32[]{:S(2)}, u32[]{:S(2)}) %collective-permute-start.23) | collective-permute-done | bytes 327712 | tf_op jit(solution)/shard_map/ppermute | solution.py:21
  167.4 1.5 collective-permute-done.24
  170.9 11.4 %collective-permute-done.16 = bf16[320,512]{1,0:T(8,128)(2,1)S(1)} collective-permute-done((bf16[320,512]{1,0:T(8,128)(2,1)S(1)}, bf16[320,512]{1,0:T(8,128)(2,1)S(1)}, u32[]{:S(2)}, u32[]{:S(2)}) %collective-permute-start.16) | collective-permute-done | bytes 327712 | tf_op jit(solution)/shard_map/ppermute | solution.py:21
  183.1 3.3 %collective-permute-start.19 = (bf16[160,256]{1,0:T(8,128)(2,1)S(1)}, bf16[160,256]{1,0:T(8,128)(2,1)S(1)}, u32[]{:S(2)}, u32[]{:S(2)}) collective-permute-start(bf16[160,256]{1,0:T(8,128)(2,1)S(1)} %get-tuple-element.31), channel_id=1, source_target_pairs={{0,24},{1,25},{8,0},{9,1},{16,8},{17,9},{24,16},{25,17},{2,26},{3,... | collective-permute-start | bytes 245768 | tf_op jit(solution)/shard_map/ppermute | solution.py:257
  186.4 2.8 %collective-permute-done.26 = bf16[320,256]{1,0:T(8,128)(2,1)S(1)} collective-permute-done((bf16[320,256]{1,0:T(8,128)(2,1)S(1)}, bf16[320,256]{1,0:T(8,128)(2,1)S(1)}, u32[]{:S(2)}, u32[]{:S(2)}) %collective-permute-start.26) | collective-permute-done | bytes 163872 | tf_op jit(solution)/shard_map/ppermute | solution.py:21
  189.2 1.0 collective-permute-start.21
  190.6 4.2 %collective-permute-start.28 = (bf16[160,256]{1,0:T(8,128)(2,1)S(1)}, bf16[160,256]{1,0:T(8,128)(2,1)S(1)}, u32[]{:S(2)}, u32[]{:S(2)}) collective-permute-start(bf16[160,256]{1,0:T(8,128)(2,1)S(1)} %get-tuple-element.35), channel_id=1, source_target_pairs={{0,16},{1,17},{8,24},{9,25},{16,0},{17,1},{24,8},{25,9},{2,18},{3,... | collective-permute-start | bytes 245768 | tf_op jit(solution)/shard_map/ppermute | solution.py:257
  195.0 3.0 %collective-permute-done.28.refs_6_ = bf16[160,256]{1,0:T(8,128)(2,1)S(1)} collective-permute-done((bf16[160,256]{1,0:T(8,128)(2,1)S(1)}, bf16[160,256]{1,0:T(8,128)(2,1)S(1)}, u32[]{:S(2)}, u32[]{:S(2)}) %collective-permute-start.28) | collective-permute-done | bytes 81952 | tf_op jit(solution)/shard_map/ppermute | solution.py:257
  198.0 3.1 %collective-permute-done.29.refs_7_ = bf16[160,256]{1,0:T(8,128)(2,1)S(1)} collective-permute-done((bf16[160,256]{1,0:T(8,128)(2,1)S(1)}, bf16[160,256]{1,0:T(8,128)(2,1)S(1)}, u32[]{:S(2)}, u32[]{:S(2)}) %collective-permute-start.29) | collective-permute-done | bytes 81952 | tf_op jit(solution)/shard_map/ppermute | solution.py:257
  201.7 2.4 %place.1 = bf16[512,640]{1,0:T(8,128)(2,1)} custom-call(bf16[160,256]{1,0:T(8,128)(2,1)} %get-tuple-element.37.refs_0_, bf16[160,256]{1,0:T(8,128)(2,1)} %copy-done.2, bf16[160,256]{1,0:T(8,128)(2,1)} %copy-done.3, bf16[160,256]{1,0:T(8,128)(2,1)} %copy-done.4, bf16[160,256]{1,0:T(8,128)(2,1)} %copy-done.5, bf16[160,256]{1,0:T(8,128)(2,1)} %copy-done.6, ...), custom_call_target="tpu_custom_call" | custom-call | tf_op jit(solution)/shard_map/place/pallas_call | solution.py:274
  (112 shorter events, 19.3 us)
Async XLA Ops:
  7.2 56.3 %all-gather.5.cloned.1.call-start = ((), (), s32[]{:S(2)}) async-start(), calls=%async_computation.1 | async-start | bytes 2949120 | tf_op jit(solution)/shard_map/all_gather | solution.py:141
  10.7 23.8 %collective-permute-start.1 = (bf16[160,256]{1,0:T(8,128)(2,1)S(1)}, bf16[160,256]{1,0:T(8,128)(2,1)S(1)}, u32[]{:S(2)}, u32[]{:S(2)}) collective-permute-start(bf16[160,256]{1,0:T(8,128)(2,1)S(1)} %get-tuple-element.33), channel_id=1, source_target_pairs={{0,8},{8,16},{16,24},{24,0},{1,9},{9,17},{17,25},{25,1},{2,10},{10... | collective-permute-start | bytes 245768 | tf_op jit(solution)/shard_map/ppermute | solution.py:21
  12.3 23.8 %collective-permute-start = (bf16[160,256]{1,0:T(8,128)(2,1)S(1)}, bf16[160,256]{1,0:T(8,128)(2,1)S(1)}, u32[]{:S(2)}, u32[]{:S(2)}) collective-permute-start(bf16[160,256]{1,0:T(8,128)(2,1)S(1)} %get-tuple-element.33), channel_id=1, source_target_pairs={{0,24},{8,0},{16,8},{24,16},{1,25},{9,1},{17,9},{25,17},{2,26},{10... | collective-permute-start | bytes 245768 | tf_op jit(solution)/shard_map/ppermute | solution.py:21
  17.8 45.8 %all-to-all-start = ((bf16[32,8,768]{2,1,0:T(8,128)(2,1)}), bf16[32,8,768]{2,1,0:T(8,128)(2,1)S(1)}, u32[]{:S(2)}, u32[]{:S(2)}) async-start(bf16[32,8,768]{2,1,0:T(8,128)(2,1)} %pad_maximum_fusion.2), calls=%async_computation | async-start | bytes 786432 | tf_op jit(solution)/shard_map/all_to_all | solution.py:157
  29.1 89.0 %all-gather.7.cloned.1.call-start = ((), (), s32[]{:S(2)}) async-start(), calls=%async_computation.2 | async-start | bytes 2949120 | tf_op jit(solution)/shard_map/all_gather | solution.py:144
  34.6 4.9 %collective-permute-start.2 = (bf16[160,256]{1,0:T(8,128)(2,1)S(1)}, bf16[160,256]{1,0:T(8,128)(2,1)S(1)}, u32[]{:S(2)}, u32[]{:S(2)}) collective-permute-start(bf16[160,256]{1,0:T(8,128)(2,1)S(1)} %collective-permute-done.1), channel_id=1, source_target_pairs={{0,8},{8,16},{16,24},{24,0},{1,9},{9,17},{17,25},{25,1},{2,10},{10... | collective-permute-start | bytes 245768 | tf_op jit(solution)/shard_map/ppermute | solution.py:21
  64.3 7.5 %collective-permute-start.3 = (bf16[64,640]{1,0:T(8,128)(2,1)S(1)}, bf16[64,640]{1,0:T(8,128)(2,1)S(1)}, u32[]{:S(2)}, u32[]{:S(2)}) collective-permute-start(bf16[64,640]{1,0:T(8,128)(2,1)S(1)} %bitcast_select_fusion), channel_id=1, source_target_pairs={{0,8},{8,0},{16,24},{24,16},{1,9},{9,1},{17,25},{25,17},{2,10},{10... | collective-permute-start | bytes 245768 | tf_op jit(solution)/shard_map/ppermute | solution.py:160
  71.8 8.0 %copy-start.1 = (bf16[64,2,8,640]{3,2,1,0:T(8,128)(2,1)S(1)}, bf16[64,2,8,640]{3,2,1,0:T(8,128)(2,1)}, u32[]{:S(2)}) copy-start(bf16[64,2,8,640]{3,2,1,0:T(8,128)(2,1)} %param.14) | copy-start | bytes 3932164
  74.2 32.0 %collective-permute-start.4 = (bf16[8,160,640]{2,1,0:T(8,128)(2,1)S(1)}, bf16[8,160,640]{2,1,0:T(8,128)(2,1)}, u32[]{:S(2)}, u32[]{:S(2)}) collective-permute-start(bf16[8,160,640]{2,1,0:T(8,128)(2,1)S(1)} %slice.101), channel_id=1, source_target_pairs={{0,1},{1,0},{2,3},{3,2},{4,5},{5,4},{6,7},{7,6},{8,9},{9,8},{10,11... | collective-permute-start | bytes 4915208 | tf_op jit(solution)/shard_map/ppermute | solution.py:187
  76.6 24.4 %collective-permute-start.5 = (bf16[8,160,384]{2,1,0:T(8,128)(2,1)}, bf16[8,160,384]{2,1,0:T(8,128)(2,1)}, u32[]{:S(2)}, u32[]{:S(2)}) collective-permute-start(bf16[8,160,384]{2,1,0:T(8,128)(2,1)} %slice.104.rest_1_), channel_id=1, source_target_pairs={{0,8},{8,16},{16,24},{24,0},{1,9},{9,17},{17,25},{25,1},{2,10},{10... | collective-permute-start | bytes 2949128 | tf_op jit(solution)/shard_map/ppermute | solution.py:21
  78.6 25.6 %collective-permute-start.6 = (bf16[8,160,384]{2,1,0:T(8,128)(2,1)}, bf16[8,160,384]{2,1,0:T(8,128)(2,1)}, u32[]{:S(2)}, u32[]{:S(2)}) collective-permute-start(bf16[8,160,384]{2,1,0:T(8,128)(2,1)} %slice.104.rest_1_), channel_id=1, source_target_pairs={{0,24},{8,0},{16,8},{24,16},{1,25},{9,1},{17,9},{25,17},{2,26},{10... | collective-permute-start | bytes 2949128 | tf_op jit(solution)/shard_map/ppermute | solution.py:21
  102.1 13.8 %collective-permute-start.7 = (bf16[4,160,384]{2,1,0:T(8,128)(2,1)S(1)}, bf16[4,160,384]{2,1,0:T(8,128)(2,1)S(1)}, u32[]{:S(2)}, u32[]{:S(2)}) collective-permute-start(bf16[4,160,384]{2,1,0:T(8,128)(2,1)S(1)} %slice.126), channel_id=1, source_target_pairs={{0,8},{8,16},{16,24},{24,0},{1,9},{9,17},{17,25},{25,1},{2,10},{10... | collective-permute-start | bytes 1474568 | tf_op jit(solution)/shard_map/ppermute | solution.py:21
  105.3 12.7 %collective-permute-start.8 = (bf16[4,160,384]{2,1,0:T(8,128)(2,1)S(1)}, bf16[4,160,384]{2,1,0:T(8,128)(2,1)S(1)}, u32[]{:S(2)}, u32[]{:S(2)}) collective-permute-start(bf16[4,160,384]{2,1,0:T(8,128)(2,1)S(1)} %slice.127), channel_id=1, source_target_pairs={{0,24},{8,0},{16,8},{24,16},{1,25},{9,1},{17,9},{25,17},{2,26},{10... | collective-permute-start | bytes 1474568 | tf_op jit(solution)/shard_map/ppermute | solution.py:21
  115.9 2.2 %copy-start.9 = (bf16[4,160,384]{2,1,0:T(8,128)(2,1)}, bf16[4,160,384]{2,1,0:T(8,128)(2,1)S(1)}, u32[]{:S(2)}) copy-start(bf16[4,160,384]{2,1,0:T(8,128)(2,1)S(1)} %collective-permute-done.7.rest_4_) | copy-start | bytes 1474564
  118.1 0.8 copy-start.10
  130.8 3.5 %copy-start = (bf16[4,320,1280]{2,1,0:T(8,128)(2,1)S(1)}, bf16[4,320,1280]{2,1,0:T(8,128)(2,1)}, u32[]{:S(2)}) copy-start(bf16[4,320,1280]{2,1,0:T(8,128)(2,1)} %pad_maximum_fusion.1) | copy-start | bytes 9830404
  130.8 1.9 collective-permute-start.9
  135.1 7.8 %collective-permute-start.10 = (bf16[320,256]{1,0:T(8,128)(2,1)S(1)}, bf16[320,256]{1,0:T(8,128)(2,1)S(1)}, u32[]{:S(2)}, u32[]{:S(2)}) collective-permute-start(bf16[320,256]{1,0:T(8,128)(2,1)S(1)} %convolution_convert_fusion.10), channel_id=1, source_target_pairs={{0,2},{2,4},{4,6},{6,0},{1,3},{3,5},{5,7},{7,1},{8,10},{10,12},{12... | collective-permute-start | bytes 491528 | tf_op jit(solution)/shard_map/ppermute | solution.py:21
  136.7 10.6 %collective-permute-start.11 = (bf16[320,256]{1,0:T(8,128)(2,1)S(1)}, bf16[320,256]{1,0:T(8,128)(2,1)S(1)}, u32[]{:S(2)}, u32[]{:S(2)}) collective-permute-start(bf16[320,256]{1,0:T(8,128)(2,1)S(1)} %convolution_convert_fusion.9), channel_id=1, source_target_pairs={{0,4},{2,6},{4,0},{6,2},{1,5},{3,7},{5,1},{7,3},{8,12},{10,14},{12... | collective-permute-start | bytes 491528 | tf_op jit(solution)/shard_map/ppermute | solution.py:21
  139.6 7.7 %collective-permute-start.12 = (bf16[320,256]{1,0:T(8,128)(2,1)S(1)}, bf16[320,256]{1,0:T(8,128)(2,1)S(1)}, u32[]{:S(2)}, u32[]{:S(2)}) collective-permute-start(bf16[320,256]{1,0:T(8,128)(2,1)S(1)} %convolution_convert_fusion.8), channel_id=1, source_target_pairs={{0,6},{2,0},{4,2},{6,4},{1,7},{3,1},{5,3},{7,5},{8,14},{10,8},{12,... | collective-permute-start | bytes 491528 | tf_op jit(solution)/shard_map/ppermute | solution.py:21
  140.9 15.9 %collective-permute-start.14 = (bf16[256,1280]{1,0:T(8,128)(2,1)S(1)}, bf16[256,1280]{1,0:T(8,128)(2,1)S(1)}, u32[]{:S(2)}, u32[]{:S(2)}) collective-permute-start(bf16[256,1280]{1,0:T(8,128)(2,1)S(1)} %constant_dynamic-update-slice_fusion), channel_id=1, source_target_pairs={{0,8},{8,16},{16,24},{24,0},{1,9},{9,17},{17,25},{25,1},{2,10},{10... | collective-permute-start | bytes 1966088 | tf_op jit(solution)/shard_map/ppermute | solution.py:21
  142.4 16.8 %collective-permute-start.15 = (bf16[256,1280]{1,0:T(8,128)(2,1)S(1)}, bf16[256,1280]{1,0:T(8,128)(2,1)S(1)}, u32[]{:S(2)}, u32[]{:S(2)}) collective-permute-start(bf16[256,1280]{1,0:T(8,128)(2,1)S(1)} %constant_dynamic-update-slice_fusion), channel_id=1, source_target_pairs={{0,24},{8,0},{16,8},{24,16},{1,25},{9,1},{17,9},{25,17},{2,26},{10... | collective-permute-start | bytes 1966088 | tf_op jit(solution)/shard_map/ppermute | solution.py:21
  148.4 42.2 %collective-permute-start.13 = (bf16[160,256]{1,0:T(8,128)(2,1)S(1)}, bf16[160,256]{1,0:T(8,128)(2,1)S(1)}, u32[]{:S(2)}, u32[]{:S(2)}) collective-permute-start(bf16[160,256]{1,0:T(8,128)(2,1)S(1)} %get-tuple-element.36), channel_id=1, source_target_pairs={{0,1},{1,0},{8,9},{9,8},{16,17},{17,16},{24,25},{25,24},{2,3},{3,2... | collective-permute-start | bytes 245768 | tf_op jit(solution)/shard_map/ppermute | solution.py:257
  156.9 10.0 %collective-permute-start.23 = (bf16[128,1280]{1,0:T(8,128)(2,1)S(1)}, bf16[128,1280]{1,0:T(8,128)(2,1)S(1)}, u32[]{:S(2)}, u32[]{:S(2)}) collective-permute-start(bf16[128,1280]{1,0:T(8,128)(2,1)S(1)} %slice.134), channel_id=1, source_target_pairs={{0,8},{8,16},{16,24},{24,0},{1,9},{9,17},{17,25},{25,1},{2,10},{10... | collective-permute-start | bytes 983048 | tf_op jit(solution)/shard_map/ppermute | solution.py:21
  160.6 8.3 %collective-permute-start.24 = (bf16[128,1280]{1,0:T(8,128)(2,1)S(1)}, bf16[128,1280]{1,0:T(8,128)(2,1)S(1)}, u32[]{:S(2)}, u32[]{:S(2)}) collective-permute-start(bf16[128,1280]{1,0:T(8,128)(2,1)S(1)} %slice.135), channel_id=1, source_target_pairs={{0,24},{8,0},{16,8},{24,16},{1,25},{9,1},{17,9},{25,17},{2,26},{10... | collective-permute-start | bytes 983048 | tf_op jit(solution)/shard_map/ppermute | solution.py:21
  162.4 20.0 %collective-permute-start.16 = (bf16[320,512]{1,0:T(8,128)(2,1)S(1)}, bf16[320,512]{1,0:T(8,128)(2,1)S(1)}, u32[]{:S(2)}, u32[]{:S(2)}) collective-permute-start(bf16[320,512]{1,0:T(8,128)(2,1)S(1)} %convolution_convert_fusion.2), channel_id=1, source_target_pairs={{0,2},{2,4},{4,6},{6,0},{1,3},{3,5},{5,7},{7,1},{8,10},{10,12},{12... | collective-permute-start | bytes 983048 | tf_op jit(solution)/shard_map/ppermute | solution.py:21
  163.4 19.0 %collective-permute-start.17 = (bf16[320,512]{1,0:T(8,128)(2,1)S(1)}, bf16[320,512]{1,0:T(8,128)(2,1)S(1)}, u32[]{:S(2)}, u32[]{:S(2)}) collective-permute-start(bf16[320,512]{1,0:T(8,128)(2,1)S(1)} %convolution_convert_fusion.1), channel_id=1, source_target_pairs={{0,4},{2,6},{4,0},{6,2},{1,5},{3,7},{5,1},{7,3},{8,12},{10,14},{12... | collective-permute-start | bytes 983048 | tf_op jit(solution)/shard_map/ppermute | solution.py:21
  166.8 15.5 %collective-permute-start.18 = (bf16[320,512]{1,0:T(8,128)(2,1)S(1)}, bf16[320,512]{1,0:T(8,128)(2,1)S(1)}, u32[]{:S(2)}, u32[]{:S(2)}) collective-permute-start(bf16[320,512]{1,0:T(8,128)(2,1)S(1)} %convolution_convert_fusion), channel_id=1, source_target_pairs={{0,6},{2,0},{4,2},{6,4},{1,7},{3,1},{5,3},{7,5},{8,14},{10,8},{12,... | collective-permute-start | bytes 983048 | tf_op jit(solution)/shard_map/ppermute | solution.py:21
  169.7 16.6 %collective-permute-start.25 = (bf16[320,256]{1,0:T(8,128)(2,1)S(1)}, bf16[320,256]{1,0:T(8,128)(2,1)S(1)}, u32[]{:S(2)}, u32[]{:S(2)}) collective-permute-start(bf16[320,256]{1,0:T(8,128)(2,1)S(1)} %convolution_convert_fusion.6), channel_id=1, source_target_pairs={{0,2},{2,4},{4,6},{6,0},{1,3},{3,5},{5,7},{7,1},{8,10},{10,12},{12... | collective-permute-start | bytes 491528 | tf_op jit(solution)/shard_map/ppermute | solution.py:21
  182.3 6.8 %collective-permute-start.26 = (bf16[320,256]{1,0:T(8,128)(2,1)S(1)}, bf16[320,256]{1,0:T(8,128)(2,1)S(1)}, u32[]{:S(2)}, u32[]{:S(2)}) collective-permute-start(bf16[320,256]{1,0:T(8,128)(2,1)S(1)} %convolution_convert_fusion.5), channel_id=1, source_target_pairs={{0,4},{2,6},{4,0},{6,2},{1,5},{3,7},{5,1},{7,3},{8,12},{10,14},{12... | collective-permute-start | bytes 491528 | tf_op jit(solution)/shard_map/ppermute | solution.py:21
  182.4 7.8 %collective-permute-start.27 = (bf16[320,256]{1,0:T(8,128)(2,1)S(1)}, bf16[320,256]{1,0:T(8,128)(2,1)S(1)}, u32[]{:S(2)}, u32[]{:S(2)}) collective-permute-start(bf16[320,256]{1,0:T(8,128)(2,1)S(1)} %convolution_convert_fusion.4), channel_id=1, source_target_pairs={{0,6},{2,0},{4,2},{6,4},{1,7},{3,1},{5,3},{7,5},{8,14},{10,8},{12,... | collective-permute-start | bytes 491528 | tf_op jit(solution)/shard_map/ppermute | solution.py:21
  183.1 11.8 %collective-permute-start.19 = (bf16[160,256]{1,0:T(8,128)(2,1)S(1)}, bf16[160,256]{1,0:T(8,128)(2,1)S(1)}, u32[]{:S(2)}, u32[]{:S(2)}) collective-permute-start(bf16[160,256]{1,0:T(8,128)(2,1)S(1)} %get-tuple-element.31), channel_id=1, source_target_pairs={{0,24},{1,25},{8,0},{9,1},{16,8},{17,9},{24,16},{25,17},{2,26},{3,... | collective-permute-start | bytes 245768 | tf_op jit(solution)/shard_map/ppermute | solution.py:257
  186.4 8.6 %collective-permute-start.20 = (bf16[160,256]{1,0:T(8,128)(2,1)S(1)}, bf16[160,256]{1,0:T(8,128)(2,1)S(1)}, u32[]{:S(2)}, u32[]{:S(2)}) collective-permute-start(bf16[160,256]{1,0:T(8,128)(2,1)S(1)} %get-tuple-element.30), channel_id=1, source_target_pairs={{0,25},{1,24},{8,1},{9,0},{16,9},{17,8},{24,17},{25,16},{2,27},{3,... | collective-permute-start | bytes 245768 | tf_op jit(solution)/shard_map/ppermute | solution.py:257
  189.2 5.8 %collective-permute-start.21 = (bf16[160,256]{1,0:T(8,128)(2,1)S(1)}, bf16[160,256]{1,0:T(8,128)(2,1)S(1)}, u32[]{:S(2)}, u32[]{:S(2)}) collective-permute-start(bf16[160,256]{1,0:T(8,128)(2,1)S(1)} %get-tuple-element.29), channel_id=1, source_target_pairs={{0,8},{1,9},{8,16},{9,17},{16,24},{17,25},{24,0},{25,1},{2,10},{3,... | collective-permute-start | bytes 245768 | tf_op jit(solution)/shard_map/ppermute | solution.py:257
  190.1 4.9 %collective-permute-start.22 = (bf16[160,256]{1,0:T(8,128)(2,1)S(1)}, bf16[160,256]{1,0:T(8,128)(2,1)S(1)}, u32[]{:S(2)}, u32[]{:S(2)}) collective-permute-start(bf16[160,256]{1,0:T(8,128)(2,1)S(1)} %get-tuple-element.28), channel_id=1, source_target_pairs={{0,9},{1,8},{8,17},{9,16},{16,25},{17,24},{24,1},{25,0},{2,11},{3,... | collective-permute-start | bytes 245768 | tf_op jit(solution)/shard_map/ppermute | solution.py:257
  190.6 10.5 %copy-start.2 = (bf16[160,256]{1,0:T(8,128)(2,1)}, bf16[160,256]{1,0:T(8,128)(2,1)S(1)}, u32[]{:S(2)}) copy-start(bf16[160,256]{1,0:T(8,128)(2,1)S(1)} %collective-permute-done.13.refs_1_) | copy-start | bytes 245764
  190.6 7.4 %collective-permute-start.28 = (bf16[160,256]{1,0:T(8,128)(2,1)S(1)}, bf16[160,256]{1,0:T(8,128)(2,1)S(1)}, u32[]{:S(2)}, u32[]{:S(2)}) collective-permute-start(bf16[160,256]{1,0:T(8,128)(2,1)S(1)} %get-tuple-element.35), channel_id=1, source_target_pairs={{0,16},{1,17},{8,24},{9,25},{16,0},{17,1},{24,8},{25,9},{2,18},{3,... | collective-permute-start | bytes 245768 | tf_op jit(solution)/shard_map/ppermute | solution.py:257
  194.9 6.2 %copy-start.3 = (bf16[160,256]{1,0:T(8,128)(2,1)}, bf16[160,256]{1,0:T(8,128)(2,1)S(1)}, u32[]{:S(2)}) copy-start(bf16[160,256]{1,0:T(8,128)(2,1)S(1)} %collective-permute-done.19.refs_2_) | copy-start | bytes 245764
  194.9 6.2 %collective-permute-start.29 = (bf16[160,256]{1,0:T(8,128)(2,1)S(1)}, bf16[160,256]{1,0:T(8,128)(2,1)S(1)}, u32[]{:S(2)}, u32[]{:S(2)}) collective-permute-start(bf16[160,256]{1,0:T(8,128)(2,1)S(1)} %get-tuple-element.34), channel_id=1, source_target_pairs={{0,17},{1,16},{8,25},{9,24},{16,1},{17,0},{24,9},{25,8},{2,19},{3,... | collective-permute-start | bytes 245768 | tf_op jit(solution)/shard_map/ppermute | solution.py:257
  195.0 6.1 %copy-start.4 = (bf16[160,256]{1,0:T(8,128)(2,1)}, bf16[160,256]{1,0:T(8,128)(2,1)S(1)}, u32[]{:S(2)}) copy-start(bf16[160,256]{1,0:T(8,128)(2,1)S(1)} %collective-permute-done.20.refs_3_) | copy-start | bytes 245764
  195.0 6.1 %copy-start.5 = (bf16[160,256]{1,0:T(8,128)(2,1)}, bf16[160,256]{1,0:T(8,128)(2,1)S(1)}, u32[]{:S(2)}) copy-start(bf16[160,256]{1,0:T(8,128)(2,1)S(1)} %collective-permute-done.21.refs_4_) | copy-start | bytes 245764
  195.0 6.1 %copy-start.6 = (bf16[160,256]{1,0:T(8,128)(2,1)}, bf16[160,256]{1,0:T(8,128)(2,1)S(1)}, u32[]{:S(2)}) copy-start(bf16[160,256]{1,0:T(8,128)(2,1)S(1)} %collective-permute-done.22.refs_5_) | copy-start | bytes 245764
  198.0 3.1 %copy-start.7 = (bf16[160,256]{1,0:T(8,128)(2,1)}, bf16[160,256]{1,0:T(8,128)(2,1)S(1)}, u32[]{:S(2)}) copy-start(bf16[160,256]{1,0:T(8,128)(2,1)S(1)} %collective-permute-done.28.refs_6_) | copy-start | bytes 245764
  201.1 0.6 copy-start.8
Sparse Core Ops, SparseCore 0:
  10.3 53.0 all-gather.4
  65.2 40.4 all-gather.6

commit v3 on v2

--- a/solution.py
+++ b/solution.py
@@ -41,6 +41,12 @@
 
 def in_order(got, n):
     return jnp.stack([next(a for a, off, _ in got if off % n == i) for i in range(n)])
+
+
+def join_kernel(cut, q_ref, o_ref, early_ref, joint_ref):
+    early_ref[...] = q_ref[:, :cut]
+    joint_ref[:, : q_ref.shape[1] - cut] = q_ref[:, cut:]
+    joint_ref[:, q_ref.shape[1] - cut:] = o_ref[...]
 
 
 def attend_kernel(plan, rows, nx, chunks, xm_ref, k_ref, v_ref, *rest):
@@ -137,9 +143,16 @@
 
     cut = 2 * HEAD_SIZE
     late = width - cut
-    joint = jnp.concatenate([query_weight[:, cut:], output_weight.T], axis=1)
+    early, joint = pl.pallas_call(
+        functools.partial(join_kernel, cut),
+        out_shape=(
+            jax.ShapeDtypeStruct((rows, cut), jnp.bfloat16),
+            jax.ShapeDtypeStruct((rows, late + width), jnp.bfloat16),
+        ),
+        name="join",
+    )(query_weight, output_weight.T)
     joint = lax.all_gather(joint, "mem_0", axis=0, tiled=False)
-    q_a = in_order(around(query_weight[:, :cut], "mem_1", True), nx)
+    q_a = in_order(around(early, "mem_1", True), nx)
     q_a, joint = lax.optimization_barrier((q_a, joint))
     q_a = lax.all_gather(q_a, "mem_0", axis=0, tiled=False)
 
@@ -242,7 +255,10 @@
         return [home] + [term(d, group) for d in range(1, ny)]
 
     def sent(parts):
-        return [parts[0]] + [shift(parts[d], "tp_0", d) for d in range(1, ny)]
+        out = [parts[0]]
+        for d in range(1, ny):
+            out.append(shift(parts[d], "tp_0", d))
+        return out
 
     def summed(parts):
         total = sum(part.astype(jnp.float32) for part in parts).astype(jnp.bfloat16)

time: 214 us -> 214 us (level)
  no operation moved by 1% of the time
where the time goes in v3:
time: 214 us; the launch traced here: 211 us
  waiting for transfers between devices  93.4 us (44%)
  starting transfers between devices  44 us (21%)
  other arithmetic  20.8 us (10%)
  Pallas kernels  16 us (7%)
  between operations  15.8 us (7%)
  local copies, waits for them, and re-layouts  13.8 us (6%)
  matrix products  7.05 us (3%)
    ppermute x20, waiting for transfers between devices, shift(): return lax.ppermute(array, axis, [(i, (i + by) % n) for i in range(n)])  61.7 us
    all_gather x1, waiting for transfers between devices, shards(): joint = lax.all_gather(joint, 'mem_0', axis=0, tiled=False)  24.8 us
    ppermute x20, starting transfers between devices, shift(): return lax.ppermute(array, axis, [(i, (i + by) % n) for i in range(n)])  23.2 us
    pallas_call x1, Pallas kernels, shards(): pl.pallas_call(functools.partial(attend_kernel, plan, rows, nx, chunks),...  11.9 us
    all_to_all x1, starting transfers between devices, shards(): lax.all_to_all(outgoing, MEM, split_axis=0, concat_axis=0, tiled=True)  11.4 us
    ppermute x7, starting transfers between devices, returned(): return lax.ppermute(block, ('mem_1', 'tp_1'), pairs)  8.49 us
    dot_general x12, matrix products, term(): lax.dot_general(weight[d], group, (((1,), (1,)), ((), ())), preferred_ele...  7.05 us
    convert_element_type x1, other arithmetic, shards(): (values * factor * (1.0 + modrow[0]) + modrow[1]).astype(jnp.bfloat16)  6.84 us
  transfers between devices with their start and end apart: 33, of which 15 were waited for; matrix products, arithmetic and copies ran while one was open for 18% of the time, Pallas kernels for 0%

profile of v3, /device:TPU:2, one launch (start us, length us, event | category | flops | bytes accessed | tf_op | source)
XLA Modules:
  0.0 210.9 jit_solution(7497838782557883886)
XLA Ops:
  7.2 1.8 join.1
  9.0 1.6 collective-permute-start.1
  10.6 0.8 collective-permute-start
  12.4 1.9 gather_fusion
  16.1 11.4 %all-to-all-start = ((bf16[32,8,768]{2,1,0:T(8,128)(2,1)}), bf16[32,8,768]{2,1,0:T(8,128)(2,1)S(1)}, u32[]{:S(2)}, u32[]{:S(2)}) async-start(bf16[32,8,768]{2,1,0:T(8,128)(2,1)} %pad_maximum_fusion.2), calls=%async_computation | async-start | bytes 786432 | tf_op jit(solution)/shard_map/all_to_all | solution.py:170
  28.2 3.6 %fusion = f32[512]{0:T(512)S(1)} fusion(bf16[512,5120]{1,0:T(8,128)(2,1)} %param.9), kind=kLoop, calls=%fused_computation.4 | loop fusion | flops 7863808 | bytes 5244928 | tf_op jit(solution)/shard_map/reduce_sum | solution.py:180
  31.8 0.9 dynamic-slice_add_fusion
  32.9 1.5 collective-permute-start.2
  34.5 3.4 %collective-permute-done.2 = bf16[160,256]{1,0:T(8,128)(2,1)S(1)} collective-permute-done((bf16[160,256]{1,0:T(8,128)(2,1)S(1)}, bf16[160,256]{1,0:T(8,128)(2,1)S(1)}, u32[]{:S(2)}, u32[]{:S(2)}) %collective-permute-start.2) | collective-permute-done | bytes 81952 | tf_op jit(solution)/shard_map/ppermute | solution.py:21
  38.7 24.8 %all-gather.5.cloned.1.call-done = bf16[1280,1024]{1,0:T(8,128)(2,1)} async-done(((bf16[160,1024]{1,0:T(8,128)(2,1)}), bf16[1280,1024]{1,0:T(8,128)(2,1)}) %all-gather.5.cloned.1.call-update) | async-done | bytes 2621456 | tf_op jit(solution)/shard_map/all_gather | solution.py:154
  64.9 6.8 %fusion.3.xm_ref = bf16[512,5120]{1,0:T(8,128)(2,1)} fusion(bf16[512,5120]{1,0:T(8,128)(2,1)} %param.9, f32[5120]{0:T(1024)S(1)} %bitcast.87, f32[5120]{0:T(1024)S(1)} %bitcast.86, f32[512]{0:T(512)S(1)} %add_rsqrt_fusion), kind=kLoop, calls=%fused_computation.7 | loop fusion | flops 13107200 | bytes 10528768 | tf_op jit(solution)/shard_map/convert_element_type | solution.py:181
  72.5 1.6 slice.93
  74.2 2.3 %slice.96.rest_1_ = bf16[8,160,384]{2,1,0:T(8,128)(2,1)} slice(bf16[8,160,1024]{2,1,0:T(8,128)(2,1)} %bitcast.82), slice={[0:8], [0:160], [0:384]} | slice | bytes 1966080 | tf_op jit(solution)/shard_map/slice | solution.py:184
  76.5 2.1 collective-permute-start.5
  79.8 1.3 broadcast_select_fusion
  81.1 19.9 %collective-permute-done.5.rest_2_ = bf16[8,160,384]{2,1,0:T(8,128)(2,1)} collective-permute-done((bf16[8,160,384]{2,1,0:T(8,128)(2,1)}, bf16[8,160,384]{2,1,0:T(8,128)(2,1)}, u32[]{:S(2)}, u32[]{:S(2)}) %collective-permute-start.5) | collective-permute-done | bytes 983072 | tf_op jit(solution)/shard_map/ppermute | solution.py:21
  101.0 1.1 slice.118
  102.1 2.2 %collective-permute-start.7 = (bf16[4,160,384]{2,1,0:T(8,128)(2,1)S(1)}, bf16[4,160,384]{2,1,0:T(8,128)(2,1)S(1)}, u32[]{:S(2)}, u32[]{:S(2)}) collective-permute-start(bf16[4,160,384]{2,1,0:T(8,128)(2,1)S(1)} %slice.118), channel_id=1, source_target_pairs={{0,8},{8,16},{16,24},{24,0},{1,9},{9,17},{17,25},{25,1},{2,10},{10... | collective-permute-start | bytes 1474568 | tf_op jit(solution)/shard_map/ppermute | solution.py:21
  104.2 1.1 slice.119
  105.3 0.9 collective-permute-start.8
  106.2 1.7 pad_maximum_fusion
  107.9 1.2 fusion.7
  109.1 1.9 pad_maximum_fusion.1
  111.0 4.8 %collective-permute-done.7.rest_4_ = bf16[4,160,384]{2,1,0:T(8,128)(2,1)S(1)} collective-permute-done((bf16[4,160,384]{2,1,0:T(8,128)(2,1)S(1)}, bf16[4,160,384]{2,1,0:T(8,128)(2,1)S(1)}, u32[]{:S(2)}, u32[]{:S(2)}) %collective-permute-start.7) | collective-permute-done | bytes 491552 | tf_op jit(solution)/shard_map/ppermute | solution.py:21
  115.9 2.2 %collective-permute-done.8.rest_5_ = bf16[4,160,384]{2,1,0:T(8,128)(2,1)S(1)} collective-permute-done((bf16[4,160,384]{2,1,0:T(8,128)(2,1)S(1)}, bf16[4,160,384]{2,1,0:T(8,128)(2,1)S(1)}, u32[]{:S(2)}, u32[]{:S(2)}) %collective-permute-start.8) | collective-permute-done | bytes 491552 | tf_op jit(solution)/shard_map/ppermute | solution.py:21
  118.8 11.9 %query_attend.1 = (bf16[256,640]{1,0:T(8,128)(2,1)}, bf16[256,640]{1,0:T(8,128)(2,1)}) custom-call(bf16[512,5120]{1,0:T(8,128)(2,1)} %fusion.3.xm_ref, bf16[64,640]{1,0:T(8,128)(2,1)} %get-tuple-element.22.k_ref, bf16[64,640]{1,0:T(8,128)(2,1)} %get-tuple-element.23.v_ref, bf16[8,4,160,256]{3,2,1,0:T(8,128)(2,1)} %bitcast.92, ...), custom_call_target="tpu_custom_call" | custom-call | flops 3355443200 | bytes 6553600 | tf_op jit(solution)/shard_map/query_attend/pallas_call | solution.py:226
  130.8 1.2 constant_dynamic-update-slice_fusion.1
  132.7 1.5 convolution_convert_fusion.10
  135.1 1.5 collective-permute-start.10
  136.6 2.7 %collective-permute-start.11 = (bf16[320,256]{1,0:T(8,128)(2,1)S(1)}, bf16[320,256]{1,0:T(8,128)(2,1)S(1)}, u32[]{:S(2)}, u32[]{:S(2)}) collective-permute-start(bf16[320,256]{1,0:T(8,128)(2,1)S(1)} %convolution_convert_fusion.9), channel_id=1, source_target_pairs={{0,4},{2,6},{4,0},{6,2},{1,5},{3,7},{5,1},{7,3},{8,12},{10,14},{12... | collective-permute-start | bytes 491528 | tf_op jit(solution)/shard_map/ppermute | solution.py:21
  139.3 1.5 collective-permute-start.12
  140.8 1.5 collective-permute-start.14
  142.9 4.2 %collective-permute-done.11 = bf16[320,256]{1,0:T(8,128)(2,1)S(1)} collective-permute-done((bf16[320,256]{1,0:T(8,128)(2,1)S(1)}, bf16[320,256]{1,0:T(8,128)(2,1)S(1)}, u32[]{:S(2)}, u32[]{:S(2)}) %collective-permute-start.11) | collective-permute-done | bytes 163872 | tf_op jit(solution)/shard_map/ppermute | solution.py:21
  148.2 8.6 %collective-permute-done.14 = bf16[256,1280]{1,0:T(8,128)(2,1)S(1)} collective-permute-done((bf16[256,1280]{1,0:T(8,128)(2,1)S(1)}, bf16[256,1280]{1,0:T(8,128)(2,1)S(1)}, u32[]{:S(2)}, u32[]{:S(2)}) %collective-permute-start.14) | collective-permute-done | bytes 655392 | tf_op jit(solution)/shard_map/ppermute | solution.py:21
  156.8 2.0 collective-permute-start.23
  160.5 1.1 collective-permute-start.24
  162.3 0.8 collective-permute-start.16
  163.1 1.2 collective-permute-start.17
  164.3 2.4 %collective-permute-done.23 = bf16[128,1280]{1,0:T(8,128)(2,1)S(1)} collective-permute-done((bf16[128,1280]{1,0:T(8,128)(2,1)S(1)}, bf16[128,1280]{1,0:T(8,128)(2,1)S(1)}, u32[]{:S(2)}, u32[]{:S(2)}) %collective-permute-start.23) | collective-permute-done | bytes 327712 | tf_op jit(solution)/shard_map/ppermute | solution.py:21
  167.4 1.5 collective-permute-done.24
  170.7 11.6 %collective-permute-done.16 = bf16[320,512]{1,0:T(8,128)(2,1)S(1)} collective-permute-done((bf16[320,512]{1,0:T(8,128)(2,1)S(1)}, bf16[320,512]{1,0:T(8,128)(2,1)S(1)}, u32[]{:S(2)}, u32[]{:S(2)}) %collective-permute-start.16) | collective-permute-done | bytes 327712 | tf_op jit(solution)/shard_map/ppermute | solution.py:21
  183.0 3.2 %collective-permute-start.19 = (bf16[160,256]{1,0:T(8,128)(2,1)S(1)}, bf16[160,256]{1,0:T(8,128)(2,1)S(1)}, u32[]{:S(2)}, u32[]{:S(2)}) collective-permute-start(bf16[160,256]{1,0:T(8,128)(2,1)S(1)} %get-tuple-element.35), channel_id=1, source_target_pairs={{0,24},{1,25},{8,0},{9,1},{16,8},{17,9},{24,16},{25,17},{2,26},{3,... | collective-permute-start | bytes 245768 | tf_op jit(solution)/shard_map/ppermute | solution.py:273
  186.3 2.8 %collective-permute-done.26 = bf16[320,256]{1,0:T(8,128)(2,1)S(1)} collective-permute-done((bf16[320,256]{1,0:T(8,128)(2,1)S(1)}, bf16[320,256]{1,0:T(8,128)(2,1)S(1)}, u32[]{:S(2)}, u32[]{:S(2)}) %collective-permute-start.26) | collective-permute-done | bytes 163872 | tf_op jit(solution)/shard_map/ppermute | solution.py:21
  189.1 1.0 collective-permute-start.21
  190.6 4.2 %collective-permute-start.28 = (bf16[160,256]{1,0:T(8,128)(2,1)S(1)}, bf16[160,256]{1,0:T(8,128)(2,1)S(1)}, u32[]{:S(2)}, u32[]{:S(2)}) collective-permute-start(bf16[160,256]{1,0:T(8,128)(2,1)S(1)} %get-tuple-element.37), channel_id=1, source_target_pairs={{0,16},{1,17},{8,24},{9,25},{16,0},{17,1},{24,8},{25,9},{2,18},{3,... | collective-permute-start | bytes 245768 | tf_op jit(solution)/shard_map/ppermute | solution.py:273
  194.9 3.0 %collective-permute-done.28.refs_6_ = bf16[160,256]{1,0:T(8,128)(2,1)S(1)} collective-permute-done((bf16[160,256]{1,0:T(8,128)(2,1)S(1)}, bf16[160,256]{1,0:T(8,128)(2,1)S(1)}, u32[]{:S(2)}, u32[]{:S(2)}) %collective-permute-start.28) | collective-permute-done | bytes 81952 | tf_op jit(solution)/shard_map/ppermute | solution.py:273
  197.8 3.2 %collective-permute-done.29.refs_7_ = bf16[160,256]{1,0:T(8,128)(2,1)S(1)} collective-permute-done((bf16[160,256]{1,0:T(8,128)(2,1)S(1)}, bf16[160,256]{1,0:T(8,128)(2,1)S(1)}, u32[]{:S(2)}, u32[]{:S(2)}) %collective-permute-start.29) | collective-permute-done | bytes 81952 | tf_op jit(solution)/shard_map/ppermute | solution.py:273
  201.7 2.4 %place.1 = bf16[512,640]{1,0:T(8,128)(2,1)} custom-call(bf16[160,256]{1,0:T(8,128)(2,1)} %get-tuple-element.39.refs_0_, bf16[160,256]{1,0:T(8,128)(2,1)} %copy-done.2, bf16[160,256]{1,0:T(8,128)(2,1)} %copy-done.3, bf16[160,256]{1,0:T(8,128)(2,1)} %copy-done.4, bf16[160,256]{1,0:T(8,128)(2,1)} %copy-done.5, bf16[160,256]{1,0:T(8,128)(2,1)} %copy-done.6, ...), custom_call_target="tpu_custom_call" | custom-call | tf_op jit(solution)/shard_map/place/pallas_call | solution.py:290
  (112 shorter events, 17.3 us)
Async XLA Ops:
  7.2 56.3 %all-gather.5.cloned.1.call-start = ((), (), s32[]{:S(2)}) async-start(), calls=%async_computation.1 | async-start | bytes 2949120 | tf_op jit(solution)/shard_map/all_gather | solution.py:154
  9.0 23.9 %collective-permute-start.1 = (bf16[160,256]{1,0:T(8,128)(2,1)}, bf16[160,256]{1,0:T(8,128)(2,1)S(1)}, u32[]{:S(2)}, u32[]{:S(2)}) collective-permute-start(bf16[160,256]{1,0:T(8,128)(2,1)} %get-tuple-element.15), channel_id=1, source_target_pairs={{0,8},{8,16},{16,24},{24,0},{1,9},{9,17},{17,25},{25,1},{2,10},{10... | collective-permute-start | bytes 245768 | tf_op jit(solution)/shard_map/ppermute | solution.py:21
  10.6 23.9 %collective-permute-start = (bf16[160,256]{1,0:T(8,128)(2,1)}, bf16[160,256]{1,0:T(8,128)(2,1)S(1)}, u32[]{:S(2)}, u32[]{:S(2)}) collective-permute-start(bf16[160,256]{1,0:T(8,128)(2,1)} %get-tuple-element.15), channel_id=1, source_target_pairs={{0,24},{8,0},{16,8},{24,16},{1,25},{9,1},{17,9},{25,17},{2,26},{10... | collective-permute-start | bytes 245768 | tf_op jit(solution)/shard_map/ppermute | solution.py:21
  16.1 21.8 %copy-start.9 = (bf16[160,256]{1,0:T(8,128)(2,1)S(1)}, bf16[160,256]{1,0:T(8,128)(2,1)}, u32[]{:S(2)}) copy-start(bf16[160,256]{1,0:T(8,128)(2,1)} %get-tuple-element.15) | copy-start | bytes 245764
  16.1 47.6 %all-to-all-start = ((bf16[32,8,768]{2,1,0:T(8,128)(2,1)}), bf16[32,8,768]{2,1,0:T(8,128)(2,1)S(1)}, u32[]{:S(2)}, u32[]{:S(2)}) async-start(bf16[32,8,768]{2,1,0:T(8,128)(2,1)} %pad_maximum_fusion.2), calls=%async_computation | async-start | bytes 786432 | tf_op jit(solution)/shard_map/all_to_all | solution.py:170
  27.5 90.5 %all-gather.7.cloned.1.call-start = ((), (), s32[]{:S(2)}) async-start(), calls=%async_computation.2 | async-start | bytes 2949120 | tf_op jit(solution)/shard_map/all_gather | solution.py:157
  32.9 4.9 %collective-permute-start.2 = (bf16[160,256]{1,0:T(8,128)(2,1)S(1)}, bf16[160,256]{1,0:T(8,128)(2,1)S(1)}, u32[]{:S(2)}, u32[]{:S(2)}) collective-permute-start(bf16[160,256]{1,0:T(8,128)(2,1)S(1)} %collective-permute-done.1), channel_id=1, source_target_pairs={{0,8},{8,16},{16,24},{24,0},{1,9},{9,17},{17,25},{25,1},{2,10},{10... | collective-permute-start | bytes 245768 | tf_op jit(solution)/shard_map/ppermute | solution.py:21
  64.3 7.4 %collective-permute-start.3 = (bf16[64,640]{1,0:T(8,128)(2,1)S(1)}, bf16[64,640]{1,0:T(8,128)(2,1)S(1)}, u32[]{:S(2)}, u32[]{:S(2)}) collective-permute-start(bf16[64,640]{1,0:T(8,128)(2,1)S(1)} %bitcast_select_fusion), channel_id=1, source_target_pairs={{0,8},{8,0},{16,24},{24,16},{1,9},{9,1},{17,25},{25,17},{2,10},{10... | collective-permute-start | bytes 245768 | tf_op jit(solution)/shard_map/ppermute | solution.py:173
  71.8 8.1 %copy-start.1 = (bf16[64,2,8,640]{3,2,1,0:T(8,128)(2,1)S(1)}, bf16[64,2,8,640]{3,2,1,0:T(8,128)(2,1)}, u32[]{:S(2)}) copy-start(bf16[64,2,8,640]{3,2,1,0:T(8,128)(2,1)} %param.14) | copy-start | bytes 3932164
  74.1 32.1 %collective-permute-start.4 = (bf16[8,160,640]{2,1,0:T(8,128)(2,1)S(1)}, bf16[8,160,640]{2,1,0:T(8,128)(2,1)}, u32[]{:S(2)}, u32[]{:S(2)}) collective-permute-start(bf16[8,160,640]{2,1,0:T(8,128)(2,1)S(1)} %slice.93), channel_id=1, source_target_pairs={{0,1},{1,0},{2,3},{3,2},{4,5},{5,4},{6,7},{7,6},{8,9},{9,8},{10,11... | collective-permute-start | bytes 4915208 | tf_op jit(solution)/shard_map/ppermute | solution.py:200
  76.5 24.5 %collective-permute-start.5 = (bf16[8,160,384]{2,1,0:T(8,128)(2,1)}, bf16[8,160,384]{2,1,0:T(8,128)(2,1)}, u32[]{:S(2)}, u32[]{:S(2)}) collective-permute-start(bf16[8,160,384]{2,1,0:T(8,128)(2,1)} %slice.96.rest_1_), channel_id=1, source_target_pairs={{0,8},{8,16},{16,24},{24,0},{1,9},{9,17},{17,25},{25,1},{2,10},{10... | collective-permute-start | bytes 2949128 | tf_op jit(solution)/shard_map/ppermute | solution.py:21
  78.6 25.6 %collective-permute-start.6 = (bf16[8,160,384]{2,1,0:T(8,128)(2,1)}, bf16[8,160,384]{2,1,0:T(8,128)(2,1)}, u32[]{:S(2)}, u32[]{:S(2)}) collective-permute-start(bf16[8,160,384]{2,1,0:T(8,128)(2,1)} %slice.96.rest_1_), channel_id=1, source_target_pairs={{0,24},{8,0},{16,8},{24,16},{1,25},{9,1},{17,9},{25,17},{2,26},{10... | collective-permute-start | bytes 2949128 | tf_op jit(solution)/shard_map/ppermute | solution.py:21
  102.1 13.8 %collective-permute-start.7 = (bf16[4,160,384]{2,1,0:T(8,128)(2,1)S(1)}, bf16[4,160,384]{2,1,0:T(8,128)(2,1)S(1)}, u32[]{:S(2)}, u32[]{:S(2)}) collective-permute-start(bf16[4,160,384]{2,1,0:T(8,128)(2,1)S(1)} %slice.118), channel_id=1, source_target_pairs={{0,8},{8,16},{16,24},{24,0},{1,9},{9,17},{17,25},{25,1},{2,10},{10... | collective-permute-start | bytes 1474568 | tf_op jit(solution)/shard_map/ppermute | solution.py:21
  105.3 12.7 %collective-permute-start.8 = (bf16[4,160,384]{2,1,0:T(8,128)(2,1)S(1)}, bf16[4,160,384]{2,1,0:T(8,128)(2,1)S(1)}, u32[]{:S(2)}, u32[]{:S(2)}) collective-permute-start(bf16[4,160,384]{2,1,0:T(8,128)(2,1)S(1)} %slice.119), channel_id=1, source_target_pairs={{0,24},{8,0},{16,8},{24,16},{1,25},{9,1},{17,9},{25,17},{2,26},{10... | collective-permute-start | bytes 1474568 | tf_op jit(solution)/shard_map/ppermute | solution.py:21
  115.9 2.2 %copy-start.10 = (bf16[4,160,384]{2,1,0:T(8,128)(2,1)}, bf16[4,160,384]{2,1,0:T(8,128)(2,1)S(1)}, u32[]{:S(2)}) copy-start(bf16[4,160,384]{2,1,0:T(8,128)(2,1)S(1)} %collective-permute-done.7.rest_4_) | copy-start | bytes 1474564
  118.1 0.8 copy-start.11
  130.7 3.5 %copy-start = (bf16[4,320,1280]{2,1,0:T(8,128)(2,1)S(1)}, bf16[4,320,1280]{2,1,0:T(8,128)(2,1)}, u32[]{:S(2)}) copy-start(bf16[4,320,1280]{2,1,0:T(8,128)(2,1)} %pad_maximum_fusion.1) | copy-start | bytes 9830404
  130.7 1.9 collective-permute-start.9
  135.1 7.7 %collective-permute-start.10 = (bf16[320,256]{1,0:T(8,128)(2,1)S(1)}, bf16[320,256]{1,0:T(8,128)(2,1)S(1)}, u32[]{:S(2)}, u32[]{:S(2)}) collective-permute-start(bf16[320,256]{1,0:T(8,128)(2,1)S(1)} %convolution_convert_fusion.10), channel_id=1, source_target_pairs={{0,2},{2,4},{4,6},{6,0},{1,3},{3,5},{5,7},{7,1},{8,10},{10,12},{12... | collective-permute-start | bytes 491528 | tf_op jit(solution)/shard_map/ppermute | solution.py:21
  136.6 10.5 %collective-permute-start.11 = (bf16[320,256]{1,0:T(8,128)(2,1)S(1)}, bf16[320,256]{1,0:T(8,128)(2,1)S(1)}, u32[]{:S(2)}, u32[]{:S(2)}) collective-permute-start(bf16[320,256]{1,0:T(8,128)(2,1)S(1)} %convolution_convert_fusion.9), channel_id=1, source_target_pairs={{0,4},{2,6},{4,0},{6,2},{1,5},{3,7},{5,1},{7,3},{8,12},{10,14},{12... | collective-permute-start | bytes 491528 | tf_op jit(solution)/shard_map/ppermute | solution.py:21
  139.3 7.7 %collective-permute-start.12 = (bf16[320,256]{1,0:T(8,128)(2,1)S(1)}, bf16[320,256]{1,0:T(8,128)(2,1)S(1)}, u32[]{:S(2)}, u32[]{:S(2)}) collective-permute-start(bf16[320,256]{1,0:T(8,128)(2,1)S(1)} %convolution_convert_fusion.8), channel_id=1, source_target_pairs={{0,6},{2,0},{4,2},{6,4},{1,7},{3,1},{5,3},{7,5},{8,14},{10,8},{12,... | collective-permute-start | bytes 491528 | tf_op jit(solution)/shard_map/ppermute | solution.py:21
  140.8 15.9 %collective-permute-start.14 = (bf16[256,1280]{1,0:T(8,128)(2,1)S(1)}, bf16[256,1280]{1,0:T(8,128)(2,1)S(1)}, u32[]{:S(2)}, u32[]{:S(2)}) collective-permute-start(bf16[256,1280]{1,0:T(8,128)(2,1)S(1)} %constant_dynamic-update-slice_fusion), channel_id=1, source_target_pairs={{0,8},{8,16},{16,24},{24,0},{1,9},{9,17},{17,25},{25,1},{2,10},{10... | collective-permute-start | bytes 1966088 | tf_op jit(solution)/shard_map/ppermute | solution.py:21
  142.3 16.9 %collective-permute-start.15 = (bf16[256,1280]{1,0:T(8,128)(2,1)S(1)}, bf16[256,1280]{1,0:T(8,128)(2,1)S(1)}, u32[]{:S(2)}, u32[]{:S(2)}) collective-permute-start(bf16[256,1280]{1,0:T(8,128)(2,1)S(1)} %constant_dynamic-update-slice_fusion), channel_id=1, source_target_pairs={{0,24},{8,0},{16,8},{24,16},{1,25},{9,1},{17,9},{25,17},{2,26},{10... | collective-permute-start | bytes 1966088 | tf_op jit(solution)/shard_map/ppermute | solution.py:21
  148.2 42.4 %collective-permute-start.13 = (bf16[160,256]{1,0:T(8,128)(2,1)S(1)}, bf16[160,256]{1,0:T(8,128)(2,1)S(1)}, u32[]{:S(2)}, u32[]{:S(2)}) collective-permute-start(bf16[160,256]{1,0:T(8,128)(2,1)S(1)} %get-tuple-element.38), channel_id=1, source_target_pairs={{0,1},{1,0},{8,9},{9,8},{16,17},{17,16},{24,25},{25,24},{2,3},{3,2... | collective-permute-start | bytes 245768 | tf_op jit(solution)/shard_map/ppermute | solution.py:273
  156.8 10.0 %collective-permute-start.23 = (bf16[128,1280]{1,0:T(8,128)(2,1)S(1)}, bf16[128,1280]{1,0:T(8,128)(2,1)S(1)}, u32[]{:S(2)}, u32[]{:S(2)}) collective-permute-start(bf16[128,1280]{1,0:T(8,128)(2,1)S(1)} %slice.126), channel_id=1, source_target_pairs={{0,8},{8,16},{16,24},{24,0},{1,9},{9,17},{17,25},{25,1},{2,10},{10... | collective-permute-start | bytes 983048 | tf_op jit(solution)/shard_map/ppermute | solution.py:21
  160.5 8.3 %collective-permute-start.24 = (bf16[128,1280]{1,0:T(8,128)(2,1)S(1)}, bf16[128,1280]{1,0:T(8,128)(2,1)S(1)}, u32[]{:S(2)}, u32[]{:S(2)}) collective-permute-start(bf16[128,1280]{1,0:T(8,128)(2,1)S(1)} %slice.127), channel_id=1, source_target_pairs={{0,24},{8,0},{16,8},{24,16},{1,25},{9,1},{17,9},{25,17},{2,26},{10... | collective-permute-start | bytes 983048 | tf_op jit(solution)/shard_map/ppermute | solution.py:21
  162.3 20.0 %collective-permute-start.16 = (bf16[320,512]{1,0:T(8,128)(2,1)S(1)}, bf16[320,512]{1,0:T(8,128)(2,1)S(1)}, u32[]{:S(2)}, u32[]{:S(2)}) collective-permute-start(bf16[320,512]{1,0:T(8,128)(2,1)S(1)} %convolution_convert_fusion.2), channel_id=1, source_target_pairs={{0,2},{2,4},{4,6},{6,0},{1,3},{3,5},{5,7},{7,1},{8,10},{10,12},{12... | collective-permute-start | bytes 983048 | tf_op jit(solution)/shard_map/ppermute | solution.py:21
  163.1 19.2 %collective-permute-start.17 = (bf16[320,512]{1,0:T(8,128)(2,1)S(1)}, bf16[320,512]{1,0:T(8,128)(2,1)S(1)}, u32[]{:S(2)}, u32[]{:S(2)}) collective-permute-start(bf16[320,512]{1,0:T(8,128)(2,1)S(1)} %convolution_convert_fusion.1), channel_id=1, source_target_pairs={{0,4},{2,6},{4,0},{6,2},{1,5},{3,7},{5,1},{7,3},{8,12},{10,14},{12... | collective-permute-start | bytes 983048 | tf_op jit(solution)/shard_map/ppermute | solution.py:21
  166.8 15.5 %collective-permute-start.18 = (bf16[320,512]{1,0:T(8,128)(2,1)S(1)}, bf16[320,512]{1,0:T(8,128)(2,1)S(1)}, u32[]{:S(2)}, u32[]{:S(2)}) collective-permute-start(bf16[320,512]{1,0:T(8,128)(2,1)S(1)} %convolution_convert_fusion), channel_id=1, source_target_pairs={{0,6},{2,0},{4,2},{6,4},{1,7},{3,1},{5,3},{7,5},{8,14},{10,8},{12,... | collective-permute-start | bytes 983048 | tf_op jit(solution)/shard_map/ppermute | solution.py:21
  169.7 16.6 %collective-permute-start.25 = (bf16[320,256]{1,0:T(8,128)(2,1)S(1)}, bf16[320,256]{1,0:T(8,128)(2,1)S(1)}, u32[]{:S(2)}, u32[]{:S(2)}) collective-permute-start(bf16[320,256]{1,0:T(8,128)(2,1)S(1)} %convolution_convert_fusion.6), channel_id=1, source_target_pairs={{0,2},{2,4},{4,6},{6,0},{1,3},{3,5},{5,7},{7,1},{8,10},{10,12},{12... | collective-permute-start | bytes 491528 | tf_op jit(solution)/shard_map/ppermute | solution.py:21
  182.3 6.8 %collective-permute-start.26 = (bf16[320,256]{1,0:T(8,128)(2,1)S(1)}, bf16[320,256]{1,0:T(8,128)(2,1)S(1)}, u32[]{:S(2)}, u32[]{:S(2)}) collective-permute-start(bf16[320,256]{1,0:T(8,128)(2,1)S(1)} %convolution_convert_fusion.5), channel_id=1, source_target_pairs={{0,4},{2,6},{4,0},{6,2},{1,5},{3,7},{5,1},{7,3},{8,12},{10,14},{12... | collective-permute-start | bytes 491528 | tf_op jit(solution)/shard_map/ppermute | solution.py:21
  182.3 7.8 %collective-permute-start.27 = (bf16[320,256]{1,0:T(8,128)(2,1)S(1)}, bf16[320,256]{1,0:T(8,128)(2,1)S(1)}, u32[]{:S(2)}, u32[]{:S(2)}) collective-permute-start(bf16[320,256]{1,0:T(8,128)(2,1)S(1)} %convolution_convert_fusion.4), channel_id=1, source_target_pairs={{0,6},{2,0},{4,2},{6,4},{1,7},{3,1},{5,3},{7,5},{8,14},{10,8},{12,... | collective-permute-start | bytes 491528 | tf_op jit(solution)/shard_map/ppermute | solution.py:21
  183.0 11.8 %collective-permute-start.19 = (bf16[160,256]{1,0:T(8,128)(2,1)S(1)}, bf16[160,256]{1,0:T(8,128)(2,1)S(1)}, u32[]{:S(2)}, u32[]{:S(2)}) collective-permute-start(bf16[160,256]{1,0:T(8,128)(2,1)S(1)} %get-tuple-element.35), channel_id=1, source_target_pairs={{0,24},{1,25},{8,0},{9,1},{16,8},{17,9},{24,16},{25,17},{2,26},{3,... | collective-permute-start | bytes 245768 | tf_op jit(solution)/shard_map/ppermute | solution.py:273
  186.3 8.6 %collective-permute-start.20 = (bf16[160,256]{1,0:T(8,128)(2,1)S(1)}, bf16[160,256]{1,0:T(8,128)(2,1)S(1)}, u32[]{:S(2)}, u32[]{:S(2)}) collective-permute-start(bf16[160,256]{1,0:T(8,128)(2,1)S(1)} %get-tuple-element.34), channel_id=1, source_target_pairs={{0,25},{1,24},{8,1},{9,0},{16,9},{17,8},{24,17},{25,16},{2,27},{3,... | collective-permute-start | bytes 245768 | tf_op jit(solution)/shard_map/ppermute | solution.py:273
  189.1 5.8 %collective-permute-start.21 = (bf16[160,256]{1,0:T(8,128)(2,1)S(1)}, bf16[160,256]{1,0:T(8,128)(2,1)S(1)}, u32[]{:S(2)}, u32[]{:S(2)}) collective-permute-start(bf16[160,256]{1,0:T(8,128)(2,1)S(1)} %get-tuple-element.33), channel_id=1, source_target_pairs={{0,8},{1,9},{8,16},{9,17},{16,24},{17,25},{24,0},{25,1},{2,10},{3,... | collective-permute-start | bytes 245768 | tf_op jit(solution)/shard_map/ppermute | solution.py:273
  190.1 4.8 %collective-permute-start.22 = (bf16[160,256]{1,0:T(8,128)(2,1)S(1)}, bf16[160,256]{1,0:T(8,128)(2,1)S(1)}, u32[]{:S(2)}, u32[]{:S(2)}) collective-permute-start(bf16[160,256]{1,0:T(8,128)(2,1)S(1)} %get-tuple-element.32), channel_id=1, source_target_pairs={{0,9},{1,8},{8,17},{9,16},{16,25},{17,24},{24,1},{25,0},{2,11},{3,... | collective-permute-start | bytes 245768 | tf_op jit(solution)/shard_map/ppermute | solution.py:273
  190.6 10.5 %copy-start.2 = (bf16[160,256]{1,0:T(8,128)(2,1)}, bf16[160,256]{1,0:T(8,128)(2,1)S(1)}, u32[]{:S(2)}) copy-start(bf16[160,256]{1,0:T(8,128)(2,1)S(1)} %collective-permute-done.13.refs_1_) | copy-start | bytes 245764
  190.6 7.3 %collective-permute-start.28 = (bf16[160,256]{1,0:T(8,128)(2,1)S(1)}, bf16[160,256]{1,0:T(8,128)(2,1)S(1)}, u32[]{:S(2)}, u32[]{:S(2)}) collective-permute-start(bf16[160,256]{1,0:T(8,128)(2,1)S(1)} %get-tuple-element.37), channel_id=1, source_target_pairs={{0,16},{1,17},{8,24},{9,25},{16,0},{17,1},{24,8},{25,9},{2,18},{3,... | collective-permute-start | bytes 245768 | tf_op jit(solution)/shard_map/ppermute | solution.py:273
  194.8 6.2 %copy-start.3 = (bf16[160,256]{1,0:T(8,128)(2,1)}, bf16[160,256]{1,0:T(8,128)(2,1)S(1)}, u32[]{:S(2)}) copy-start(bf16[160,256]{1,0:T(8,128)(2,1)S(1)} %collective-permute-done.19.refs_2_) | copy-start | bytes 245764
  194.8 6.2 %collective-permute-start.29 = (bf16[160,256]{1,0:T(8,128)(2,1)S(1)}, bf16[160,256]{1,0:T(8,128)(2,1)S(1)}, u32[]{:S(2)}, u32[]{:S(2)}) collective-permute-start(bf16[160,256]{1,0:T(8,128)(2,1)S(1)} %get-tuple-element.36), channel_id=1, source_target_pairs={{0,17},{1,16},{8,25},{9,24},{16,1},{17,0},{24,9},{25,8},{2,19},{3,... | collective-permute-start | bytes 245768 | tf_op jit(solution)/shard_map/ppermute | solution.py:273
  194.8 6.2 %copy-start.4 = (bf16[160,256]{1,0:T(8,128)(2,1)}, bf16[160,256]{1,0:T(8,128)(2,1)S(1)}, u32[]{:S(2)}) copy-start(bf16[160,256]{1,0:T(8,128)(2,1)S(1)} %collective-permute-done.20.refs_3_) | copy-start | bytes 245764
  194.9 6.2 %copy-start.5 = (bf16[160,256]{1,0:T(8,128)(2,1)}, bf16[160,256]{1,0:T(8,128)(2,1)S(1)}, u32[]{:S(2)}) copy-start(bf16[160,256]{1,0:T(8,128)(2,1)S(1)} %collective-permute-done.21.refs_4_) | copy-start | bytes 245764
  194.9 6.2 %copy-start.6 = (bf16[160,256]{1,0:T(8,128)(2,1)}, bf16[160,256]{1,0:T(8,128)(2,1)S(1)}, u32[]{:S(2)}) copy-start(bf16[160,256]{1,0:T(8,128)(2,1)S(1)} %collective-permute-done.22.refs_5_) | copy-start | bytes 245764
  197.8 3.2 %copy-start.7 = (bf16[160,256]{1,0:T(8,128)(2,1)}, bf16[160,256]{1,0:T(8,128)(2,1)S(1)}, u32[]{:S(2)}) copy-start(bf16[160,256]{1,0:T(8,128)(2,1)S(1)} %collective-permute-done.28.refs_6_) | copy-start | bytes 245764
  201.0 0.6 copy-start.8
Sparse Core Ops, SparseCore 0:
  10.3 53.0 all-gather.4
  65.2 40.6 all-gather.6

commit v4 on v3

--- a/solution.py
+++ b/solution.py
@@ -43,8 +43,7 @@
     return jnp.stack([next(a for a, off, _ in got if off % n == i) for i in range(n)])
 
 
-def join_kernel(cut, q_ref, o_ref, early_ref, joint_ref):
-    early_ref[...] = q_ref[:, :cut]
+def join_kernel(cut, q_ref, o_ref, joint_ref):
     joint_ref[:, : q_ref.shape[1] - cut] = q_ref[:, cut:]
     joint_ref[:, q_ref.shape[1] - cut:] = o_ref[...]
 
@@ -143,16 +142,14 @@
 
     cut = 2 * HEAD_SIZE
     late = width - cut
-    early, joint = pl.pallas_call(
+    joint = pl.pallas_call(
         functools.partial(join_kernel, cut),
-        out_shape=(
-            jax.ShapeDtypeStruct((rows, cut), jnp.bfloat16),
-            jax.ShapeDtypeStruct((rows, late + width), jnp.bfloat16),
-        ),
+        out_shape=jax.ShapeDtypeStruct((rows, late + width), jnp.bfloat16),
         name="join",
     )(query_weight, output_weight.T)
+    query_weight, joint = lax.optimization_barrier((query_weight, joint))
     joint = lax.all_gather(joint, "mem_0", axis=0, tiled=False)
-    q_a = in_order(around(early, "mem_1", True), nx)
+    q_a = in_order(around(query_weight[:, :cut], "mem_1", True), nx)
     q_a, joint = lax.optimization_barrier((q_a, joint))
     q_a = lax.all_gather(q_a, "mem_0", axis=0, tiled=False)
 

time: 214 us -> 214 us (level)
  no operation moved by 1% of the time
where the time goes in v4:
time: 214 us; the launch traced here: 211 us
  waiting for transfers between devices  92.5 us (43%)
  starting transfers between devices  43.7 us (20%)
  other arithmetic  20.9 us (10%)
  Pallas kernels  16 us (7%)
  between operations  15.8 us (7%)
  local copies, waits for them, and re-layouts  14.7 us (7%)
  matrix products  7.04 us (3%)
    ppermute x20, waiting for transfers between devices, shift(): return lax.ppermute(array, axis, [(i, (i + by) % n) for i in range(n)])  61.9 us
    all_gather x1, waiting for transfers between devices, shards(): joint = lax.all_gather(joint, 'mem_0', axis=0, tiled=False)  24 us
    ppermute x20, starting transfers between devices, shift(): return lax.ppermute(array, axis, [(i, (i + by) % n) for i in range(n)])  23.2 us
    pallas_call x1, Pallas kernels, shards(): pl.pallas_call(functools.partial(attend_kernel, plan, rows, nx, chunks),...  11.9 us
    all_to_all x1, starting transfers between devices, shards(): lax.all_to_all(outgoing, MEM, split_axis=0, concat_axis=0, tiled=True)  11.3 us
    ppermute x7, starting transfers between devices, returned(): return lax.ppermute(block, ('mem_1', 'tp_1'), pairs)  8.48 us
    dot_general x12, matrix products, term(): lax.dot_general(weight[d], group, (((1,), (1,)), ((), ())), preferred_ele...  7.04 us
    convert_element_type x1, other arithmetic, shards(): (values * factor * (1.0 + modrow[0]) + modrow[1]).astype(jnp.bfloat16)  6.83 us
  transfers between devices with their start and end apart: 33, of which 15 were waited for; matrix products, arithmetic and copies ran while one was open for 18% of the time, Pallas kernels for 0%

profile of v4, /device:TPU:2, one launch (start us, length us, event | category | flops | bytes accessed | tf_op | source)
XLA Modules:
  0.0 210.7 jit_solution(11463753479184621245)
XLA Ops:
  7.2 1.8 join.1
  9.0 0.9 slice_bitcast_fusion.2
  9.9 1.6 collective-permute-start.1
  13.3 1.9 gather_fusion
  17.0 11.3 %all-to-all-start = ((bf16[32,8,768]{2,1,0:T(8,128)(2,1)}), bf16[32,8,768]{2,1,0:T(8,128)(2,1)S(1)}, u32[]{:S(2)}, u32[]{:S(2)}) async-start(bf16[32,8,768]{2,1,0:T(8,128)(2,1)} %pad_maximum_fusion.2), calls=%async_computation | async-start | bytes 786432 | tf_op jit(solution)/shard_map/all_to_all | solution.py:167
  29.0 3.6 %fusion = f32[512]{0:T(512)S(1)} fusion(bf16[512,5120]{1,0:T(8,128)(2,1)} %param.9), kind=kLoop, calls=%fused_computation.4 | loop fusion | flops 7863808 | bytes 5244928 | tf_op jit(solution)/shard_map/reduce_sum | solution.py:177
  32.6 0.9 dynamic-slice_add_fusion
  33.7 1.5 collective-permute-start.2
  35.3 3.4 %collective-permute-done.2 = bf16[160,256]{1,0:T(8,128)(2,1)S(1)} collective-permute-done((bf16[160,256]{1,0:T(8,128)(2,1)S(1)}, bf16[160,256]{1,0:T(8,128)(2,1)S(1)}, u32[]{:S(2)}, u32[]{:S(2)}) %collective-permute-start.2) | collective-permute-done | bytes 81952 | tf_op jit(solution)/shard_map/ppermute | solution.py:21
  39.5 24.0 %all-gather.5.cloned.1.call-done = bf16[1280,1024]{1,0:T(8,128)(2,1)} async-done(((bf16[160,1024]{1,0:T(8,128)(2,1)}), bf16[1280,1024]{1,0:T(8,128)(2,1)}) %all-gather.5.cloned.1.call-update) | async-done | bytes 2621456 | tf_op jit(solution)/shard_map/all_gather | solution.py:151
  64.8 6.8 %fusion.3.xm_ref = bf16[512,5120]{1,0:T(8,128)(2,1)} fusion(bf16[512,5120]{1,0:T(8,128)(2,1)} %param.9, f32[5120]{0:T(1024)S(1)} %bitcast.88, f32[5120]{0:T(1024)S(1)} %bitcast.87, f32[512]{0:T(512)S(1)} %add_rsqrt_fusion), kind=kLoop, calls=%fused_computation.7 | loop fusion | flops 13107200 | bytes 10528768 | tf_op jit(solution)/shard_map/convert_element_type | solution.py:178
  72.5 1.6 slice.97
  74.1 2.3 %slice.100.rest_1_ = bf16[8,160,384]{2,1,0:T(8,128)(2,1)} slice(bf16[8,160,1024]{2,1,0:T(8,128)(2,1)} %bitcast.83), slice={[0:8], [0:160], [0:384]} | slice | bytes 1966080 | tf_op jit(solution)/shard_map/slice | solution.py:181
  76.5 2.1 %collective-permute-start.5 = (bf16[8,160,384]{2,1,0:T(8,128)(2,1)}, bf16[8,160,384]{2,1,0:T(8,128)(2,1)}, u32[]{:S(2)}, u32[]{:S(2)}) collective-permute-start(bf16[8,160,384]{2,1,0:T(8,128)(2,1)} %slice.100.rest_1_), channel_id=1, source_target_pairs={{0,8},{8,16},{16,24},{24,0},{1,9},{9,17},{17,25},{25,1},{2,10},{10... | collective-permute-start | bytes 2949128 | tf_op jit(solution)/shard_map/ppermute | solution.py:21
  79.8 1.3 broadcast_select_fusion
  81.1 19.8 %collective-permute-done.5.rest_2_ = bf16[8,160,384]{2,1,0:T(8,128)(2,1)} collective-permute-done((bf16[8,160,384]{2,1,0:T(8,128)(2,1)}, bf16[8,160,384]{2,1,0:T(8,128)(2,1)}, u32[]{:S(2)}, u32[]{:S(2)}) %collective-permute-start.5) | collective-permute-done | bytes 983072 | tf_op jit(solution)/shard_map/ppermute | solution.py:21
  100.9 1.1 slice.122
  102.0 2.3 %collective-permute-start.7 = (bf16[4,160,384]{2,1,0:T(8,128)(2,1)S(1)}, bf16[4,160,384]{2,1,0:T(8,128)(2,1)S(1)}, u32[]{:S(2)}, u32[]{:S(2)}) collective-permute-start(bf16[4,160,384]{2,1,0:T(8,128)(2,1)S(1)} %slice.122), channel_id=1, source_target_pairs={{0,8},{8,16},{16,24},{24,0},{1,9},{9,17},{17,25},{25,1},{2,10},{10... | collective-permute-start | bytes 1474568 | tf_op jit(solution)/shard_map/ppermute | solution.py:21
  104.3 1.1 slice.123
  105.3 0.9 collective-permute-start.8
  106.2 1.7 pad_maximum_fusion
  107.9 1.2 fusion.7
  109.1 1.9 pad_maximum_fusion.1
  111.0 4.8 %collective-permute-done.7.rest_4_ = bf16[4,160,384]{2,1,0:T(8,128)(2,1)S(1)} collective-permute-done((bf16[4,160,384]{2,1,0:T(8,128)(2,1)S(1)}, bf16[4,160,384]{2,1,0:T(8,128)(2,1)S(1)}, u32[]{:S(2)}, u32[]{:S(2)}) %collective-permute-start.7) | collective-permute-done | bytes 491552 | tf_op jit(solution)/shard_map/ppermute | solution.py:21
  115.9 2.2 %collective-permute-done.8.rest_5_ = bf16[4,160,384]{2,1,0:T(8,128)(2,1)S(1)} collective-permute-done((bf16[4,160,384]{2,1,0:T(8,128)(2,1)S(1)}, bf16[4,160,384]{2,1,0:T(8,128)(2,1)S(1)}, u32[]{:S(2)}, u32[]{:S(2)}) %collective-permute-start.8) | collective-permute-done | bytes 491552 | tf_op jit(solution)/shard_map/ppermute | solution.py:21
  118.8 11.9 %query_attend.1 = (bf16[256,640]{1,0:T(8,128)(2,1)}, bf16[256,640]{1,0:T(8,128)(2,1)}) custom-call(bf16[512,5120]{1,0:T(8,128)(2,1)} %fusion.3.xm_ref, bf16[64,640]{1,0:T(8,128)(2,1)} %get-tuple-element.22.k_ref, bf16[64,640]{1,0:T(8,128)(2,1)} %get-tuple-element.23.v_ref, bf16[8,4,160,256]{3,2,1,0:T(8,128)(2,1)} %bitcast.92, ...), custom_call_target="tpu_custom_call" | custom-call | flops 3355443200 | bytes 6553600 | tf_op jit(solution)/shard_map/query_attend/pallas_call | solution.py:223
  130.9 1.2 constant_dynamic-update-slice_fusion.1
  132.7 1.6 convolution_convert_fusion.10
  135.1 1.4 collective-permute-start.10
  136.6 2.7 %collective-permute-start.11 = (bf16[320,256]{1,0:T(8,128)(2,1)S(1)}, bf16[320,256]{1,0:T(8,128)(2,1)S(1)}, u32[]{:S(2)}, u32[]{:S(2)}) collective-permute-start(bf16[320,256]{1,0:T(8,128)(2,1)S(1)} %convolution_convert_fusion.9), channel_id=1, source_target_pairs={{0,4},{2,6},{4,0},{6,2},{1,5},{3,7},{5,1},{7,3},{8,12},{10,14},{12... | collective-permute-start | bytes 491528 | tf_op jit(solution)/shard_map/ppermute | solution.py:21
  139.2 1.5 collective-permute-start.12
  140.7 1.5 collective-permute-start.14
  142.7 4.2 %collective-permute-done.11 = bf16[320,256]{1,0:T(8,128)(2,1)S(1)} collective-permute-done((bf16[320,256]{1,0:T(8,128)(2,1)S(1)}, bf16[320,256]{1,0:T(8,128)(2,1)S(1)}, u32[]{:S(2)}, u32[]{:S(2)}) %collective-permute-start.11) | collective-permute-done | bytes 163872 | tf_op jit(solution)/shard_map/ppermute | solution.py:21
  148.1 8.6 %collective-permute-done.14 = bf16[256,1280]{1,0:T(8,128)(2,1)S(1)} collective-permute-done((bf16[256,1280]{1,0:T(8,128)(2,1)S(1)}, bf16[256,1280]{1,0:T(8,128)(2,1)S(1)}, u32[]{:S(2)}, u32[]{:S(2)}) %collective-permute-start.14) | collective-permute-done | bytes 655392 | tf_op jit(solution)/shard_map/ppermute | solution.py:21
  156.7 2.0 collective-permute-start.23
  160.4 1.1 collective-permute-start.24
  162.2 0.9 collective-permute-start.16
  163.0 1.2 collective-permute-start.17
  164.2 2.4 %collective-permute-done.23 = bf16[128,1280]{1,0:T(8,128)(2,1)S(1)} collective-permute-done((bf16[128,1280]{1,0:T(8,128)(2,1)S(1)}, bf16[128,1280]{1,0:T(8,128)(2,1)S(1)}, u32[]{:S(2)}, u32[]{:S(2)}) %collective-permute-start.23) | collective-permute-done | bytes 327712 | tf_op jit(solution)/shard_map/ppermute | solution.py:21
  167.1 1.5 collective-permute-done.24
  170.6 11.7 %collective-permute-done.16 = bf16[320,512]{1,0:T(8,128)(2,1)S(1)} collective-permute-done((bf16[320,512]{1,0:T(8,128)(2,1)S(1)}, bf16[320,512]{1,0:T(8,128)(2,1)S(1)}, u32[]{:S(2)}, u32[]{:S(2)}) %collective-permute-start.16) | collective-permute-done | bytes 327712 | tf_op jit(solution)/shard_map/ppermute | solution.py:21
  183.0 3.1 %collective-permute-start.19 = (bf16[160,256]{1,0:T(8,128)(2,1)S(1)}, bf16[160,256]{1,0:T(8,128)(2,1)S(1)}, u32[]{:S(2)}, u32[]{:S(2)}) collective-permute-start(bf16[160,256]{1,0:T(8,128)(2,1)S(1)} %get-tuple-element.35), channel_id=1, source_target_pairs={{0,24},{1,25},{8,0},{9,1},{16,8},{17,9},{24,16},{25,17},{2,26},{3,... | collective-permute-start | bytes 245768 | tf_op jit(solution)/shard_map/ppermute | solution.py:270
  186.2 2.9 %collective-permute-done.26 = bf16[320,256]{1,0:T(8,128)(2,1)S(1)} collective-permute-done((bf16[320,256]{1,0:T(8,128)(2,1)S(1)}, bf16[320,256]{1,0:T(8,128)(2,1)S(1)}, u32[]{:S(2)}, u32[]{:S(2)}) %collective-permute-start.26) | collective-permute-done | bytes 163872 | tf_op jit(solution)/shard_map/ppermute | solution.py:21
  189.1 0.9 collective-permute-start.21
  190.4 4.2 %collective-permute-start.28 = (bf16[160,256]{1,0:T(8,128)(2,1)S(1)}, bf16[160,256]{1,0:T(8,128)(2,1)S(1)}, u32[]{:S(2)}, u32[]{:S(2)}) collective-permute-start(bf16[160,256]{1,0:T(8,128)(2,1)S(1)} %get-tuple-element.39), channel_id=1, source_target_pairs={{0,16},{1,17},{8,24},{9,25},{16,0},{17,1},{24,8},{25,9},{2,18},{3,... | collective-permute-start | bytes 245768 | tf_op jit(solution)/shard_map/ppermute | solution.py:270
  194.9 3.0 %collective-permute-done.28.refs_6_ = bf16[160,256]{1,0:T(8,128)(2,1)S(1)} collective-permute-done((bf16[160,256]{1,0:T(8,128)(2,1)S(1)}, bf16[160,256]{1,0:T(8,128)(2,1)S(1)}, u32[]{:S(2)}, u32[]{:S(2)}) %collective-permute-start.28) | collective-permute-done | bytes 81952 | tf_op jit(solution)/shard_map/ppermute | solution.py:270
  197.9 3.0 %collective-permute-done.29.refs_7_ = bf16[160,256]{1,0:T(8,128)(2,1)S(1)} collective-permute-done((bf16[160,256]{1,0:T(8,128)(2,1)S(1)}, bf16[160,256]{1,0:T(8,128)(2,1)S(1)}, u32[]{:S(2)}, u32[]{:S(2)}) %collective-permute-start.29) | collective-permute-done | bytes 81952 | tf_op jit(solution)/shard_map/ppermute | solution.py:270
  201.5 2.4 %place.1 = bf16[512,640]{1,0:T(8,128)(2,1)} custom-call(bf16[160,256]{1,0:T(8,128)(2,1)} %get-tuple-element.41.refs_0_, bf16[160,256]{1,0:T(8,128)(2,1)} %copy-done.2, bf16[160,256]{1,0:T(8,128)(2,1)} %copy-done.3, bf16[160,256]{1,0:T(8,128)(2,1)} %copy-done.4, bf16[160,256]{1,0:T(8,128)(2,1)} %copy-done.5, bf16[160,256]{1,0:T(8,128)(2,1)} %copy-done.6, ...), custom_call_target="tpu_custom_call" | custom-call | tf_op jit(solution)/shard_map/place/pallas_call | solution.py:287
  (111 shorter events, 18.2 us)
Async XLA Ops:
  7.2 56.3 %all-gather.5.cloned.1.call-start = ((), (), s32[]{:S(2)}) async-start(), calls=%async_computation.1 | async-start | bytes 2949120 | tf_op jit(solution)/shard_map/all_gather | solution.py:151
  9.9 23.8 %collective-permute-start.1 = (bf16[160,256]{1,0:T(8,128)(2,1)S(1)}, bf16[160,256]{1,0:T(8,128)(2,1)S(1)}, u32[]{:S(2)}, u32[]{:S(2)}) collective-permute-start(bf16[160,256]{1,0:T(8,128)(2,1)S(1)} %get-tuple-element.37), channel_id=1, source_target_pairs={{0,8},{8,16},{16,24},{24,0},{1,9},{9,17},{17,25},{25,1},{2,10},{10... | collective-permute-start | bytes 245768 | tf_op jit(solution)/shard_map/ppermute | solution.py:21
  11.5 23.8 %collective-permute-start = (bf16[160,256]{1,0:T(8,128)(2,1)S(1)}, bf16[160,256]{1,0:T(8,128)(2,1)S(1)}, u32[]{:S(2)}, u32[]{:S(2)}) collective-permute-start(bf16[160,256]{1,0:T(8,128)(2,1)S(1)} %get-tuple-element.37), channel_id=1, source_target_pairs={{0,24},{8,0},{16,8},{24,16},{1,25},{9,1},{17,9},{25,17},{2,26},{10... | collective-permute-start | bytes 245768 | tf_op jit(solution)/shard_map/ppermute | solution.py:21
  17.0 46.7 %all-to-all-start = ((bf16[32,8,768]{2,1,0:T(8,128)(2,1)}), bf16[32,8,768]{2,1,0:T(8,128)(2,1)S(1)}, u32[]{:S(2)}, u32[]{:S(2)}) async-start(bf16[32,8,768]{2,1,0:T(8,128)(2,1)} %pad_maximum_fusion.2), calls=%async_computation | async-start | bytes 786432 | tf_op jit(solution)/shard_map/all_to_all | solution.py:167
  28.3 89.8 %all-gather.7.cloned.1.call-start = ((), (), s32[]{:S(2)}) async-start(), calls=%async_computation.2 | async-start | bytes 2949120 | tf_op jit(solution)/shard_map/all_gather | solution.py:154
  33.7 4.9 %collective-permute-start.2 = (bf16[160,256]{1,0:T(8,128)(2,1)S(1)}, bf16[160,256]{1,0:T(8,128)(2,1)S(1)}, u32[]{:S(2)}, u32[]{:S(2)}) collective-permute-start(bf16[160,256]{1,0:T(8,128)(2,1)S(1)} %collective-permute-done.1), channel_id=1, source_target_pairs={{0,8},{8,16},{16,24},{24,0},{1,9},{9,17},{17,25},{25,1},{2,10},{10... | collective-permute-start | bytes 245768 | tf_op jit(solution)/shard_map/ppermute | solution.py:21
  64.3 7.3 %collective-permute-start.3 = (bf16[64,640]{1,0:T(8,128)(2,1)S(1)}, bf16[64,640]{1,0:T(8,128)(2,1)S(1)}, u32[]{:S(2)}, u32[]{:S(2)}) collective-permute-start(bf16[64,640]{1,0:T(8,128)(2,1)S(1)} %bitcast_select_fusion), channel_id=1, source_target_pairs={{0,8},{8,0},{16,24},{24,16},{1,9},{9,1},{17,25},{25,17},{2,10},{10... | collective-permute-start | bytes 245768 | tf_op jit(solution)/shard_map/ppermute | solution.py:170
  71.7 8.2 %copy-start.1 = (bf16[64,2,8,640]{3,2,1,0:T(8,128)(2,1)S(1)}, bf16[64,2,8,640]{3,2,1,0:T(8,128)(2,1)}, u32[]{:S(2)}) copy-start(bf16[64,2,8,640]{3,2,1,0:T(8,128)(2,1)} %param.14) | copy-start | bytes 3932164
  74.0 32.2 %collective-permute-start.4 = (bf16[8,160,640]{2,1,0:T(8,128)(2,1)S(1)}, bf16[8,160,640]{2,1,0:T(8,128)(2,1)}, u32[]{:S(2)}, u32[]{:S(2)}) collective-permute-start(bf16[8,160,640]{2,1,0:T(8,128)(2,1)S(1)} %slice.97), channel_id=1, source_target_pairs={{0,1},{1,0},{2,3},{3,2},{4,5},{5,4},{6,7},{7,6},{8,9},{9,8},{10,11... | collective-permute-start | bytes 4915208 | tf_op jit(solution)/shard_map/ppermute | solution.py:197
  76.5 24.4 %collective-permute-start.5 = (bf16[8,160,384]{2,1,0:T(8,128)(2,1)}, bf16[8,160,384]{2,1,0:T(8,128)(2,1)}, u32[]{:S(2)}, u32[]{:S(2)}) collective-permute-start(bf16[8,160,384]{2,1,0:T(8,128)(2,1)} %slice.100.rest_1_), channel_id=1, source_target_pairs={{0,8},{8,16},{16,24},{24,0},{1,9},{9,17},{17,25},{25,1},{2,10},{10... | collective-permute-start | bytes 2949128 | tf_op jit(solution)/shard_map/ppermute | solution.py:21
  78.6 25.6 %collective-permute-start.6 = (bf16[8,160,384]{2,1,0:T(8,128)(2,1)}, bf16[8,160,384]{2,1,0:T(8,128)(2,1)}, u32[]{:S(2)}, u32[]{:S(2)}) collective-permute-start(bf16[8,160,384]{2,1,0:T(8,128)(2,1)} %slice.100.rest_1_), channel_id=1, source_target_pairs={{0,24},{8,0},{16,8},{24,16},{1,25},{9,1},{17,9},{25,17},{2,26},{10... | collective-permute-start | bytes 2949128 | tf_op jit(solution)/shard_map/ppermute | solution.py:21
  102.0 13.9 %collective-permute-start.7 = (bf16[4,160,384]{2,1,0:T(8,128)(2,1)S(1)}, bf16[4,160,384]{2,1,0:T(8,128)(2,1)S(1)}, u32[]{:S(2)}, u32[]{:S(2)}) collective-permute-start(bf16[4,160,384]{2,1,0:T(8,128)(2,1)S(1)} %slice.122), channel_id=1, source_target_pairs={{0,8},{8,16},{16,24},{24,0},{1,9},{9,17},{17,25},{25,1},{2,10},{10... | collective-permute-start | bytes 1474568 | tf_op jit(solution)/shard_map/ppermute | solution.py:21
  105.3 12.7 %collective-permute-start.8 = (bf16[4,160,384]{2,1,0:T(8,128)(2,1)S(1)}, bf16[4,160,384]{2,1,0:T(8,128)(2,1)S(1)}, u32[]{:S(2)}, u32[]{:S(2)}) collective-permute-start(bf16[4,160,384]{2,1,0:T(8,128)(2,1)S(1)} %slice.123), channel_id=1, source_target_pairs={{0,24},{8,0},{16,8},{24,16},{1,25},{9,1},{17,9},{25,17},{2,26},{10... | collective-permute-start | bytes 1474568 | tf_op jit(solution)/shard_map/ppermute | solution.py:21
  115.9 2.2 %copy-start.9 = (bf16[4,160,384]{2,1,0:T(8,128)(2,1)}, bf16[4,160,384]{2,1,0:T(8,128)(2,1)S(1)}, u32[]{:S(2)}) copy-start(bf16[4,160,384]{2,1,0:T(8,128)(2,1)S(1)} %collective-permute-done.7.rest_4_) | copy-start | bytes 1474564
  118.1 0.8 copy-start.10
  130.8 3.5 %copy-start = (bf16[4,320,1280]{2,1,0:T(8,128)(2,1)S(1)}, bf16[4,320,1280]{2,1,0:T(8,128)(2,1)}, u32[]{:S(2)}) copy-start(bf16[4,320,1280]{2,1,0:T(8,128)(2,1)} %pad_maximum_fusion.1) | copy-start | bytes 9830404
  130.8 1.9 collective-permute-start.9
  135.1 7.6 %collective-permute-start.10 = (bf16[320,256]{1,0:T(8,128)(2,1)S(1)}, bf16[320,256]{1,0:T(8,128)(2,1)S(1)}, u32[]{:S(2)}, u32[]{:S(2)}) collective-permute-start(bf16[320,256]{1,0:T(8,128)(2,1)S(1)} %convolution_convert_fusion.10), channel_id=1, source_target_pairs={{0,2},{2,4},{4,6},{6,0},{1,3},{3,5},{5,7},{7,1},{8,10},{10,12},{12... | collective-permute-start | bytes 491528 | tf_op jit(solution)/shard_map/ppermute | solution.py:21
  136.6 10.4 %collective-permute-start.11 = (bf16[320,256]{1,0:T(8,128)(2,1)S(1)}, bf16[320,256]{1,0:T(8,128)(2,1)S(1)}, u32[]{:S(2)}, u32[]{:S(2)}) collective-permute-start(bf16[320,256]{1,0:T(8,128)(2,1)S(1)} %convolution_convert_fusion.9), channel_id=1, source_target_pairs={{0,4},{2,6},{4,0},{6,2},{1,5},{3,7},{5,1},{7,3},{8,12},{10,14},{12... | collective-permute-start | bytes 491528 | tf_op jit(solution)/shard_map/ppermute | solution.py:21
  139.2 7.7 %collective-permute-start.12 = (bf16[320,256]{1,0:T(8,128)(2,1)S(1)}, bf16[320,256]{1,0:T(8,128)(2,1)S(1)}, u32[]{:S(2)}, u32[]{:S(2)}) collective-permute-start(bf16[320,256]{1,0:T(8,128)(2,1)S(1)} %convolution_convert_fusion.8), channel_id=1, source_target_pairs={{0,6},{2,0},{4,2},{6,4},{1,7},{3,1},{5,3},{7,5},{8,14},{10,8},{12,... | collective-permute-start | bytes 491528 | tf_op jit(solution)/shard_map/ppermute | solution.py:21
  140.7 15.9 %collective-permute-start.14 = (bf16[256,1280]{1,0:T(8,128)(2,1)S(1)}, bf16[256,1280]{1,0:T(8,128)(2,1)S(1)}, u32[]{:S(2)}, u32[]{:S(2)}) collective-permute-start(bf16[256,1280]{1,0:T(8,128)(2,1)S(1)} %constant_dynamic-update-slice_fusion), channel_id=1, source_target_pairs={{0,8},{8,16},{16,24},{24,0},{1,9},{9,17},{17,25},{25,1},{2,10},{10... | collective-permute-start | bytes 1966088 | tf_op jit(solution)/shard_map/ppermute | solution.py:21
  142.2 16.9 %collective-permute-start.15 = (bf16[256,1280]{1,0:T(8,128)(2,1)S(1)}, bf16[256,1280]{1,0:T(8,128)(2,1)S(1)}, u32[]{:S(2)}, u32[]{:S(2)}) collective-permute-start(bf16[256,1280]{1,0:T(8,128)(2,1)S(1)} %constant_dynamic-update-slice_fusion), channel_id=1, source_target_pairs={{0,24},{8,0},{16,8},{24,16},{1,25},{9,1},{17,9},{25,17},{2,26},{10... | collective-permute-start | bytes 1966088 | tf_op jit(solution)/shard_map/ppermute | solution.py:21
  148.1 42.3 %collective-permute-start.13 = (bf16[160,256]{1,0:T(8,128)(2,1)S(1)}, bf16[160,256]{1,0:T(8,128)(2,1)S(1)}, u32[]{:S(2)}, u32[]{:S(2)}) collective-permute-start(bf16[160,256]{1,0:T(8,128)(2,1)S(1)} %get-tuple-element.40), channel_id=1, source_target_pairs={{0,1},{1,0},{8,9},{9,8},{16,17},{17,16},{24,25},{25,24},{2,3},{3,2... | collective-permute-start | bytes 245768 | tf_op jit(solution)/shard_map/ppermute | solution.py:270
  156.7 10.0 %collective-permute-start.23 = (bf16[128,1280]{1,0:T(8,128)(2,1)S(1)}, bf16[128,1280]{1,0:T(8,128)(2,1)S(1)}, u32[]{:S(2)}, u32[]{:S(2)}) collective-permute-start(bf16[128,1280]{1,0:T(8,128)(2,1)S(1)} %slice.130), channel_id=1, source_target_pairs={{0,8},{8,16},{16,24},{24,0},{1,9},{9,17},{17,25},{25,1},{2,10},{10... | collective-permute-start | bytes 983048 | tf_op jit(solution)/shard_map/ppermute | solution.py:21
  160.4 8.3 %collective-permute-start.24 = (bf16[128,1280]{1,0:T(8,128)(2,1)S(1)}, bf16[128,1280]{1,0:T(8,128)(2,1)S(1)}, u32[]{:S(2)}, u32[]{:S(2)}) collective-permute-start(bf16[128,1280]{1,0:T(8,128)(2,1)S(1)} %slice.131), channel_id=1, source_target_pairs={{0,24},{8,0},{16,8},{24,16},{1,25},{9,1},{17,9},{25,17},{2,26},{10... | collective-permute-start | bytes 983048 | tf_op jit(solution)/shard_map/ppermute | solution.py:21
  162.2 20.1 %collective-permute-start.16 = (bf16[320,512]{1,0:T(8,128)(2,1)S(1)}, bf16[320,512]{1,0:T(8,128)(2,1)S(1)}, u32[]{:S(2)}, u32[]{:S(2)}) collective-permute-start(bf16[320,512]{1,0:T(8,128)(2,1)S(1)} %convolution_convert_fusion.2), channel_id=1, source_target_pairs={{0,2},{2,4},{4,6},{6,0},{1,3},{3,5},{5,7},{7,1},{8,10},{10,12},{12... | collective-permute-start | bytes 983048 | tf_op jit(solution)/shard_map/ppermute | solution.py:21
  163.0 19.2 %collective-permute-start.17 = (bf16[320,512]{1,0:T(8,128)(2,1)S(1)}, bf16[320,512]{1,0:T(8,128)(2,1)S(1)}, u32[]{:S(2)}, u32[]{:S(2)}) collective-permute-start(bf16[320,512]{1,0:T(8,128)(2,1)S(1)} %convolution_convert_fusion.1), channel_id=1, source_target_pairs={{0,4},{2,6},{4,0},{6,2},{1,5},{3,7},{5,1},{7,3},{8,12},{10,14},{12... | collective-permute-start | bytes 983048 | tf_op jit(solution)/shard_map/ppermute | solution.py:21
  166.6 15.6 %collective-permute-start.18 = (bf16[320,512]{1,0:T(8,128)(2,1)S(1)}, bf16[320,512]{1,0:T(8,128)(2,1)S(1)}, u32[]{:S(2)}, u32[]{:S(2)}) collective-permute-start(bf16[320,512]{1,0:T(8,128)(2,1)S(1)} %convolution_convert_fusion), channel_id=1, source_target_pairs={{0,6},{2,0},{4,2},{6,4},{1,7},{3,1},{5,3},{7,5},{8,14},{10,8},{12,... | collective-permute-start | bytes 983048 | tf_op jit(solution)/shard_map/ppermute | solution.py:21
  169.5 16.6 %collective-permute-start.25 = (bf16[320,256]{1,0:T(8,128)(2,1)S(1)}, bf16[320,256]{1,0:T(8,128)(2,1)S(1)}, u32[]{:S(2)}, u32[]{:S(2)}) collective-permute-start(bf16[320,256]{1,0:T(8,128)(2,1)S(1)} %convolution_convert_fusion.6), channel_id=1, source_target_pairs={{0,2},{2,4},{4,6},{6,0},{1,3},{3,5},{5,7},{7,1},{8,10},{10,12},{12... | collective-permute-start | bytes 491528 | tf_op jit(solution)/shard_map/ppermute | solution.py:21
  182.2 6.8 %collective-permute-start.26 = (bf16[320,256]{1,0:T(8,128)(2,1)S(1)}, bf16[320,256]{1,0:T(8,128)(2,1)S(1)}, u32[]{:S(2)}, u32[]{:S(2)}) collective-permute-start(bf16[320,256]{1,0:T(8,128)(2,1)S(1)} %convolution_convert_fusion.5), channel_id=1, source_target_pairs={{0,4},{2,6},{4,0},{6,2},{1,5},{3,7},{5,1},{7,3},{8,12},{10,14},{12... | collective-permute-start | bytes 491528 | tf_op jit(solution)/shard_map/ppermute | solution.py:21
  182.3 7.7 %collective-permute-start.27 = (bf16[320,256]{1,0:T(8,128)(2,1)S(1)}, bf16[320,256]{1,0:T(8,128)(2,1)S(1)}, u32[]{:S(2)}, u32[]{:S(2)}) collective-permute-start(bf16[320,256]{1,0:T(8,128)(2,1)S(1)} %convolution_convert_fusion.4), channel_id=1, source_target_pairs={{0,6},{2,0},{4,2},{6,4},{1,7},{3,1},{5,3},{7,5},{8,14},{10,8},{12,... | collective-permute-start | bytes 491528 | tf_op jit(solution)/shard_map/ppermute | solution.py:21
  183.0 11.7 %collective-permute-start.19 = (bf16[160,256]{1,0:T(8,128)(2,1)S(1)}, bf16[160,256]{1,0:T(8,128)(2,1)S(1)}, u32[]{:S(2)}, u32[]{:S(2)}) collective-permute-start(bf16[160,256]{1,0:T(8,128)(2,1)S(1)} %get-tuple-element.35), channel_id=1, source_target_pairs={{0,24},{1,25},{8,0},{9,1},{16,8},{17,9},{24,16},{25,17},{2,26},{3,... | collective-permute-start | bytes 245768 | tf_op jit(solution)/shard_map/ppermute | solution.py:270
  186.1 8.8 %collective-permute-start.20 = (bf16[160,256]{1,0:T(8,128)(2,1)S(1)}, bf16[160,256]{1,0:T(8,128)(2,1)S(1)}, u32[]{:S(2)}, u32[]{:S(2)}) collective-permute-start(bf16[160,256]{1,0:T(8,128)(2,1)S(1)} %get-tuple-element.34), channel_id=1, source_target_pairs={{0,25},{1,24},{8,1},{9,0},{16,9},{17,8},{24,17},{25,16},{2,27},{3,... | collective-permute-start | bytes 245768 | tf_op jit(solution)/shard_map/ppermute | solution.py:270
  189.1 5.8 %collective-permute-start.21 = (bf16[160,256]{1,0:T(8,128)(2,1)S(1)}, bf16[160,256]{1,0:T(8,128)(2,1)S(1)}, u32[]{:S(2)}, u32[]{:S(2)}) collective-permute-start(bf16[160,256]{1,0:T(8,128)(2,1)S(1)} %get-tuple-element.33), channel_id=1, source_target_pairs={{0,8},{1,9},{8,16},{9,17},{16,24},{17,25},{24,0},{25,1},{2,10},{3,... | collective-permute-start | bytes 245768 | tf_op jit(solution)/shard_map/ppermute | solution.py:270
  189.9 5.0 %collective-permute-start.22 = (bf16[160,256]{1,0:T(8,128)(2,1)S(1)}, bf16[160,256]{1,0:T(8,128)(2,1)S(1)}, u32[]{:S(2)}, u32[]{:S(2)}) collective-permute-start(bf16[160,256]{1,0:T(8,128)(2,1)S(1)} %get-tuple-element.32), channel_id=1, source_target_pairs={{0,9},{1,8},{8,17},{9,16},{16,25},{17,24},{24,1},{25,0},{2,11},{3,... | collective-permute-start | bytes 245768 | tf_op jit(solution)/shard_map/ppermute | solution.py:270
  190.4 10.5 %copy-start.2 = (bf16[160,256]{1,0:T(8,128)(2,1)}, bf16[160,256]{1,0:T(8,128)(2,1)S(1)}, u32[]{:S(2)}) copy-start(bf16[160,256]{1,0:T(8,128)(2,1)S(1)} %collective-permute-done.13.refs_1_) | copy-start | bytes 245764
  190.4 7.5 %collective-permute-start.28 = (bf16[160,256]{1,0:T(8,128)(2,1)S(1)}, bf16[160,256]{1,0:T(8,128)(2,1)S(1)}, u32[]{:S(2)}, u32[]{:S(2)}) collective-permute-start(bf16[160,256]{1,0:T(8,128)(2,1)S(1)} %get-tuple-element.39), channel_id=1, source_target_pairs={{0,16},{1,17},{8,24},{9,25},{16,0},{17,1},{24,8},{25,9},{2,18},{3,... | collective-permute-start | bytes 245768 | tf_op jit(solution)/shard_map/ppermute | solution.py:270
  194.7 6.2 %copy-start.3 = (bf16[160,256]{1,0:T(8,128)(2,1)}, bf16[160,256]{1,0:T(8,128)(2,1)S(1)}, u32[]{:S(2)}) copy-start(bf16[160,256]{1,0:T(8,128)(2,1)S(1)} %collective-permute-done.19.refs_2_) | copy-start | bytes 245764
  194.7 6.2 %collective-permute-start.29 = (bf16[160,256]{1,0:T(8,128)(2,1)S(1)}, bf16[160,256]{1,0:T(8,128)(2,1)S(1)}, u32[]{:S(2)}, u32[]{:S(2)}) collective-permute-start(bf16[160,256]{1,0:T(8,128)(2,1)S(1)} %get-tuple-element.38), channel_id=1, source_target_pairs={{0,17},{1,16},{8,25},{9,24},{16,1},{17,0},{24,9},{25,8},{2,19},{3,... | collective-permute-start | bytes 245768 | tf_op jit(solution)/shard_map/ppermute | solution.py:270
  194.9 6.0 %copy-start.4 = (bf16[160,256]{1,0:T(8,128)(2,1)}, bf16[160,256]{1,0:T(8,128)(2,1)S(1)}, u32[]{:S(2)}) copy-start(bf16[160,256]{1,0:T(8,128)(2,1)S(1)} %collective-permute-done.20.refs_3_) | copy-start | bytes 245764
  194.9 6.0 %copy-start.5 = (bf16[160,256]{1,0:T(8,128)(2,1)}, bf16[160,256]{1,0:T(8,128)(2,1)S(1)}, u32[]{:S(2)}) copy-start(bf16[160,256]{1,0:T(8,128)(2,1)S(1)} %collective-permute-done.21.refs_4_) | copy-start | bytes 245764
  194.9 6.0 %copy-start.6 = (bf16[160,256]{1,0:T(8,128)(2,1)}, bf16[160,256]{1,0:T(8,128)(2,1)S(1)}, u32[]{:S(2)}) copy-start(bf16[160,256]{1,0:T(8,128)(2,1)S(1)} %collective-permute-done.22.refs_5_) | copy-start | bytes 245764
  197.9 3.0 %copy-start.7 = (bf16[160,256]{1,0:T(8,128)(2,1)}, bf16[160,256]{1,0:T(8,128)(2,1)S(1)}, u32[]{:S(2)}) copy-start(bf16[160,256]{1,0:T(8,128)(2,1)S(1)} %collective-permute-done.28.refs_6_) | copy-start | bytes 245764
  200.9 0.6 copy-start.8
Sparse Core Ops, SparseCore 0:
  10.3 53.0 all-gather.4
  65.2 40.4 all-gather.6
